TPU v7x, 32 devices: a whole 2x2x4 slice. The times are simulated.
32 devices in a mesh: blk: 8 (over z, x), lay: 4 (over y, core).
Axes of the slice: x: 2, y: 2, z: 4, core: 2. Of those that a mesh axis runs over, the one named last changes fastest.
Arguments:
- three_centre: bfloat16 [512, 512, 512], P('blk', 'lay'), may hold values from -224 to 224, as said below
- metric: bfloat16 [512, 64], P('blk'), may hold values from -2 to 6
- tile_pattern: int32 [512, 16, 16], P('blk'), may hold values from 0 to 1, as said below
- density: bfloat16 [512, 512], P('lay'), may hold values from -0.00048828125 to 0.00048828125
- dens_pattern: int32 [16, 16], replicated, may hold values 0 or 1
Outputs:
- exchange: float32 [512, 512], P('lay')
Inputs may be any that keep to these rules, and one draw needn't show every extreme that they name: three_centre(P, mu, lambda) equals three_centre(P, lambda, mu). `tile_pattern`: symmetric in its last two dimensions; diagonal tiles are 1; the share of ones is drawn per group of 64 consecutive functions.
All inputs are finite; a program needn't handle non-finite values.
Results may differ from a plain program's by a relative error of at most 0.0043.
Values may be sent and summed in bfloat16 or wider, within the bound.
No kernel may reach another device: no remote copies, remote signals or barrier semaphores. Data moves between devices by JAX's collectives and lax.ppermute only.
A program may use at most 128 MiB of HBM per device.

v0:
```python
import jax
import jax.numpy as jnp
from jax import lax
from jax.sharding import PartitionSpec as P

TILE = 32


def density_adder(left_side, dens_pattern, segment):
    count = segment.shape[0]
    block_ids = jnp.arange(count, dtype=jnp.int32) // TILE
    row_pattern = jnp.take(dens_pattern, block_ids, axis=0)
    dens_mask = jnp.repeat(row_pattern, TILE, axis=1)
    kept = jnp.where(dens_mask > 0, segment, jnp.zeros_like(segment))
    return jnp.dot(left_side, kept, preferred_element_type=jnp.float32)


def per_device(three_centre, metric, tile_pattern, density, dens_pattern):
    group_size = three_centre.shape[0]
    row_count = three_centre.shape[1]
    ao_width = three_centre.shape[2]
    layers = lax.axis_size("lay")
    row_start = lax.axis_index("lay") * row_count
    row_blocks = (row_start + jnp.arange(row_count, dtype=jnp.int32)) // TILE
    pattern_rows = jnp.take(tile_pattern, row_blocks, axis=1)
    tile_mask = jnp.repeat(pattern_rows, TILE, axis=2)
    masked = jnp.where(tile_mask > 0, three_centre, jnp.zeros_like(three_centre))
    coeffs = jnp.einsum("pq,qmn->pmn", metric, masked, preferred_element_type=jnp.float32).astype(
        jnp.bfloat16
    )
    left_side = coeffs.reshape(group_size * row_count, ao_width)
    inter = density_adder(
        left_side, dens_pattern, lax.all_gather(density, "lay", axis=0, tiled=True)
    )
    column_count = ao_width // layers
    inter = inter.astype(jnp.bfloat16).reshape(group_size, row_count, layers, column_count)
    outgoing = jnp.transpose(inter, (2, 1, 0, 3)).reshape(
        layers, row_count, group_size * column_count
    )
    moved = lax.all_to_all(outgoing, "lay", split_axis=0, concat_axis=1, tiled=True)
    moved = moved.reshape(ao_width, group_size * column_count)
    partial_value = jnp.dot(
        moved, coeffs.reshape(group_size * row_count, ao_width), preferred_element_type=jnp.float32
    )
    row_sums = lax.psum_scatter(partial_value, "lay", scatter_dimension=0, tiled=True)
    return lax.psum(row_sums, "blk")


def solution(mesh):
    return jax.shard_map(
        per_device,
        mesh=mesh,
        in_specs=(P("blk", "lay", None), P("blk", None), P("blk", None, None), P("lay", None), P()),
        out_specs=P("lay", None),
        check_vma=False,
    )
```

profile of v0, /device:TPU:0, one launch (start us, length us, event | category | flops | bytes accessed | tf_op | source)
XLA Modules:
  0.0 340.7 jit_solution(9691291641924943559)
XLA Ops:
  6.5 0.0 copy-start
  6.5 0.0 reduce-scatter.2.cloned.1.call-start
  6.6 1.0 copy.28
  7.7 1.7 gather_fusion.1
  9.4 0.1 copy.27
  9.5 8.7 %all_gather.3 = bf16[512,512]{0,1:T(8,128)(2,1)S(1)} all-gather(bf16[128,512]{0,1:T(8,128)(2,1)S(1)} %copy.28), channel_id=1, replica_groups=mesh['blk'=8,'lay'=4] {'lay'}, dimensions={0}, use_global_device_ids=true | all-gather | bytes 655360 | tf_op jit(solution)/shard_map/all_gather | solution.py:33
  18.2 0.0 copy-done
  18.2 0.8 gather_fusion
  18.9 0.3 fusion
  19.2 0.7 copy.23
  19.9 11.9 %copy.24 = bf16[64,128,512]{1,2,0:T(8,128)(2,1)} copy(bf16[64,128,512]{2,1,0:T(8,128)(2,1)} %param.5) | data formatting | bytes 16777216 | tf_op args[0]
  31.9 7.5 %bitcast_select_fusion = bf16[64,128,512]{1,2,0:T(8,128)(2,1)} fusion(bf16[64,128,512]{1,2,0:T(8,128)(2,1)} %copy.24, pred[64,128,16]{1,2,0:T(8,128)(4,1)S(1)} %copy.23), kind=kLoop, calls=%fused_computation.2 | loop fusion | flops 4194304 | bytes 16908288 | tf_op jit(solution)/shard_map/jit(_where)/select_n | solution.py:27
  39.4 0.0 copy-start.2
  39.4 12.6 %copy.25 = bf16[64,128,512]{2,0,1:T(8,128)(2,1)} copy(bf16[64,128,512]{1,2,0:T(8,128)(2,1)} %bitcast_select_fusion) | data formatting | bytes 16777216 | tf_op jit(solution)/shard_map/jit(_where)/select_n | solution.py:27
  52.0 0.0 copy-done.2
  52.0 8.9 %convert_bitcast_fusion = bf16[64,128,512]{2,0,1:T(8,128)(2,1)} fusion(bf16[64,128,512]{2,0,1:T(8,128)(2,1)} %copy.25, bf16[64,64]{1,0:T(8,128)(2,1)S(1)} %copy-done.2), kind=kOutput, calls=%fused_computation.4 | convolution fusion | flops 541065216 | bytes 16785408 | tf_op jit(solution)/shard_map/pq,qmn->pmn/dot_general | solution.py:28
  60.9 11.3 %copy.26 = bf16[64,128,512]{2,1,0:T(8,128)(2,1)} copy(bf16[64,128,512]{2,0,1:T(8,128)(2,1)} %convert_bitcast_fusion) | data formatting | bytes 16777216 | tf_op jit(solution)/shard_map/convert_element_type | solution.py:28
  72.2 0.1 bitcast_select_fusion.1
  72.3 10.2 %convolution_convert_fusion = bf16[8192,512]{1,0:T(8,128)(2,1)} fusion(bf16[8192,512]{1,0:T(8,128)(2,1)} %bitcast.25, bf16[512,512]{0,1:T(8,128)(2,1)S(1)} %bitcast_select_fusion.1), kind=kOutput, calls=%fused_computation.3 | convolution fusion | flops 4299161600 | bytes 17301504 | tf_op jit(solution)/shard_map/dot_general | solution.py:15
  82.5 12.5 %reshape.138 = bf16[64,128,4,128]{3,2,1,0:T(4,128)(2,1)} reshape(bf16[8192,512]{1,0:T(8,128)(2,1)} %convolution_convert_fusion) | data formatting | bytes 16777216 | tf_op jit(solution)/shard_map/reshape | solution.py:36
  95.0 13.6 %copy.29 = bf16[64,128,4,128]{1,3,0,2:T(8,128)(2,1)} copy(bf16[64,128,4,128]{3,2,1,0:T(4,128)(2,1)} %reshape.138) | data formatting | bytes 16777216 | tf_op jit(solution)/shard_map/reshape | solution.py:36
  108.7 100.6 %all_to_all.4 = bf16[4,128,8192]{1,2,0:T(8,128)(2,1)} all-to-all(bf16[4,128,8192]{1,2,0:T(8,128)(2,1)} %bitcast.24), channel_id=1, replica_groups=mesh['blk'=8,'lay'=4] {'lay'}, dimensions={0} | all-to-all | bytes 16777216 | tf_op jit(solution)/shard_map/all_to_all | solution.py:40
  209.2 12.0 %copy.30 = bf16[4,128,8192]{2,1,0:T(8,128)(2,1)} copy(bf16[4,128,8192]{1,2,0:T(8,128)(2,1)} %all_to_all.4) | data formatting | bytes 16777216 | tf_op jit(solution)/shard_map/all_to_all | solution.py:40
  221.2 0.0 copy-start.1
  221.2 11.3 %fusion.6 = f32[512,512]{1,0:T(8,128)} fusion(bf16[512,8192]{1,0:T(8,128)(2,1)} %bitcast.27, bf16[8192,512]{1,0:T(8,128)(2,1)} %bitcast.26), kind=kOutput, calls=%fused_computation.38 | convolution fusion | flops 4294967296 | bytes 17825792 | tf_op jit(solution)/shard_map/dot_general | solution.py:42
  232.5 0.0 reduce-scatter.2.cloned.1.call-update
  232.5 0.0 all-reduce.2.cloned.1.call-start
  232.6 25.2 %reduce-scatter.2.cloned.1.call-done = f32[128,512]{1,0:T(8,128)} async-done(((f32[512,512]{1,0:T(8,128)}), f32[128,512]{1,0:T(8,128)}) %reduce-scatter.2.cloned.1.call-update) | async-done | bytes 262160 | tf_op jit(solution)/shard_map/reduce_scatter | solution.py:45
  257.7 0.0 all-reduce.2.cloned.1.call-update
  257.8 74.4 %all-reduce.2.cloned.1.call-done = f32[128,512]{1,0:T(8,128)} async-done(((f32[128,512]{1,0:T(8,128)}), f32[128,512]{1,0:T(8,128)}) %all-reduce.2.cloned.1.call-update) | async-done | bytes 262160 | tf_op jit(solution)/shard_map/psum | solution.py:46
  332.1 1.7 copy.32
  333.8 0.0 copy-done.1
  (7 shorter events, 0.1 us)
Async XLA Ops:
  6.5 11.6 %copy-start = (s32[64,16,16]{0,2,1:T(8,128)S(1)}, s32[64,16,16]{0,2,1:T(8,128)}, u32[]{:S(2)}) copy-start(s32[64,16,16]{0,2,1:T(8,128)} %param.7) | copy-start | bytes 196612
  6.5 251.2 %reduce-scatter.2.cloned.1.call-start = ((), (), s32[]{:S(2)}) async-start(), calls=%async_computation.2 | async-start | bytes 1310720 | tf_op jit(solution)/shard_map/reduce_scatter | solution.py:45
  39.4 12.6 %copy-start.2 = (bf16[64,64]{1,0:T(8,128)(2,1)S(1)}, bf16[64,64]{1,0:T(8,128)(2,1)}, u32[]{:S(2)}) copy-start(bf16[64,64]{1,0:T(8,128)(2,1)} %param.6) | copy-start | bytes 24580
  221.2 112.6 %copy-start.1 = (s32[64,16,16]{0,2,1:T(8,128)S(1)}, s32[64,16,16]{0,2,1:T(8,128)}, u32[]{:S(2)}) copy-start(s32[64,16,16]{0,2,1:T(8,128)} %param.7) | copy-start | bytes 196612
  232.5 99.6 %all-reduce.2.cloned.1.call-start = ((), (), s32[]{:S(2)}) async-start(), calls=%async_computation.3 | async-start | bytes 524288 | tf_op jit(solution)/shard_map/psum | solution.py:46
Sparse Core Ops, SparseCore 0:
  232.6 25.0 reduce-scatter.1
  261.1 70.9 all-reduce.1
where the time goes:
time: 343 us; the launch traced here: 341 us
  blocking collectives  109 us (32%)
  waiting for transfers between devices  99.6 us (29%)
  local copies, waits for them, and re-layouts  80 us (23%)
  matrix products  30.4 us (9%)
  between operations  13.5 us (4%)
  other arithmetic  7.89 us (2%)
    all_to_all x1, blocking collectives, per_device(): lax.all_to_all(outgoing, 'lay', split_axis=0, concat_axis=1, tiled=True)  101 us
    psum x1, waiting for transfers between devices, per_device(): return lax.psum(row_sums, 'blk')  74.4 us
    reshape x2, local copies, waits for them, and re-layouts, per_device(): inter.astype(jnp.bfloat16)  26.2 us
    reduce_scatter x1, waiting for transfers between devices, per_device(): lax.psum_scatter(partial_value, 'lay', scatter_dimension=0, tiled=True)  25.2 us
    unnamed x9, local copies, waits for them, and re-layouts  14.6 us
    select_n x1, local copies, waits for them, and re-layouts, per_device(): jnp.where(tile_mask > 0, three_centre, jnp.zeros_like(three_centre))  12.6 us
    all_to_all x1, local copies, waits for them, and re-layouts, per_device(): lax.all_to_all(outgoing, 'lay', split_axis=0, concat_axis=1, tiled=True)  12 us
    convert_element_type x1, local copies, waits for them, and re-layouts, per_device(): jnp.einsum('pq,qmn->pmn', metric, masked, preferred_element_type=jnp.floa...  11.3 us
  transfers between devices with their start and end apart: 2, of which 2 were waited for; matrix products, arithmetic and copies ran while one was open for 0% of the time, Pallas kernels for 0%

commit v1 on v0

--- a/solution.py
+++ b/solution.py
@@ -1,9 +1,15 @@
+import functools
 import jax
 import jax.numpy as jnp
 from jax import lax
+from jax.experimental import pallas as pl
+from jax.experimental.pallas import tpu as pltpu
 from jax.sharding import PartitionSpec as P
 
 TILE = 32
+SUB = 16
+BF = jnp.bfloat16
+F32 = jnp.float32
 
 
 def density_adder(left_side, dens_pattern, segment):
@@ -15,7 +21,7 @@
     return jnp.dot(left_side, kept, preferred_element_type=jnp.float32)
 
 
-def per_device(three_centre, metric, tile_pattern, density, dens_pattern):
+def per_device_any(three_centre, metric, tile_pattern, density, dens_pattern):
     group_size = three_centre.shape[0]
     row_count = three_centre.shape[1]
     ao_width = three_centre.shape[2]
@@ -46,9 +52,285 @@
     return lax.psum(row_sums, "blk")
 
 
+def dot(a, b):
+    return jnp.dot(a, b, preferred_element_type=F32)
+
+
+def dot_t(a, b):
+    return lax.dot_general(a, b, (((1,), (1,)), ((), ())), preferred_element_type=F32)
+
+
+def iota(shape, dim):
+    return lax.broadcasted_iota(jnp.int32, shape, dim)
+
+
+def spread_metric(l, metric_ref, spread_ref, orders):
+    group = metric_ref.shape[0]
+    part = group // 4
+    rows, cols = part * SUB, group * SUB
+    widen = (iota((rows, part), 0) // SUB == iota((rows, part), 1)).astype(BF)
+    along = (iota((group, cols), 1) // SUB == iota((group, cols), 0)).astype(BF)
+    same = iota((rows, cols), 0) % SUB == iota((rows, cols), 1) % SUB
+    for n, p in enumerate(orders):
+        start = pl.multiple_of((l ^ p) * part, part)
+        tall = dot(widen, metric_ref[pl.ds(start, part), :]).astype(BF)
+        full = dot(tall, along)
+        spread_ref[n * rows : (n + 1) * rows, :] = jnp.where(same, full, 0.0).astype(BF)
+
+
+def masked_columns(l, order, base, three_ref, pattern):
+    group, sub, width = three_ref.shape
+    block = pattern.shape[1] * TILE // 4
+    tiles = pattern.shape[1]
+    out = []
+    for j in order:
+        start = (l ^ j) * block
+        here = (iota((tiles, block), 0) == (start // TILE) + iota((tiles, block), 1) // TILE).astype(BF)
+        mask = dot(pattern, here).astype(BF)
+        piece = three_ref[:, :, pl.ds(pl.multiple_of(start - base, block), block)]
+        out.append((piece * mask[:, None, :]).reshape(group * sub, block))
+    return jnp.concatenate(out, axis=1)
+
+
+def near_kernel(l_ref, three_ref, metric_ref, pattern_ref, straight_ref, cross_ref, spread_ref):
+    l = l_ref[0]
+
+    @pl.when(pl.program_id(0) == 0)
+    def _():
+        spread_metric(l, metric_ref, spread_ref, (2, 3))
+
+    part, sub, width = straight_ref.shape
+    data = masked_columns(l, (0, 1), (l // 2) * width, three_ref, pattern_ref[0])
+    got = dot(spread_ref[...], data).astype(BF)
+    straight_ref[...] = got[: part * sub].reshape(part, sub, width)
+    cross_ref[...] = got[part * sub :, : width // 2].reshape(part, sub, width // 2)
+
+
+def rest_kernel(l_ref, three_ref, metric_ref, pattern_ref, keep_ref, send_ref, spread_ref):
+    l = l_ref[0]
+
+    @pl.when(pl.program_id(0) == 0)
+    def _():
+        spread_metric(l, metric_ref, spread_ref, (0, 2, 1, 3))
+
+    both, part, sub, width = keep_ref.shape
+    block = width // 4
+    data = masked_columns(l, (0, 1, 2, 3), 0, three_ref, pattern_ref[0])
+    half = 2 * part * sub
+    keep_ref[...] = dot(spread_ref[:half], data).astype(BF).reshape(both, part, sub, width)
+    got = dot(spread_ref[half:], data).astype(BF).reshape(both, part, sub, width)
+    for j in range(4):
+        send_ref[:, :, :, j * block : (j + 1) * block] = got[
+            :, :, :, (j ^ 1) * block : ((j ^ 1) + 1) * block
+        ]
+
+
+def local_kernel(
+    l_ref, mine_ref, peer_ref, d0_ref, d1_ref, d2_ref, d3_ref, dp_ref, own_ref, far_ref, left_ref, dens_ref, mask_ref
+):
+    l = l_ref[0]
+    step = pl.program_id(0)
+    width = mine_ref.shape[2]
+    block = width // 4
+    half = width // 2
+
+    @pl.when(step == 0)
+    def _():
+        tiles = dp_ref.shape[0]
+        pat = (dp_ref[...] > 0).astype(BF)
+        tall = (iota((width, tiles), 0) // TILE == iota((width, tiles), 1)).astype(BF)
+        wide = (iota((tiles, width), 1) // TILE == iota((tiles, width), 0)).astype(BF)
+        mask_ref[...] = dot(dot(tall, pat).astype(BF), wide)
+        for i, d_ref in enumerate((d0_ref, d1_ref, d2_ref, d3_ref)):
+            r = pl.multiple_of((l ^ i) * block, block)
+            for j in range(4):
+                c = pl.multiple_of((l ^ j) * block, block)
+                tile = d_ref[:, pl.ds(c, block)].astype(F32) * mask_ref[pl.ds(r, block), pl.ds(c, block)]
+                dens_ref[i * block : (i + 1) * block, j * block : (j + 1) * block] = tile.astype(BF)
+                dens_ref[j * block : (j + 1) * block, width + i * block : width + (i + 1) * block] = tile.T.astype(BF)
+        own_ref[...] = jnp.zeros_like(own_ref)
+        far_ref[...] = jnp.zeros_like(far_ref)
+
+    count = mine_ref.shape[0]
+    near = pl.num_programs(0) // 2
+
+    @pl.when(step < near)
+    def _():
+        for n in range(count):
+            rows = jnp.concatenate([mine_ref[n], peer_ref[n]], axis=0)
+            both = dot(rows, dens_ref[...]).astype(BF)
+            own_ref[...] += dot_t(both[:, :width], rows)
+            far_ref[:half] += dot(both[:, :half], rows[:, half:])
+            far_ref[half:] += dot(both[:, width : width + half], rows[:, half:])
+            left_ref[n, :half] = both[:, half:width]
+            left_ref[n, half:] = both[:, width + half :]
+
+    @pl.when(step >= near)
+    def _():
+        for n in range(count):
+            rows = jnp.concatenate([mine_ref[n], peer_ref[n]], axis=0)
+            one = dot(rows, dens_ref[:, :width]).astype(BF)
+            own_ref[...] += dot_t(one, rows)
+
+
+def far_kernel(left_ref, straight_ref, cross_ref, begun_ref, keep_ref, send_ref, sum_ref):
+    step = pl.program_id(0)
+    count, block, half = straight_ref.shape
+
+    @pl.when(step == 0)
+    def _():
+        sum_ref[...] = begun_ref[...]
+
+    total = sum_ref[...]
+    for n in range(count):
+        top = straight_ref[n]
+        low = jnp.concatenate([top[:, block:].T, cross_ref[n]], axis=1)
+        total += dot(left_ref[n], jnp.concatenate([top, low], axis=0))
+    sum_ref[...] = total
+
+    @pl.when(step == pl.num_programs(0) - 1)
+    def _():
+        ab = sum_ref[:half]
+        ba = sum_ref[half:].T
+        keep_ref[:block] = ab[:block]
+        keep_ref[block:] = ba[:block]
+        send_ref[:block] = jnp.concatenate([ab[block:, block:], ab[block:, :block]], axis=1)
+        send_ref[block:] = jnp.concatenate([ba[block:, block:], ba[block:, :block]], axis=1)
+
+
+def call(kernel, grid, in_specs, out_specs, out_shape, scratch, flops, nbytes, name):
+    return pl.pallas_call(
+        kernel,
+        grid_spec=pltpu.PrefetchScalarGridSpec(
+            num_scalar_prefetch=1, grid=grid, in_specs=in_specs, out_specs=out_specs, scratch_shapes=scratch
+        ),
+        out_shape=out_shape,
+        cost_estimate=pl.CostEstimate(flops=flops, bytes_accessed=nbytes, transcendentals=0),
+        compiler_params=pltpu.CompilerParams(
+            dimension_semantics=("arbitrary",), vmem_limit_bytes=40 * 1024 * 1024
+        ),
+        name=name,
+    )
+
+
+def swap(x, axis, bit):
+    return lax.ppermute(x, axis, [(i, i ^ bit) for i in range(lax.axis_size(axis))])
+
+
+def per_device_four(three, metric, tile_pattern, density, dens_pattern):
+    group, block, width = three.shape
+    part, half = group // 4, width // 2
+    tiles = tile_pattern.shape[2]
+    strips = block // SUB
+    index = lax.axis_index("lay")
+    l = jnp.reshape(index, (1,)).astype(jnp.int32)
+    S = jax.ShapeDtypeStruct
+
+    d1 = swap(density, "lay", 1)
+    d2 = swap(density, "lay", 2)
+    d3 = swap(d2, "lay", 1)
+
+    pattern = lax.dynamic_slice(
+        tile_pattern, (0, index * (block // TILE), 0), (group, block // TILE, tiles)
+    )
+    pattern = (jnp.transpose(pattern, (1, 0, 2)) > 0).astype(BF)
+    per = TILE // SUB
+    common = [
+        pl.BlockSpec((group, group), lambda t, s: (0, 0)),
+        pl.BlockSpec((1, group, tiles), lambda t, s: (t // per, 0, 0)),
+    ]
+    straight, cross = call(
+        near_kernel,
+        (strips,),
+        [pl.BlockSpec((group, SUB, half), lambda t, s: (0, t, s[0] // 2))] + common,
+        [
+            pl.BlockSpec((part, SUB, half), lambda t, s: (0, t, 0)),
+            pl.BlockSpec((part, SUB, block), lambda t, s: (0, t, 0)),
+        ],
+        [S((part, block, half), BF), S((part, block, block), BF)],
+        [pltpu.VMEM((2 * part * SUB, group * SUB), BF)],
+        2 * 2 * part * SUB * group * SUB * half * strips,
+        group * block * half * 4,
+        "near",
+    )(l, three, metric, pattern)
+    straight = swap(straight, "lay", 2)
+    cross = swap(cross, "lay", 3)
+
+    keep, send = call(
+        rest_kernel,
+        (strips,),
+        [pl.BlockSpec((group, SUB, width), lambda t, s: (0, t, 0))] + common,
+        [pl.BlockSpec((2, part, SUB, width), lambda t, s: (0, 0, t, 0))] * 2,
+        [S((2, part, block, width), BF)] * 2,
+        [pltpu.VMEM((group * SUB, group * SUB), BF)],
+        2 * group * SUB * group * SUB * width * strips,
+        group * block * width * 4,
+        "rest",
+    )(l, three, metric, pattern)
+    peer = swap(send, "lay", 1)
+    keep = keep.reshape(2 * part, block, width)
+    peer = peer.reshape(2 * part, block, width)
+
+    count = 2
+    whole = lambda shape: pl.BlockSpec(shape, lambda t, s: (0,) * len(shape))
+    own, far, left = call(
+        local_kernel,
+        (2 * part // count,),
+        [pl.BlockSpec((count, block, width), lambda t, s: (t, 0, 0))] * 2
+        + [whole((block, width))] * 4
+        + [whole(dens_pattern.shape)],
+        [
+            whole((half, half)),
+            whole((width, half)),
+            pl.BlockSpec((count, width, half), lambda t, s: (jnp.minimum(t, part // count - 1), 0, 0)),
+        ],
+        [S((half, half), F32), S((width, half), F32), S((part, width, half), BF)],
+        [pltpu.VMEM((width, 2 * width), BF), pltpu.VMEM((width, width), F32)],
+        2 * part * (2 * half * width * width * 3 + 2 * half * width * half * 3),
+        4 * part * block * width * 2 + part * width * half * 2,
+        "local",
+    )(l, keep, peer, density, d1, d2, d3, dens_pattern)
+
+    count = 4
+    kept, sent = call(
+        lambda l_ref, *refs: far_kernel(*refs),
+        (part // count,),
+        [
+            pl.BlockSpec((count, width, half), lambda t, s: (t, 0, 0)),
+            pl.BlockSpec((count, block, half), lambda t, s: (t, 0, 0)),
+            pl.BlockSpec((count, block, block), lambda t, s: (t, 0, 0)),
+            whole((width, half)),
+        ],
+        [whole((half, half))] * 2,
+        [S((half, half), F32)] * 2,
+        [pltpu.VMEM((width, half), F32)],
+        2 * part * width * half * half,
+        part * width * half * 4,
+        "far",
+    )(l, left, straight, cross, far)
+
+    own_sum = own[:block] + swap(
+        jnp.concatenate([own[block:, block:], own[block:, :block]], axis=1), "lay", 1
+    )
+    far_sum = kept + swap(sent, "lay", 1)
+    far_sum = far_sum[:block] + swap(far_sum[block:], "lay", 2)
+    total = jnp.concatenate([own_sum, far_sum], axis=1)
+    bit = 1
+    while bit < lax.axis_size("blk"):
+        total = total + swap(total, "blk", bit)
+        bit *= 2
+    odd, far_half = index % 2 == 1, index // 2 == 1
+    pairs = total.reshape(block, 2, 2, block)
+    pairs = jnp.where(odd, pairs[:, :, ::-1], pairs)
+    pairs = jnp.where(far_half, pairs[:, ::-1], pairs)
+    return pairs.reshape(block, width)
+
+
 def solution(mesh):
+    groups, layers = mesh.shape["blk"], mesh.shape["lay"]
+    four = layers == 4 and groups & (groups - 1) == 0
     return jax.shard_map(
-        per_device,
+        per_device_four if four else per_device_any,
         mesh=mesh,
         in_specs=(P("blk", "lay", None), P("blk", None), P("blk", None, None), P("lay", None), P()),
         out_specs=P("lay", None),

time: 343 us -> 108 us (0.31)
  blocking collectives: 109 us -> 0 us
  local copies, waits for them, and re-layouts: 80 us -> 11.9 us
  waiting for transfers between devices: 99.6 us -> 42.4 us
  Pallas kernels: 0 us -> 38.8 us
  matrix products: 30.4 us -> 0 us
  starting transfers between devices: 0.04 us -> 14.1 us
  between operations: 13.5 us -> 0.17 us
  other arithmetic: 7.89 us -> 0.49 us
    all_to_all x1 -> x0, blocking collectives: 101 us -> none  [per_device(): lax.all_to_all(outgoing, 'lay', split_axis=0, concat_axis=1, tiled=True)]
    psum x1 -> x0, waiting for transfers between devices: 74.4 us -> none  [per_device(): return lax.psum(row_sums, 'blk')]
    ppermute x0 -> x12, waiting for transfers between devices: none -> 42.4 us  [swap(): lax.ppermute(x, axis, [(i, i ^ bit) for i in range(lax.axis_size(axis))])]
    pallas_call x0 -> x4, Pallas kernels: none -> 38.8 us  [the longest x1 15.2 us: per_device_four(): call(local_kernel, (2 * part // count,), [pl.BlockSpec((count, block, wid...]
    dot_general x3 -> x0, matrix products: 30.4 us -> none  [the longest x1 11.3 us: per_device(): jnp.dot(moved, coeffs.reshape(group_size * row_count, ao_width), preferre...]
    reduce_scatter x1 -> x0, waiting for transfers between devices: 25.2 us -> none  [per_device(): lax.psum_scatter(partial_value, 'lay', scatter_dimension=0, tiled=True)]
    reshape x2, local copies, waits for them, and re-layouts: 26.2 us -> 1.08 us  [the longest x1 0.91 us: per_device_four(): return pairs.reshape(block, width)]
    ppermute x0 -> x12, starting transfers between devices: none -> 14.1 us  [swap(): lax.ppermute(x, axis, [(i, i ^ bit) for i in range(lax.axis_size(axis))])]
  transfers between devices with their start and end apart: 2 -> 12, of which waited for: 2 -> 7; matrix products, arithmetic and copies ran while one was open for 0% -> 0% of each run, Pallas kernels for 0% -> 20%
where the time goes in v1:
time: 108 us
  waiting for transfers between devices  42.4 us (39%)
  Pallas kernels  38.8 us (36%)
  starting transfers between devices  14.1 us (13%)
  local copies, waits for them, and re-layouts  11.9 us (11%)
    ppermute x12, waiting for transfers between devices, swap(): lax.ppermute(x, axis, [(i, i ^ bit) for i in range(lax.axis_size(axis))])  42.4 us
    pallas_call x1, Pallas kernels, per_device_four(): call(local_kernel, (2 * part // count,), [pl.BlockSpec((count, block, wid...  15.2 us
    pallas_call x1, Pallas kernels, per_device_four(): call(rest_kernel, (strips,), [pl.BlockSpec((group, SUB, width), lambda t,...  15 us
    ppermute x12, starting transfers between devices, swap(): lax.ppermute(x, axis, [(i, i ^ bit) for i in range(lax.axis_size(axis))])  14.1 us
    unnamed x19, local copies, waits for them, and re-layouts  10 us
    pallas_call x1, Pallas kernels, per_device_four(): call(near_kernel, (strips,), [pl.BlockSpec((group, SUB, half), lambda t,...  6.43 us
  transfers between devices with their start and end apart: 12, of which 7 were waited for; matrix products, arithmetic and copies ran while one was open for 0% of the time, Pallas kernels for 20%

profile of v1, /device:TPU:0, one launch (start us, length us, event | category | flops | bytes accessed | tf_op | source)
XLA Modules:
  0.0 107.8 jit_solution(9539464650690301747)
XLA Ops:
  0.0 0.9 copy-done
  1.0 0.7 copy-done.2
  1.8 15.0 %rest.1 = (bf16[2,16,128,512]{3,2,1,0:T(8,128)(2,1)S(1)}, bf16[2,16,128,512]{3,2,1,0:T(8,128)(2,1)S(1)}) custom-call(s32[1]{0:T(128)} %bitcast.l_ref, bf16[64,128,512]{2,1,0:T(8,128)(2,1)} %three_ref.3, bf16[64,64]{1,0:T(8,128)(2,1)S(1)} %copy-done.2, bf16[4,64,16]{2,1,0:T(8,128)(2,1)S(1)} %fusion.pattern_ref), custom_call_target="tpu_custom_call" | custom-call | flops 8589934592 | bytes 16777216 | tf_op jit(solution)/shard_map/rest/pallas_call | solution.py:259
  16.8 1.9 %copy-done.7 = bf16[2,16,128,512]{3,2,1,0:T(8,128)(2,1)} copy-done((bf16[2,16,128,512]{3,2,1,0:T(8,128)(2,1)}, bf16[2,16,128,512]{3,2,1,0:T(8,128)(2,1)S(1)}, u32[]{:S(2)}) %copy-start.7) | copy-done | bytes 4194328
  18.7 0.5 collective-permute-start
  19.2 2.6 %collective-permute-start.2 = (bf16[128,512]{1,0:T(8,128)(2,1)S(1)}, bf16[128,512]{1,0:T(8,128)(2,1)S(1)}, u32[]{:S(2)}, u32[]{:S(2)}) collective-permute-start(bf16[128,512]{1,0:T(8,128)(2,1)S(1)} %copy-done.5), channel_id=1, source_target_pairs={{0,2},{1,3},{2,0},{3,1},{4,6},{5,7},{6,4},{7,5},{8,10},{9,11},{10,... | collective-permute-start | bytes 393224 | tf_op jit(solution)/shard_map/ppermute | solution.py:217
  21.8 0.2 collective-permute-start.1
  22.0 3.9 %collective-permute-done.2.d2_ref = bf16[128,512]{1,0:T(8,128)(2,1)S(1)} collective-permute-done((bf16[128,512]{1,0:T(8,128)(2,1)S(1)}, bf16[128,512]{1,0:T(8,128)(2,1)S(1)}, u32[]{:S(2)}, u32[]{:S(2)}) %collective-permute-start.2) | collective-permute-done | bytes 131104 | tf_op jit(solution)/shard_map/ppermute | solution.py:217
  25.9 6.4 %near.1 = (bf16[16,128,256]{2,1,0:T(8,128)(2,1)S(1)}, bf16[16,128,128]{2,1,0:T(8,128)(2,1)S(1)}) custom-call(s32[1]{0:T(128)} %bitcast.l_ref, bf16[64,128,512]{2,1,0:T(8,128)(2,1)S(1)} %copy-done.1, bf16[64,64]{1,0:T(8,128)(2,1)S(1)} %copy-done.2, bf16[4,64,16]{2,1,0:T(8,128)(2,1)S(1)} %fusion.pattern_ref), custom_call_target="tpu_custom_call" | custom-call | flops 2147483648 | bytes 8388608 | tf_op jit(solution)/shard_map/near/pallas_call | solution.py:242
  32.4 1.8 %collective-permute-start.5 = (bf16[16,128,256]{2,1,0:T(8,128)(2,1)S(1)}, bf16[16,128,256]{2,1,0:T(8,128)(2,1)S(1)}, u32[]{:S(2)}, u32[]{:S(2)}) collective-permute-start(bf16[16,128,256]{2,1,0:T(8,128)(2,1)S(1)} %get-tuple-element.18), channel_id=1, source_target_pairs={{0,2},{1,3},{2,0},{3,1},{4,6},{5,7},{6,4},{7,5},{8,10},{9,11},{10,... | collective-permute-start | bytes 3145736 | tf_op jit(solution)/shard_map/ppermute | solution.py:217
  34.2 0.2 collective-permute-start.6
  34.4 2.0 %copy-done.3 = bf16[2,16,128,512]{3,2,1,0:T(8,128)(2,1)} copy-done((bf16[2,16,128,512]{3,2,1,0:T(8,128)(2,1)}, bf16[2,16,128,512]{3,2,1,0:T(8,128)(2,1)S(1)}, u32[]{:S(2)}) %copy-start.3) | copy-done | bytes 4194328
  36.4 2.2 %copy-done.4 = bf16[2,16,128,512]{3,2,1,0:T(8,128)(2,1)S(1)} copy-done((bf16[2,16,128,512]{3,2,1,0:T(8,128)(2,1)S(1)}, bf16[2,16,128,512]{3,2,1,0:T(8,128)(2,1)}, u32[]{:S(2)}) %copy-start.4) | copy-done | bytes 4194328
  38.6 2.2 %copy-done.8 = bf16[2,16,128,512]{3,2,1,0:T(8,128)(2,1)S(1)} copy-done((bf16[2,16,128,512]{3,2,1,0:T(8,128)(2,1)S(1)}, bf16[2,16,128,512]{3,2,1,0:T(8,128)(2,1)}, u32[]{:S(2)}) %copy-start.8) | copy-done | bytes 4194328
  40.8 15.2 %local.1 = (f32[256,256]{1,0:T(8,128)S(1)}, f32[512,256]{1,0:T(8,128)S(1)}, bf16[16,512,256]{2,1,0:T(8,128)(2,1)S(1)}) custom-call(s32[1]{0:T(128)} %bitcast.l_ref, bf16[32,128,512]{2,1,0:T(8,128)(2,1)S(1)} %bitcast.6, bf16[32,128,512]{2,1,0:T(8,128)(2,1)S(1)} %bitcast.5, bf16[128,512]{1,0:T(8,128)(2,1)S(1)} %copy-done.5, ...), custom_call_target="tpu_custom_call" | custom-call | flops 19327352832 | bytes 12582912 | tf_op jit(solution)/shard_map/local/pallas_call | solution.py:276
  56.0 12.8 %collective-permute-done.6.refs_2_ = bf16[16,128,128]{2,1,0:T(8,128)(2,1)S(1)} collective-permute-done((bf16[16,128,128]{2,1,0:T(8,128)(2,1)S(1)}, bf16[16,128,128]{2,1,0:T(8,128)(2,1)S(1)}, u32[]{:S(2)}, u32[]{:S(2)}) %collective-permute-start.6) | collective-permute-done | bytes 524320 | tf_op jit(solution)/shard_map/ppermute | solution.py:217
  68.8 2.1 %far.1 = (f32[256,256]{1,0:T(8,128)S(1)}, f32[256,256]{1,0:T(8,128)S(1)}) custom-call(s32[1]{0:T(128)} %bitcast.l_ref, bf16[16,512,256]{2,1,0:T(8,128)(2,1)S(1)} %get-tuple-element.17.refs_0_, bf16[16,128,256]{2,1,0:T(8,128)(2,1)S(1)} %collective-permute-done.5.refs_1_, bf16[16,128,128]{2,1,0:T(8,128)(2,1)S(1)} %collective-permute-done.6.refs_2_, ...), custom_call_target="tpu_custom_call" | custom-call | flops 1073741824 | bytes 8388608 | tf_op jit(solution)/shard_map/far/pallas_call | solution.py:295
  70.9 0.3 collective-permute-start.7
  71.3 0.3 collective-permute-start.4
  71.6 0.9 collective-permute-done.7
  72.6 1.8 %collective-permute-start.8 = (f32[128,256]{1,0:T(8,128)S(1)}, f32[128,256]{1,0:T(8,128)S(1)}, u32[]{:S(2)}, u32[]{:S(2)}) collective-permute-start(f32[128,256]{1,0:T(8,128)S(1)} %slice.21), channel_id=1, source_target_pairs={{0,2},{1,3},{2,0},{3,1},{4,6},{5,7},{6,4},{7,5},{8,10},{9,11},{10,... | collective-permute-start | bytes 393224 | tf_op jit(solution)/shard_map/ppermute | solution.py:217
  74.4 3.9 %collective-permute-done.8 = f32[128,256]{1,0:T(8,128)S(1)} collective-permute-done((f32[128,256]{1,0:T(8,128)S(1)}, f32[128,256]{1,0:T(8,128)S(1)}, u32[]{:S(2)}, u32[]{:S(2)}) %collective-permute-start.8) | collective-permute-done | bytes 131104 | tf_op jit(solution)/shard_map/ppermute | solution.py:217
  78.3 1.7 %collective-permute-start.9 = (f32[128,512]{1,0:T(8,128)S(1)}, f32[128,512]{1,0:T(8,128)S(1)}, u32[]{:S(2)}, u32[]{:S(2)}) collective-permute-start(f32[128,512]{1,0:T(8,128)S(1)} %pad_maximum_fusion), channel_id=1, source_target_pairs={{0,4},{4,0},{8,12},{12,8},{16,20},{20,16},{24,28},{28,24},{1,5},{5... | collective-permute-start | bytes 786440 | tf_op jit(solution)/shard_map/ppermute | solution.py:217
  80.1 6.0 %collective-permute-done.9 = f32[128,512]{1,0:T(8,128)S(1)} collective-permute-done((f32[128,512]{1,0:T(8,128)S(1)}, f32[128,512]{1,0:T(8,128)S(1)}, u32[]{:S(2)}, u32[]{:S(2)}) %collective-permute-start.9) | collective-permute-done | bytes 262176 | tf_op jit(solution)/shard_map/ppermute | solution.py:217
  86.1 1.8 %collective-permute-start.10 = (f32[128,512]{1,0:T(8,128)S(1)}, f32[128,512]{1,0:T(8,128)S(1)}, u32[]{:S(2)}, u32[]{:S(2)}) collective-permute-start(f32[128,512]{1,0:T(8,128)S(1)} %fusion.1), channel_id=1, source_target_pairs={{0,8},{4,12},{8,0},{12,4},{16,24},{20,28},{24,16},{28,20},{1,9},{5... | collective-permute-start | bytes 786440 | tf_op jit(solution)/shard_map/ppermute | solution.py:217
  87.9 5.0 %collective-permute-done.10 = f32[128,512]{1,0:T(8,128)S(1)} collective-permute-done((f32[128,512]{1,0:T(8,128)S(1)}, f32[128,512]{1,0:T(8,128)S(1)}, u32[]{:S(2)}, u32[]{:S(2)}) %collective-permute-start.10) | collective-permute-done | bytes 262176 | tf_op jit(solution)/shard_map/ppermute | solution.py:217
  93.0 2.8 %collective-permute-start.11 = (f32[128,512]{1,0:T(8,128)S(1)}, f32[128,512]{1,0:T(8,128)S(1)}, u32[]{:S(2)}, u32[]{:S(2)}) collective-permute-start(f32[128,512]{1,0:T(8,128)S(1)} %add.32), channel_id=1, source_target_pairs={{0,16},{4,20},{8,24},{12,28},{16,0},{20,4},{24,8},{28,12},{1,17},{... | collective-permute-start | bytes 786440 | tf_op jit(solution)/shard_map/ppermute | solution.py:217
  95.8 9.8 %collective-permute-done.11 = f32[128,512]{1,0:T(8,128)S(1)} collective-permute-done((f32[128,512]{1,0:T(8,128)S(1)}, f32[128,512]{1,0:T(8,128)S(1)}, u32[]{:S(2)}, u32[]{:S(2)}) %collective-permute-start.11) | collective-permute-done | bytes 262176 | tf_op jit(solution)/shard_map/ppermute | solution.py:217
  105.7 0.2 reshape.18
  105.9 0.7 rev.6
  106.6 0.1 broadcast_select_fusion
  106.9 0.9 reshape.19
  (32 shorter events, 0.5 us)
Async XLA Ops:
  0.0 0.9 copy-start
  1.0 0.7 copy-start.2
  1.8 17.5 %copy-start.5 = (bf16[128,512]{1,0:T(8,128)(2,1)S(1)}, bf16[128,512]{1,0:T(8,128)(2,1)}, u32[]{:S(2)}) copy-start(bf16[128,512]{1,0:T(8,128)(2,1)} %d0_ref.1) | copy-start | bytes 393220
  1.8 24.2 %copy-start.1 = (bf16[64,128,512]{2,1,0:T(8,128)(2,1)S(1)}, bf16[64,128,512]{2,1,0:T(8,128)(2,1)}, u32[]{:S(2)}) copy-start(bf16[64,128,512]{2,1,0:T(8,128)(2,1)} %three_ref.3) | copy-start | bytes 25165828
  16.8 1.9 %copy-start.7 = (bf16[2,16,128,512]{3,2,1,0:T(8,128)(2,1)}, bf16[2,16,128,512]{3,2,1,0:T(8,128)(2,1)S(1)}, u32[]{:S(2)}) copy-start(bf16[2,16,128,512]{3,2,1,0:T(8,128)(2,1)S(1)} %get-tuple-element.14) | copy-start | bytes 12582916
  18.7 17.7 %copy-start.6 = (s32[16,16]{1,0:T(8,128)S(1)}, s32[16,16]{1,0:T(8,128)}, u32[]{:S(2)}) copy-start(s32[16,16]{1,0:T(8,128)} %dp_ref.1) | copy-start | bytes 3076
  18.7 15.7 %collective-permute-start = (bf16[2,16,128,512]{3,2,1,0:T(8,128)(2,1)S(1)}, bf16[2,16,128,512]{3,2,1,0:T(8,128)(2,1)S(1)}, u32[]{:S(2)}, u32[]{:S(2)}) collective-permute-start(bf16[2,16,128,512]{3,2,1,0:T(8,128)(2,1)S(1)} %get-tuple-element.15), channel_id=1, source_target_pairs={{0,1},{1,0},{2,3},{3,2},{4,5},{5,4},{6,7},{7,6},{8,9},{9,8},{10,11... | collective-permute-start | bytes 12582920 | tf_op jit(solution)/shard_map/ppermute | solution.py:217
  19.2 6.7 %collective-permute-start.2 = (bf16[128,512]{1,0:T(8,128)(2,1)S(1)}, bf16[128,512]{1,0:T(8,128)(2,1)S(1)}, u32[]{:S(2)}, u32[]{:S(2)}) collective-permute-start(bf16[128,512]{1,0:T(8,128)(2,1)S(1)} %copy-done.5), channel_id=1, source_target_pairs={{0,2},{1,3},{2,0},{3,1},{4,6},{5,7},{6,4},{7,5},{8,10},{9,11},{10,... | collective-permute-start | bytes 393224 | tf_op jit(solution)/shard_map/ppermute | solution.py:217
  21.8 12.6 %collective-permute-start.1 = (bf16[128,512]{1,0:T(8,128)(2,1)S(1)}, bf16[128,512]{1,0:T(8,128)(2,1)S(1)}, u32[]{:S(2)}, u32[]{:S(2)}) collective-permute-start(bf16[128,512]{1,0:T(8,128)(2,1)S(1)} %copy-done.5), channel_id=1, source_target_pairs={{0,1},{1,0},{2,3},{3,2},{4,5},{5,4},{6,7},{7,6},{8,9},{9,8},{10,11... | collective-permute-start | bytes 393224 | tf_op jit(solution)/shard_map/ppermute | solution.py:217
  25.9 8.5 %collective-permute-start.3 = (bf16[128,512]{1,0:T(8,128)(2,1)S(1)}, bf16[128,512]{1,0:T(8,128)(2,1)S(1)}, u32[]{:S(2)}, u32[]{:S(2)}) collective-permute-start(bf16[128,512]{1,0:T(8,128)(2,1)S(1)} %collective-permute-done.2.d2_ref), channel_id=1, source_target_pairs={{0,1},{1,0},{2,3},{3,2},{4,5},{5,4},{6,7},{7,6},{8,9},{9,8},{10,11... | collective-permute-start | bytes 393224 | tf_op jit(solution)/shard_map/ppermute | solution.py:217
  32.4 36.4 %collective-permute-start.5 = (bf16[16,128,256]{2,1,0:T(8,128)(2,1)S(1)}, bf16[16,128,256]{2,1,0:T(8,128)(2,1)S(1)}, u32[]{:S(2)}, u32[]{:S(2)}) collective-permute-start(bf16[16,128,256]{2,1,0:T(8,128)(2,1)S(1)} %get-tuple-element.18), channel_id=1, source_target_pairs={{0,2},{1,3},{2,0},{3,1},{4,6},{5,7},{6,4},{7,5},{8,10},{9,11},{10,... | collective-permute-start | bytes 3145736 | tf_op jit(solution)/shard_map/ppermute | solution.py:217
  34.2 34.6 %collective-permute-start.6 = (bf16[16,128,128]{2,1,0:T(8,128)(2,1)S(1)}, bf16[16,128,128]{2,1,0:T(8,128)(2,1)S(1)}, u32[]{:S(2)}, u32[]{:S(2)}) collective-permute-start(bf16[16,128,128]{2,1,0:T(8,128)(2,1)S(1)} %get-tuple-element.19), channel_id=1, source_target_pairs={{0,3},{1,2},{2,1},{3,0},{4,7},{5,6},{6,5},{7,4},{8,11},{9,10},{10,... | collective-permute-start | bytes 1572872 | tf_op jit(solution)/shard_map/ppermute | solution.py:217
  34.4 2.0 %copy-start.3 = (bf16[2,16,128,512]{3,2,1,0:T(8,128)(2,1)}, bf16[2,16,128,512]{3,2,1,0:T(8,128)(2,1)S(1)}, u32[]{:S(2)}) copy-start(bf16[2,16,128,512]{3,2,1,0:T(8,128)(2,1)S(1)} %collective-permute-done) | copy-start | bytes 12582916
  36.4 2.2 %copy-start.4 = (bf16[2,16,128,512]{3,2,1,0:T(8,128)(2,1)S(1)}, bf16[2,16,128,512]{3,2,1,0:T(8,128)(2,1)}, u32[]{:S(2)}) copy-start(bf16[2,16,128,512]{3,2,1,0:T(8,128)(2,1)} %copy-done.3) | copy-start | bytes 12582916
  38.6 2.2 %copy-start.8 = (bf16[2,16,128,512]{3,2,1,0:T(8,128)(2,1)S(1)}, bf16[2,16,128,512]{3,2,1,0:T(8,128)(2,1)}, u32[]{:S(2)}) copy-start(bf16[2,16,128,512]{3,2,1,0:T(8,128)(2,1)} %copy-done.7) | copy-start | bytes 12582916
  70.9 1.6 %collective-permute-start.7 = (f32[256,256]{1,0:T(8,128)S(1)}, f32[256,256]{1,0:T(8,128)S(1)}, u32[]{:S(2)}, u32[]{:S(2)}) collective-permute-start(f32[256,256]{1,0:T(8,128)S(1)} %get-tuple-element.22), channel_id=1, source_target_pairs={{0,1},{1,0},{2,3},{3,2},{4,5},{5,4},{6,7},{7,6},{8,9},{9,8},{10,11... | collective-permute-start | bytes 786440 | tf_op jit(solution)/shard_map/ppermute | solution.py:217
  71.3 3.1 %collective-permute-start.4 = (f32[128,256]{1,0:T(8,128)S(1)}, f32[128,256]{1,0:T(8,128)S(1)}, u32[]{:S(2)}, u32[]{:S(2)}) collective-permute-start(f32[128,256]{1,0:T(8,128)S(1)} %pad_maximum_fusion.1), channel_id=1, source_target_pairs={{0,1},{1,0},{2,3},{3,2},{4,5},{5,4},{6,7},{7,6},{8,9},{9,8},{10,11... | collective-permute-start | bytes 393224 | tf_op jit(solution)/shard_map/ppermute | solution.py:217
  72.6 5.7 %collective-permute-start.8 = (f32[128,256]{1,0:T(8,128)S(1)}, f32[128,256]{1,0:T(8,128)S(1)}, u32[]{:S(2)}, u32[]{:S(2)}) collective-permute-start(f32[128,256]{1,0:T(8,128)S(1)} %slice.21), channel_id=1, source_target_pairs={{0,2},{1,3},{2,0},{3,1},{4,6},{5,7},{6,4},{7,5},{8,10},{9,11},{10,... | collective-permute-start | bytes 393224 | tf_op jit(solution)/shard_map/ppermute | solution.py:217
  78.3 7.7 %collective-permute-start.9 = (f32[128,512]{1,0:T(8,128)S(1)}, f32[128,512]{1,0:T(8,128)S(1)}, u32[]{:S(2)}, u32[]{:S(2)}) collective-permute-start(f32[128,512]{1,0:T(8,128)S(1)} %pad_maximum_fusion), channel_id=1, source_target_pairs={{0,4},{4,0},{8,12},{12,8},{16,20},{20,16},{24,28},{28,24},{1,5},{5... | collective-permute-start | bytes 786440 | tf_op jit(solution)/shard_map/ppermute | solution.py:217
  86.1 6.9 %collective-permute-start.10 = (f32[128,512]{1,0:T(8,128)S(1)}, f32[128,512]{1,0:T(8,128)S(1)}, u32[]{:S(2)}, u32[]{:S(2)}) collective-permute-start(f32[128,512]{1,0:T(8,128)S(1)} %fusion.1), channel_id=1, source_target_pairs={{0,8},{4,12},{8,0},{12,4},{16,24},{20,28},{24,16},{28,20},{1,9},{5... | collective-permute-start | bytes 786440 | tf_op jit(solution)/shard_map/ppermute | solution.py:217
  93.0 12.6 %collective-permute-start.11 = (f32[128,512]{1,0:T(8,128)S(1)}, f32[128,512]{1,0:T(8,128)S(1)}, u32[]{:S(2)}, u32[]{:S(2)}) collective-permute-start(f32[128,512]{1,0:T(8,128)S(1)} %add.32), channel_id=1, source_target_pairs={{0,16},{4,20},{8,24},{12,28},{16,0},{20,4},{24,8},{28,12},{1,17},{... | collective-permute-start | bytes 786440 | tf_op jit(solution)/shard_map/ppermute | solution.py:217

commit v2 on v0

--- a/solution.py
+++ b/solution.py
@@ -1,9 +1,16 @@
+import functools
 import jax
 import jax.numpy as jnp
 from jax import lax
+from jax.experimental import pallas as pl
+from jax.experimental.pallas import tpu as pltpu
 from jax.sharding import PartitionSpec as P
 
+
 TILE = 32
+SUB = 16
+BF = jnp.bfloat16
+F32 = jnp.float32
 
 
 def density_adder(left_side, dens_pattern, segment):
@@ -15,7 +22,7 @@
     return jnp.dot(left_side, kept, preferred_element_type=jnp.float32)
 
 
-def per_device(three_centre, metric, tile_pattern, density, dens_pattern):
+def per_device_any(three_centre, metric, tile_pattern, density, dens_pattern):
     group_size = three_centre.shape[0]
     row_count = three_centre.shape[1]
     ao_width = three_centre.shape[2]
@@ -46,9 +53,360 @@
     return lax.psum(row_sums, "blk")
 
 
+def dot(a, b):
+    return jnp.dot(a, b, preferred_element_type=F32)
+
+
+def dot_t(a, b):
+    return lax.dot_general(a, b, (((1,), (1,)), ((), ())), preferred_element_type=F32)
+
+
+def iota(shape, dim):
+    return lax.broadcasted_iota(jnp.int32, shape, dim)
+
+
+def spread_metric(l, metric_ref, spread_ref, orders):
+    group = metric_ref.shape[0]
+    part = group // 4
+    rows, cols = part * SUB, group * SUB
+    widen = (iota((rows, part), 0) // SUB == iota((rows, part), 1)).astype(BF)
+    along = (iota((group, cols), 1) // SUB == iota((group, cols), 0)).astype(BF)
+    same = iota((rows, cols), 0) % SUB == iota((rows, cols), 1) % SUB
+    for n, p in enumerate(orders):
+        start = pl.multiple_of((l ^ p) * part, part)
+        tall = dot(widen, metric_ref[pl.ds(start, part), :]).astype(BF)
+        full = dot(tall, along)
+        spread_ref[n * rows : (n + 1) * rows, :] = jnp.where(same, full, 0.0).astype(BF)
+
+
+def masked_columns(l, order, base, three_ref, pattern_ref):
+    group, sub, _ = three_ref.shape
+    tiles = pattern_ref.shape[1]
+    block = tiles * TILE // 4
+    pattern = (pattern_ref[0] > 0).astype(BF)
+    out = []
+    for j in order:
+        start = (l ^ j) * block
+        here = (iota((tiles, block), 0) == (start // TILE) + iota((tiles, block), 1) // TILE).astype(BF)
+        mask = lax.dot_general(pattern, here, (((0,), (0,)), ((), ())), preferred_element_type=F32)
+        mask = jnp.broadcast_to(mask[:, None, :], (group, sub, block)).astype(BF)
+        piece = three_ref[:, :, pl.ds(pl.multiple_of(start - base, block), block)]
+        out.append((piece * mask).reshape(group * sub, block))
+    return jnp.concatenate(out, axis=1)
+
+
+def near_kernel(l_ref, three_ref, metric_ref, pattern_ref, straight_ref, cross_ref, core_ref, spread_ref):
+    l = l_ref[0]
+
+    @pl.when(pl.program_id(0) == 0)
+    def _():
+        spread_metric(l, metric_ref, spread_ref, (2, 3))
+
+    part, sub, width = straight_ref.shape
+    block = width // 2
+    data = masked_columns(l, (0, 1), (l // 2) * width, three_ref, pattern_ref)
+    got = dot(spread_ref[...], data).astype(BF)
+    straight_ref[...] = got[: part * sub].reshape(part, sub, width)
+    low = got[part * sub :].reshape(part, sub, width)
+    cross_ref[...] = low[:, :, :block]
+    core_ref[:, :, :block] = low[:, :, block:]
+    core_ref[:, :, block:] = low[:, :, :block]
+
+
+def swapped(x, block):
+    parts = []
+    for j in range(x.shape[-1] // block):
+        k = j ^ 1
+        parts.append(x[..., k * block : (k + 1) * block])
+    return jnp.concatenate(parts, axis=-1)
+
+
+def rest_kernel(l_ref, three_ref, metric_ref, pattern_ref, keep_ref, send_ref, spread_ref, *, cut, orders):
+    l = l_ref[0]
+
+    @pl.when(pl.program_id(0) == 0)
+    def _():
+        spread_metric(l, metric_ref, spread_ref, orders)
+
+    part, sub, width = keep_ref.shape
+    block = width // len(cut)
+    base = (l ^ cut[0]) // 2 * width if len(cut) == 2 else 0
+    data = masked_columns(l, cut, base, three_ref, pattern_ref)
+    got = dot(spread_ref[...], data).astype(BF)
+    keep_ref[...] = got[: part * sub].reshape(part, sub, width)
+    send_ref[...] = swapped(got[part * sub :].reshape(part, sub, width), block)
+
+
+def settle_kernel(l_ref, d0_ref, d1_ref, d2_ref, d3_ref, dp_ref, dens_ref, mask_ref):
+    l = l_ref[0]
+    block, width = d0_ref.shape
+    tiles = dp_ref.shape[0]
+    pat = (dp_ref[...] > 0).astype(BF)
+    tall = (iota((width, tiles), 0) // TILE == iota((width, tiles), 1)).astype(BF)
+    wide = (iota((tiles, width), 1) // TILE == iota((tiles, width), 0)).astype(BF)
+    mask_ref[...] = dot(dot(tall, pat).astype(BF), wide)
+    for i, d_ref in enumerate((d0_ref, d1_ref, d2_ref, d3_ref)):
+        r = pl.multiple_of((l ^ i) * block, block)
+        for j in range(4):
+            c = pl.multiple_of((l ^ j) * block, block)
+            tile = d_ref[:, pl.ds(c, block)].astype(F32) * mask_ref[pl.ds(r, block), pl.ds(c, block)]
+            dens_ref[i * block : (i + 1) * block, j * block : (j + 1) * block] = tile.astype(BF)
+            dens_ref[j * block : (j + 1) * block, width + i * block : width + (i + 1) * block] = tile.T.astype(BF)
+
+
+def own_kernel(a_ref, pa_ref, b0_ref, b1_ref, pb0_ref, pb1_ref, dens_ref, inter_ref, keep_ref, send_ref, sum_ref):
+    step = pl.program_id(0)
+    count, block, _ = a_ref.shape
+    dens = dens_ref[...]
+
+    @pl.when(step == 0)
+    def _():
+        sum_ref[...] = jnp.zeros_like(sum_ref)
+
+    total = sum_ref[...]
+    for n in range(count):
+        rows = jnp.concatenate([a_ref[n], pa_ref[n]], axis=0)
+        inter = dot(rows, dens).astype(BF)
+        inter_ref[n] = inter
+        total += dot_t(inter, rows)
+        top = jnp.concatenate([b0_ref[n], b1_ref[n]], axis=1)
+        low = jnp.concatenate([pb0_ref[n], pb1_ref[n]], axis=1)
+        rows = jnp.concatenate([top, low], axis=0)
+        total += dot_t(dot(rows, dens).astype(BF), rows)
+    sum_ref[...] = total
+
+    @pl.when(step == pl.num_programs(0) - 1)
+    def _():
+        keep_ref[...] = total[:block]
+        send_ref[...] = swapped(total[block:], block)
+
+
+def local_kernel(a_ref, pa_ref, inter_ref, dens_ref, left_ref, far_ref):
+    step = pl.program_id(0)
+    count, _, width = a_ref.shape
+    half = width // 2
+
+    @pl.when(step == 0)
+    def _():
+        far_ref[...] = jnp.zeros_like(far_ref)
+
+    dens = dens_ref[...]
+    for n in range(count):
+        rows = jnp.concatenate([a_ref[n], pa_ref[n]], axis=0)
+        turned = dot(rows, dens).astype(BF)
+        side = rows[:, half:]
+        far_ref[:half] += dot(inter_ref[n, :, :half], side)
+        far_ref[half:] += dot(turned[:, :half], side)
+        left_ref[n, :half] = inter_ref[n, :, half:]
+        left_ref[n, half:] = turned[:, half:]
+
+
+def far_kernel(left_ref, straight_ref, cross_ref, begun_ref, keep_ref, send_ref, sum_ref):
+    step = pl.program_id(0)
+    count, block, half = straight_ref.shape
+
+    @pl.when(step == 0)
+    def _():
+        sum_ref[...] = begun_ref[...]
+
+    total = sum_ref[...]
+    for n in range(count):
+        top = straight_ref[n]
+        low = jnp.concatenate([top[:, block:].T, cross_ref[n]], axis=1)
+        total += dot(left_ref[n], jnp.concatenate([top, low], axis=0))
+    sum_ref[...] = total
+
+    @pl.when(step == pl.num_programs(0) - 1)
+    def _():
+        ab = total[:half]
+        ba = total[half:].T
+        keep_ref[:block] = ab[:block]
+        keep_ref[block:] = ba[:block]
+        send_ref[:block] = swapped(ab[block:], block)
+        send_ref[block:] = swapped(ba[block:], block)
+
+
+def place_kernel(l_ref, own_ref, own_got_ref, far_ref, far_got_ref, out_ref):
+    l = l_ref[0]
+    block = out_ref.shape[0]
+    for j, (a_ref, b_ref) in enumerate(((own_ref, own_got_ref),) * 2 + ((far_ref, far_got_ref),) * 2):
+        at = j % 2 * block
+        total = a_ref[:, at : at + block] + b_ref[:, at : at + block].astype(F32)
+        out_ref[:, pl.ds(pl.multiple_of((l ^ j) * block, block), block)] = total
+
+
+def call(kernel, grid, in_specs, out_specs, out_shape, scratch, flops, nbytes, vmem=20):
+    return pl.pallas_call(
+        kernel,
+        grid_spec=pltpu.PrefetchScalarGridSpec(
+            num_scalar_prefetch=1, grid=grid, in_specs=in_specs, out_specs=out_specs, scratch_shapes=scratch
+        ),
+        out_shape=out_shape,
+        cost_estimate=pl.CostEstimate(flops=flops, bytes_accessed=nbytes, transcendentals=0),
+        compiler_params=pltpu.CompilerParams(
+            dimension_semantics=("arbitrary",), vmem_limit_bytes=vmem * 1024 * 1024
+        ),
+    )
+
+
+def no_index(kernel):
+    return lambda l_ref, *refs: kernel(*refs)
+
+
+def swap(x, axis, bit):
+    return lax.ppermute(x, axis, [(i, i ^ bit) for i in range(lax.axis_size(axis))])
+
+
+def rounded(x):
+    return lax.reduce_precision(x, 8, 7)
+
+
+def bits_of(groups):
+    return [1 << n for n in range(groups.bit_length() - 1)]
+
+
+def per_device_four(three, metric, tile_pattern, density, dens_pattern):
+    return exchange_four(three, metric, tile_pattern, density, dens_pattern)
+
+
+def exchange_four(three, metric, tile_pattern, density, dens_pattern):
+    group, block, width = three.shape
+    part, half = group // 4, width // 2
+    tiles = tile_pattern.shape[2]
+    strips = block // SUB
+    index = lax.axis_index("lay")
+    l = jnp.reshape(index, (1,)).astype(jnp.int32)
+    S = jax.ShapeDtypeStruct
+    whole = lambda shape: pl.BlockSpec(shape, lambda t, s: (0,) * len(shape))
+
+    d2 = swap(density, "lay", 2)
+    d1 = swap(density, "lay", 1)
+    d3 = swap(d2, "lay", 1)
+
+    pattern = jnp.transpose(tile_pattern, (1, 2, 0))
+    per, here = TILE // SUB, block // TILE
+    common = [
+        pl.BlockSpec((group, group), lambda t, s: (0, 0)),
+        pl.BlockSpec((1, tiles, group), lambda t, s: (s[0] * here + t // per, 0, 0)),
+    ]
+    strip = lambda n: pl.BlockSpec((part, SUB, n), lambda t, s: (0, t, 0))
+    straight, cross, send3 = call(
+        near_kernel,
+        (strips,),
+        [pl.BlockSpec((group, SUB, half), lambda t, s: (0, t, s[0] // 2))] + common,
+        [strip(half), strip(block), strip(half)],
+        [S((part, block, half), BF), S((part, block, block), BF), S((part, block, half), BF)],
+        [pltpu.VMEM((2 * part * SUB, group * SUB), BF)],
+        2 * 2 * part * SUB * group * SUB * half * strips,
+        group * block * half * 4,
+        vmem=NEAR_VMEM,
+    )(l, three, metric, pattern)
+    far_straight = swap(straight, "lay", 2)
+    far_cross = swap(cross, "lay", 3)
+    got3 = swap(send3, "lay", 1)
+
+    def rest(cut, orders, columns):
+        n = len(cut) * block
+        return call(
+            functools.partial(rest_kernel, cut=cut, orders=orders),
+            (strips,),
+            [pl.BlockSpec((group, SUB, n), columns)] + common,
+            [strip(n)] * 2,
+            [S((part, block, n), BF)] * 2,
+            [pltpu.VMEM((2 * part * SUB, group * SUB), BF)],
+            2 * 2 * part * SUB * group * SUB * n * strips,
+            group * block * n * 4,
+            vmem=NEAR_VMEM,
+        )(l, three, metric, pattern)
+
+    keep0, send1 = rest((0, 1, 2, 3), (0, 1), lambda t, s: (0, t, 0))
+    got1 = swap(send1, "lay", 1)
+    keep2, send4 = rest((2, 3), (2, 3), lambda t, s: (0, t, 1 - s[0] // 2))
+    got4 = swap(send4, "lay", 1)
+
+    dens = call(
+        settle_kernel,
+        (1,),
+        [whole((block, width))] * 4 + [whole(dens_pattern.shape)],
+        whole((width, 2 * width)),
+        S((width, 2 * width), BF),
+        [pltpu.VMEM((width, width), F32)],
+        4 * width * width * tiles,
+        4 * width * width * 2,
+    )(l, density, d1, d2, d3, dens_pattern)
+
+    count = 2
+    many = lambda a, b: pl.BlockSpec((count, a, b), lambda t, s: (t, 0, 0))
+    inter, own_keep, own_send = call(
+        no_index(own_kernel),
+        (part // count,),
+        [many(block, width)] * 2 + [many(block, half)] * 4 + [pl.BlockSpec((width, width), lambda t, s: (0, 0))],
+        [many(half, width), whole((block, half)), whole((block, half))],
+        [S((part, half, width), BF), S((block, half), F32), S((block, half), F32)],
+        [pltpu.VMEM((half, half), F32)],
+        2 * part * 2 * half * width * (width + half),
+        2 * part * half * width * 2,
+    )(l, keep0, got1, straight, keep2, got3, got4, dens)
+    own = own_keep + swap(own_send, "lay", 1)
+
+    left, far = call(
+        no_index(local_kernel),
+        (part // count,),
+        [many(block, width)] * 2
+        + [many(half, width), pl.BlockSpec((width, width), lambda t, s: (0, 1))],
+        [many(width, half), whole((width, half))],
+        [S((part, width, half), BF), S((width, half), F32)],
+        [],
+        part * 2 * half * (width * width + 2 * half * half),
+        part * half * width * 8,
+    )(l, keep0, got1, inter, dens)
+
+    count = 4
+    kept, sent = call(
+        no_index(far_kernel),
+        (part // count,),
+        [many(width, half), many(block, half), many(block, block), whole((width, half))],
+        [whole((half, half))] * 2,
+        [S((half, half), F32)] * 2,
+        [pltpu.VMEM((width, half), F32)],
+        2 * part * width * half * half,
+        part * width * half * 4,
+    )(l, left, far_straight, far_cross, far)
+    far = kept + swap(sent, "lay", 1)
+    far = far[:block] + swap(far[block:].astype(BF), "lay", 2).astype(F32)
+
+    def over_groups(x):
+        steps = bits_of(lax.axis_size("blk"))
+        for n, bit in enumerate(steps):
+            x = rounded(x)
+            got = swap(x.astype(BF), "blk", bit if n < 2 else bit | steps[n - 1])
+            if n == len(steps) - 1:
+                return x, got
+            x = x + got.astype(F32)
+        return x, jnp.zeros(x.shape, BF)
+
+    own, own_got = over_groups(own)
+    far, far_got = over_groups(far)
+    return call(
+        place_kernel,
+        (1,),
+        [whole((block, half))] * 4,
+        whole((block, width)),
+        S((block, width), F32),
+        [],
+        block * width,
+        block * width * 10,
+    )(l, own, own_got, far, far_got)
+
+
+NEAR_VMEM = 57
+
+
 def solution(mesh):
+    groups, layers = mesh.shape["blk"], mesh.shape["lay"]
+    four = layers == 4 and groups & (groups - 1) == 0
     return jax.shard_map(
-        per_device,
+        per_device_four if four else per_device_any,
         mesh=mesh,
         in_specs=(P("blk", "lay", None), P("blk", None), P("blk", None, None), P("lay", None), P()),
         out_specs=P("lay", None),

time: 343 us -> 98.9 us (0.29)
  blocking collectives: 109 us -> 0 us
  local copies, waits for them, and re-layouts: 80 us -> 1.25 us
  waiting for transfers between devices: 99.6 us -> 23.1 us
  Pallas kernels: 0 us -> 50.6 us
  matrix products: 30.4 us -> 0 us
  starting transfers between devices: 0.04 us -> 22.9 us
  between operations: 13.5 us -> 0.15 us
  other arithmetic: 7.89 us -> 0.21 us
    all_to_all x1 -> x0, blocking collectives: 101 us -> none  [per_device(): lax.all_to_all(outgoing, 'lay', split_axis=0, concat_axis=1, tiled=True)]
    psum x1 -> x0, waiting for transfers between devices: 74.4 us -> none  [per_device(): return lax.psum(row_sums, 'blk')]
    pallas_call x0 -> x8, Pallas kernels: none -> 50.6 us  [the longest x2 21.9 us: rest(): call(functools.partial(rest_kernel, cut=cut, orders=orders), (strips,), [...]
    dot_general x3 -> x0, matrix products: 30.4 us -> none  [the longest x1 11.3 us: per_device(): jnp.dot(moved, coeffs.reshape(group_size * row_count, ao_width), preferre...]
    reshape x2 -> x0, local copies, waits for them, and re-layouts: 26.2 us -> none  [per_device(): inter.astype(jnp.bfloat16)]
    reduce_scatter x1 -> x0, waiting for transfers between devices: 25.2 us -> none  [per_device(): lax.psum_scatter(partial_value, 'lay', scatter_dimension=0, tiled=True)]
    ppermute x0 -> x17, waiting for transfers between devices: none -> 23.1 us  [swap(): lax.ppermute(x, axis, [(i, i ^ bit) for i in range(lax.axis_size(axis))])]
    ppermute x0 -> x17, starting transfers between devices: none -> 22.9 us  [swap(): lax.ppermute(x, axis, [(i, i ^ bit) for i in range(lax.axis_size(axis))])]
  transfers between devices with their start and end apart: 2 -> 17, of which waited for: 2 -> 9; matrix products, arithmetic and copies ran while one was open for 0% -> 0% of each run, Pallas kernels for 0% -> 36%
where the time goes in v2:
time: 98.9 us; the launch traced here: 98.2 us
  Pallas kernels  50.6 us (51%)
  waiting for transfers between devices  23.1 us (23%)
  starting transfers between devices  22.9 us (23%)
  local copies, waits for them, and re-layouts  1.25 us (1%)
    ppermute x17, waiting for transfers between devices, swap(): lax.ppermute(x, axis, [(i, i ^ bit) for i in range(lax.axis_size(axis))])  23.1 us
    ppermute x17, starting transfers between devices, swap(): lax.ppermute(x, axis, [(i, i ^ bit) for i in range(lax.axis_size(axis))])  22.9 us
    pallas_call x2, Pallas kernels, rest(): call(functools.partial(rest_kernel, cut=cut, orders=orders), (strips,), [...  21.9 us
    pallas_call x1, Pallas kernels, exchange_four(): call(no_index(own_kernel), (part // count,), [many(block, width)] * 2 + [...  10.3 us
    pallas_call x1, Pallas kernels, exchange_four(): call(near_kernel, (strips,), [pl.BlockSpec((group, SUB, half), lambda t,...  9.64 us
    pallas_call x1, Pallas kernels, exchange_four(): call(no_index(local_kernel), (part // count,), [many(block, width)] * 2 +...  5.22 us
    pallas_call x1, Pallas kernels, exchange_four(): call(no_index(far_kernel), (part // count,), [many(width, half), many(blo...  2.12 us
  transfers between devices with their start and end apart: 17, of which 9 were waited for; matrix products, arithmetic and copies ran while one was open for 0% of the time, Pallas kernels for 36%

profile of v2, /device:TPU:0, one launch (start us, length us, event | category | flops | bytes accessed | tf_op | source)
XLA Modules:
  0.0 98.2 jit_solution(17253861445911061730)
XLA Ops:
  0.0 12.2 %shard_map.55 = (bf16[16,128,512]{2,1,0:T(8,128)(2,1)}, bf16[16,128,512]{2,1,0:T(8,128)(2,1)}) custom-call(s32[1]{0:T(128)} %bitcast.l_ref, bf16[64,128,512]{2,1,0:T(8,128)(2,1)} %three_ref.5, bf16[64,64]{1,0:T(8,128)(2,1)} %metric_ref.5, s32[16,16,64]{2,1,0:T(8,128)} %bitcast.2), custom_call_target="tpu_custom_call" | custom-call | flops 4294967296 | bytes 16777216 | tf_op jit(solution)/shard_map/pallas_call | solution.py:310
  12.2 0.5 collective-permute-start
  12.7 9.6 %shard_map.56 = (bf16[16,128,256]{2,1,0:T(8,128)(2,1)}, bf16[16,128,128]{2,1,0:T(8,128)(2,1)}, bf16[16,128,256]{2,1,0:T(8,128)(2,1)}) custom-call(s32[1]{0:T(128)} %bitcast.l_ref, bf16[64,128,512]{2,1,0:T(8,128)(2,1)} %three_ref.5, bf16[64,64]{1,0:T(8,128)(2,1)} %metric_ref.5, s32[16,16,64]{2,1,0:T(8,128)} %bitcast.3), custom_call_target="tpu_custom_call" | custom-call | flops 2147483648 | bytes 8388608 | tf_op jit(solution)/shard_map/pallas_call | solution.py:293
  22.5 9.7 %shard_map.57 = (bf16[16,128,256]{2,1,0:T(8,128)(2,1)}, bf16[16,128,256]{2,1,0:T(8,128)(2,1)}) custom-call(s32[1]{0:T(128)} %bitcast.l_ref, bf16[64,128,512]{2,1,0:T(8,128)(2,1)} %three_ref.5, bf16[64,64]{1,0:T(8,128)(2,1)} %metric_ref.5, s32[16,16,64]{2,1,0:T(8,128)} %bitcast.4), custom_call_target="tpu_custom_call" | custom-call | flops 2147483648 | bytes 8388608 | tf_op jit(solution)/shard_map/pallas_call | solution.py:310
  32.2 0.6 collective-permute-start.2
  32.9 2.9 %collective-permute-start.4 = (bf16[128,512]{1,0:T(8,128)(2,1)S(1)}, bf16[128,512]{1,0:T(8,128)(2,1)S(1)}, u32[]{:S(2)}, u32[]{:S(2)}) collective-permute-start(bf16[128,512]{1,0:T(8,128)(2,1)S(1)} %copy-done), channel_id=1, source_target_pairs={{0,2},{1,3},{2,0},{3,1},{4,6},{5,7},{6,4},{7,5},{8,10},{9,11},{10,... | collective-permute-start | bytes 393224 | tf_op jit(solution)/shard_map/ppermute | solution.py:257
  35.8 2.5 %collective-permute-start.10 = (bf16[16,128,256]{2,1,0:T(8,128)(2,1)S(1)}, bf16[16,128,256]{2,1,0:T(8,128)(2,1)S(1)}, u32[]{:S(2)}, u32[]{:S(2)}) collective-permute-start(bf16[16,128,256]{2,1,0:T(8,128)(2,1)S(1)} %copy-done.2), channel_id=1, source_target_pairs={{0,2},{1,3},{2,0},{3,1},{4,6},{5,7},{6,4},{7,5},{8,10},{9,11},{10,... | collective-permute-start | bytes 3145736 | tf_op jit(solution)/shard_map/ppermute | solution.py:257
  38.3 1.4 %collective-permute-done.4.d2_ref = bf16[128,512]{1,0:T(8,128)(2,1)S(1)} collective-permute-done((bf16[128,512]{1,0:T(8,128)(2,1)S(1)}, bf16[128,512]{1,0:T(8,128)(2,1)S(1)}, u32[]{:S(2)}, u32[]{:S(2)}) %collective-permute-start.4) | collective-permute-done | bytes 131104 | tf_op jit(solution)/shard_map/ppermute | solution.py:257
  39.7 1.3 %collective-permute-done.5.d3_ref = bf16[128,512]{1,0:T(8,128)(2,1)S(1)} collective-permute-done((bf16[128,512]{1,0:T(8,128)(2,1)S(1)}, bf16[128,512]{1,0:T(8,128)(2,1)S(1)}, u32[]{:S(2)}, u32[]{:S(2)}) %collective-permute-start.5) | collective-permute-done | bytes 131104 | tf_op jit(solution)/shard_map/ppermute | solution.py:257
  41.0 1.5 %collective-permute-start.11 = (bf16[16,128,128]{2,1,0:T(8,128)(2,1)S(1)}, bf16[16,128,128]{2,1,0:T(8,128)(2,1)S(1)}, u32[]{:S(2)}, u32[]{:S(2)}) collective-permute-start(bf16[16,128,128]{2,1,0:T(8,128)(2,1)S(1)} %copy-done.5), channel_id=1, source_target_pairs={{0,3},{1,2},{2,1},{3,0},{4,7},{5,6},{6,5},{7,4},{8,11},{9,10},{10,... | collective-permute-start | bytes 1572872 | tf_op jit(solution)/shard_map/ppermute | solution.py:257
  42.5 0.7 shard_map.58.refs_6_.refs_3_
  43.3 1.2 %copy-done.3 = bf16[16,128,256]{2,1,0:T(8,128)(2,1)S(1)} copy-done((bf16[16,128,256]{2,1,0:T(8,128)(2,1)S(1)}, bf16[16,128,256]{2,1,0:T(8,128)(2,1)}, u32[]{:S(2)}) %copy-start.3) | copy-done | bytes 1048600
  44.5 10.3 %shard_map.59 = (bf16[16,256,512]{2,1,0:T(8,128)(2,1)S(1)}, f32[128,256]{1,0:T(8,128)S(1)}, f32[128,256]{1,0:T(8,128)S(1)}) custom-call(s32[1]{0:T(128)} %bitcast.l_ref, bf16[16,128,512]{2,1,0:T(8,128)(2,1)S(1)} %copy-done.4, bf16[16,128,512]{2,1,0:T(8,128)(2,1)S(1)} %collective-permute-done.refs_1_, bf16[16,128,256]{2,1,0:T(8,128)(2,1)S(1)} %copy-done.2, ...), custom_call_target="tpu_custom_call" | custom-call | flops 6442450944 | bytes 8388608 | tf_op jit(solution)/shard_map/pallas_call | solution.py:340
  54.8 5.2 %shard_map.60 = (bf16[16,512,256]{2,1,0:T(8,128)(2,1)S(1)}, f32[512,256]{1,0:T(8,128)S(1)}) custom-call(s32[1]{0:T(128)} %bitcast.l_ref, bf16[16,128,512]{2,1,0:T(8,128)(2,1)S(1)} %copy-done.4, bf16[16,128,512]{2,1,0:T(8,128)(2,1)S(1)} %collective-permute-done.refs_1_, bf16[16,256,512]{2,1,0:T(8,128)(2,1)S(1)} %get-tuple-element.27.refs_2_, ...), custom_call_target="tpu_custom_call" | custom-call | flops 3221225472 | bytes 16777216 | tf_op jit(solution)/shard_map/pallas_call | solution.py:352
  60.1 12.8 %collective-permute-done.11.refs_2_ = bf16[16,128,128]{2,1,0:T(8,128)(2,1)S(1)} collective-permute-done((bf16[16,128,128]{2,1,0:T(8,128)(2,1)S(1)}, bf16[16,128,128]{2,1,0:T(8,128)(2,1)S(1)}, u32[]{:S(2)}, u32[]{:S(2)}) %collective-permute-start.11) | collective-permute-done | bytes 524320 | tf_op jit(solution)/shard_map/ppermute | solution.py:257
  72.8 2.1 %shard_map.61 = (f32[256,256]{1,0:T(8,128)S(1)}, f32[256,256]{1,0:T(8,128)S(1)}) custom-call(s32[1]{0:T(128)} %bitcast.l_ref, bf16[16,512,256]{2,1,0:T(8,128)(2,1)S(1)} %get-tuple-element.28.refs_0_, bf16[16,128,256]{2,1,0:T(8,128)(2,1)S(1)} %collective-permute-done.10.refs_1_, bf16[16,128,128]{2,1,0:T(8,128)(2,1)S(1)} %collective-permute-done.11.refs_2_, ...), custom_call_target="tpu_custom_call" | custom-call | flops 1073741824 | bytes 8388608 | tf_op jit(solution)/shard_map/pallas_call | solution.py:365
  75.0 0.2 collective-permute-start.12
  75.2 0.3 collective-permute-start.6
  75.5 1.0 %collective-permute-done.12 = f32[256,256]{1,0:T(8,128)S(1)} collective-permute-done((f32[256,256]{1,0:T(8,128)S(1)}, f32[256,256]{1,0:T(8,128)S(1)}, u32[]{:S(2)}, u32[]{:S(2)}) %collective-permute-start.12) | collective-permute-done | bytes 262176 | tf_op jit(solution)/shard_map/ppermute | solution.py:257
  76.6 1.6 %collective-permute-start.13 = (bf16[128,256]{1,0:T(8,128)(2,1)S(1)}, bf16[128,256]{1,0:T(8,128)(2,1)S(1)}, u32[]{:S(2)}, u32[]{:S(2)}) collective-permute-start(bf16[128,256]{1,0:T(8,128)(2,1)S(1)} %slice.21), channel_id=1, source_target_pairs={{0,2},{1,3},{2,0},{3,1},{4,6},{5,7},{6,4},{7,5},{8,10},{9,11},{10,... | collective-permute-start | bytes 196616 | tf_op jit(solution)/shard_map/ppermute | solution.py:257
  78.3 1.6 %collective-permute-start.7 = (bf16[128,256]{1,0:T(8,128)(2,1)S(1)}, bf16[128,256]{1,0:T(8,128)(2,1)S(1)}, u32[]{:S(2)}, u32[]{:S(2)}) collective-permute-start(bf16[128,256]{1,0:T(8,128)(2,1)S(1)} %fusion.4), channel_id=1, source_target_pairs={{0,4},{4,0},{8,12},{12,8},{16,20},{20,16},{24,28},{28,24},{1,5},{5... | collective-permute-start | bytes 196616 | tf_op jit(solution)/shard_map/ppermute | solution.py:257
  79.8 1.1 %collective-permute-done.13 = bf16[128,256]{1,0:T(8,128)(2,1)S(1)} collective-permute-done((bf16[128,256]{1,0:T(8,128)(2,1)S(1)}, bf16[128,256]{1,0:T(8,128)(2,1)S(1)}, u32[]{:S(2)}, u32[]{:S(2)}) %collective-permute-start.13) | collective-permute-done | bytes 65568 | tf_op jit(solution)/shard_map/ppermute | solution.py:257
  81.0 1.7 %collective-permute-start.14 = (bf16[128,256]{1,0:T(8,128)(2,1)S(1)}, bf16[128,256]{1,0:T(8,128)(2,1)S(1)}, u32[]{:S(2)}, u32[]{:S(2)}) collective-permute-start(bf16[128,256]{1,0:T(8,128)(2,1)S(1)} %fusion.3), channel_id=1, source_target_pairs={{0,4},{4,0},{8,12},{12,8},{16,20},{20,16},{24,28},{28,24},{1,5},{5... | collective-permute-start | bytes 196616 | tf_op jit(solution)/shard_map/ppermute | solution.py:257
  82.7 1.6 %collective-permute-start.8 = (bf16[128,256]{1,0:T(8,128)(2,1)S(1)}, bf16[128,256]{1,0:T(8,128)(2,1)S(1)}, u32[]{:S(2)}, u32[]{:S(2)}) collective-permute-start(bf16[128,256]{1,0:T(8,128)(2,1)S(1)} %fusion.1), channel_id=1, source_target_pairs={{0,8},{4,12},{8,0},{12,4},{16,24},{20,28},{24,16},{28,20},{1,9},{5... | collective-permute-start | bytes 196616 | tf_op jit(solution)/shard_map/ppermute | solution.py:257
  84.4 0.9 collective-permute-done.14
  85.3 1.8 %collective-permute-start.15 = (bf16[128,256]{1,0:T(8,128)(2,1)S(1)}, bf16[128,256]{1,0:T(8,128)(2,1)S(1)}, u32[]{:S(2)}, u32[]{:S(2)}) collective-permute-start(bf16[128,256]{1,0:T(8,128)(2,1)S(1)} %fusion.2), channel_id=1, source_target_pairs={{0,8},{4,12},{8,0},{12,4},{16,24},{20,28},{24,16},{28,20},{1,9},{5... | collective-permute-start | bytes 196616 | tf_op jit(solution)/shard_map/ppermute | solution.py:257
  87.1 0.6 collective-permute-done.8
  87.8 3.5 %collective-permute-start.9 = (bf16[128,256]{1,0:T(8,128)(2,1)S(1)}, bf16[128,256]{1,0:T(8,128)(2,1)S(1)}, u32[]{:S(2)}, u32[]{:S(2)}) collective-permute-start(bf16[128,256]{1,0:T(8,128)(2,1)S(1)} %get-tuple-element.35), channel_id=1, source_target_pairs={{0,24},{4,28},{8,16},{12,20},{16,8},{20,12},{24,0},{28,4},{1,25},{... | collective-permute-start | bytes 196616 | tf_op jit(solution)/shard_map/ppermute | solution.py:257
  91.3 2.2 %collective-permute-start.16 = (bf16[128,256]{1,0:T(8,128)(2,1)S(1)}, bf16[128,256]{1,0:T(8,128)(2,1)S(1)}, u32[]{:S(2)}, u32[]{:S(2)}) collective-permute-start(bf16[128,256]{1,0:T(8,128)(2,1)S(1)} %get-tuple-element.33), channel_id=1, source_target_pairs={{0,24},{4,28},{8,16},{12,20},{16,8},{20,12},{24,0},{28,4},{1,25},{... | collective-permute-start | bytes 196616 | tf_op jit(solution)/shard_map/ppermute | solution.py:257
  93.5 0.9 collective-permute-done.9.own_got_ref
  94.4 3.1 %collective-permute-done.16.far_got_ref = bf16[128,256]{1,0:T(8,128)(2,1)S(1)} collective-permute-done((bf16[128,256]{1,0:T(8,128)(2,1)S(1)}, bf16[128,256]{1,0:T(8,128)(2,1)S(1)}, u32[]{:S(2)}, u32[]{:S(2)}) %collective-permute-start.16) | collective-permute-done | bytes 65568 | tf_op jit(solution)/shard_map/ppermute | solution.py:257
  97.5 0.7 shard_map.62
  (30 shorter events, 0.4 us)
Async XLA Ops:
  12.2 31.1 %collective-permute-start = (bf16[16,128,512]{2,1,0:T(8,128)(2,1)}, bf16[16,128,512]{2,1,0:T(8,128)(2,1)S(1)}, u32[]{:S(2)}, u32[]{:S(2)}) collective-permute-start(bf16[16,128,512]{2,1,0:T(8,128)(2,1)} %get-tuple-element.20), channel_id=1, source_target_pairs={{0,1},{1,0},{2,3},{3,2},{4,5},{5,4},{6,7},{7,6},{8,9},{9,8},{10,11... | collective-permute-start | bytes 6291464 | tf_op jit(solution)/shard_map/ppermute | solution.py:257
  22.3 10.5 %copy-start = (bf16[128,512]{1,0:T(8,128)(2,1)S(1)}, bf16[128,512]{1,0:T(8,128)(2,1)}, u32[]{:S(2)}) copy-start(bf16[128,512]{1,0:T(8,128)(2,1)} %d0_ref.1) | copy-start | bytes 393220
  22.3 13.4 %copy-start.2 = (bf16[16,128,256]{2,1,0:T(8,128)(2,1)S(1)}, bf16[16,128,256]{2,1,0:T(8,128)(2,1)}, u32[]{:S(2)}) copy-start(bf16[16,128,256]{2,1,0:T(8,128)(2,1)} %get-tuple-element.21.refs_2_) | copy-start | bytes 3145732
  22.3 18.7 %copy-start.5 = (bf16[16,128,128]{2,1,0:T(8,128)(2,1)S(1)}, bf16[16,128,128]{2,1,0:T(8,128)(2,1)}, u32[]{:S(2)}) copy-start(bf16[16,128,128]{2,1,0:T(8,128)(2,1)} %get-tuple-element.29) | copy-start | bytes 1572868
  22.3 20.2 %copy-start.1 = (s32[16,16]{1,0:T(8,128)S(1)}, s32[16,16]{1,0:T(8,128)}, u32[]{:S(2)}) copy-start(s32[16,16]{1,0:T(8,128)} %dp_ref.1) | copy-start | bytes 3076
  22.4 20.9 %copy-start.4 = (bf16[16,128,512]{2,1,0:T(8,128)(2,1)S(1)}, bf16[16,128,512]{2,1,0:T(8,128)(2,1)}, u32[]{:S(2)}) copy-start(bf16[16,128,512]{2,1,0:T(8,128)(2,1)} %get-tuple-element.19.refs_0_) | copy-start | bytes 6291460
  22.4 20.9 %collective-permute-start.1 = (bf16[16,128,256]{2,1,0:T(8,128)(2,1)}, bf16[16,128,256]{2,1,0:T(8,128)(2,1)S(1)}, u32[]{:S(2)}, u32[]{:S(2)}) collective-permute-start(bf16[16,128,256]{2,1,0:T(8,128)(2,1)} %get-tuple-element.23), channel_id=1, source_target_pairs={{0,1},{1,0},{2,3},{3,2},{4,5},{5,4},{6,7},{7,6},{8,9},{9,8},{10,11... | collective-permute-start | bytes 3145736 | tf_op jit(solution)/shard_map/ppermute | solution.py:257
  32.2 11.1 %collective-permute-start.2 = (bf16[16,128,256]{2,1,0:T(8,128)(2,1)}, bf16[16,128,256]{2,1,0:T(8,128)(2,1)S(1)}, u32[]{:S(2)}, u32[]{:S(2)}) collective-permute-start(bf16[16,128,256]{2,1,0:T(8,128)(2,1)} %get-tuple-element.24), channel_id=1, source_target_pairs={{0,1},{1,0},{2,3},{3,2},{4,5},{5,4},{6,7},{7,6},{8,9},{9,8},{10,11... | collective-permute-start | bytes 3145736 | tf_op jit(solution)/shard_map/ppermute | solution.py:257
  32.8 3.0 %collective-permute-start.3 = (bf16[128,512]{1,0:T(8,128)(2,1)S(1)}, bf16[128,512]{1,0:T(8,128)(2,1)S(1)}, u32[]{:S(2)}, u32[]{:S(2)}) collective-permute-start(bf16[128,512]{1,0:T(8,128)(2,1)S(1)} %copy-done), channel_id=1, source_target_pairs={{0,1},{1,0},{2,3},{3,2},{4,5},{5,4},{6,7},{7,6},{8,9},{9,8},{10,11... | collective-permute-start | bytes 393224 | tf_op jit(solution)/shard_map/ppermute | solution.py:257
  32.9 6.8 %collective-permute-start.4 = (bf16[128,512]{1,0:T(8,128)(2,1)S(1)}, bf16[128,512]{1,0:T(8,128)(2,1)S(1)}, u32[]{:S(2)}, u32[]{:S(2)}) collective-permute-start(bf16[128,512]{1,0:T(8,128)(2,1)S(1)} %copy-done), channel_id=1, source_target_pairs={{0,2},{1,3},{2,0},{3,1},{4,6},{5,7},{6,4},{7,5},{8,10},{9,11},{10,... | collective-permute-start | bytes 393224 | tf_op jit(solution)/shard_map/ppermute | solution.py:257
  35.8 37.1 %collective-permute-start.10 = (bf16[16,128,256]{2,1,0:T(8,128)(2,1)S(1)}, bf16[16,128,256]{2,1,0:T(8,128)(2,1)S(1)}, u32[]{:S(2)}, u32[]{:S(2)}) collective-permute-start(bf16[16,128,256]{2,1,0:T(8,128)(2,1)S(1)} %copy-done.2), channel_id=1, source_target_pairs={{0,2},{1,3},{2,0},{3,1},{4,6},{5,7},{6,4},{7,5},{8,10},{9,11},{10,... | collective-permute-start | bytes 3145736 | tf_op jit(solution)/shard_map/ppermute | solution.py:257
  39.7 1.3 %collective-permute-start.5 = (bf16[128,512]{1,0:T(8,128)(2,1)S(1)}, bf16[128,512]{1,0:T(8,128)(2,1)S(1)}, u32[]{:S(2)}, u32[]{:S(2)}) collective-permute-start(bf16[128,512]{1,0:T(8,128)(2,1)S(1)} %collective-permute-done.4.d2_ref), channel_id=1, source_target_pairs={{0,1},{1,0},{2,3},{3,2},{4,5},{5,4},{6,7},{7,6},{8,9},{9,8},{10,11... | collective-permute-start | bytes 393224 | tf_op jit(solution)/shard_map/ppermute | solution.py:257
  41.0 31.8 %collective-permute-start.11 = (bf16[16,128,128]{2,1,0:T(8,128)(2,1)S(1)}, bf16[16,128,128]{2,1,0:T(8,128)(2,1)S(1)}, u32[]{:S(2)}, u32[]{:S(2)}) collective-permute-start(bf16[16,128,128]{2,1,0:T(8,128)(2,1)S(1)} %copy-done.5), channel_id=1, source_target_pairs={{0,3},{1,2},{2,1},{3,0},{4,7},{5,6},{6,5},{7,4},{8,11},{9,10},{10,... | collective-permute-start | bytes 1572872 | tf_op jit(solution)/shard_map/ppermute | solution.py:257
  43.3 1.2 %copy-start.3 = (bf16[16,128,256]{2,1,0:T(8,128)(2,1)S(1)}, bf16[16,128,256]{2,1,0:T(8,128)(2,1)}, u32[]{:S(2)}) copy-start(bf16[16,128,256]{2,1,0:T(8,128)(2,1)} %get-tuple-element.22.refs_3_) | copy-start | bytes 3145732
  75.0 1.6 %collective-permute-start.12 = (f32[256,256]{1,0:T(8,128)S(1)}, f32[256,256]{1,0:T(8,128)S(1)}, u32[]{:S(2)}, u32[]{:S(2)}) collective-permute-start(f32[256,256]{1,0:T(8,128)S(1)} %get-tuple-element.32), channel_id=1, source_target_pairs={{0,1},{1,0},{2,3},{3,2},{4,5},{5,4},{6,7},{7,6},{8,9},{9,8},{10,11... | collective-permute-start | bytes 786440 | tf_op jit(solution)/shard_map/ppermute | solution.py:257
  75.2 3.0 %collective-permute-start.6 = (f32[128,256]{1,0:T(8,128)S(1)}, f32[128,256]{1,0:T(8,128)S(1)}, u32[]{:S(2)}, u32[]{:S(2)}) collective-permute-start(f32[128,256]{1,0:T(8,128)S(1)} %get-tuple-element.26), channel_id=1, source_target_pairs={{0,1},{1,0},{2,3},{3,2},{4,5},{5,4},{6,7},{7,6},{8,9},{9,8},{10,11... | collective-permute-start | bytes 393224 | tf_op jit(solution)/shard_map/ppermute | solution.py:257
  76.6 4.3 %collective-permute-start.13 = (bf16[128,256]{1,0:T(8,128)(2,1)S(1)}, bf16[128,256]{1,0:T(8,128)(2,1)S(1)}, u32[]{:S(2)}, u32[]{:S(2)}) collective-permute-start(bf16[128,256]{1,0:T(8,128)(2,1)S(1)} %slice.21), channel_id=1, source_target_pairs={{0,2},{1,3},{2,0},{3,1},{4,6},{5,7},{6,4},{7,5},{8,10},{9,11},{10,... | collective-permute-start | bytes 196616 | tf_op jit(solution)/shard_map/ppermute | solution.py:257
  78.3 4.4 %collective-permute-start.7 = (bf16[128,256]{1,0:T(8,128)(2,1)S(1)}, bf16[128,256]{1,0:T(8,128)(2,1)S(1)}, u32[]{:S(2)}, u32[]{:S(2)}) collective-permute-start(bf16[128,256]{1,0:T(8,128)(2,1)S(1)} %fusion.4), channel_id=1, source_target_pairs={{0,4},{4,0},{8,12},{12,8},{16,20},{20,16},{24,28},{28,24},{1,5},{5... | collective-permute-start | bytes 196616 | tf_op jit(solution)/shard_map/ppermute | solution.py:257
  81.0 4.3 %collective-permute-start.14 = (bf16[128,256]{1,0:T(8,128)(2,1)S(1)}, bf16[128,256]{1,0:T(8,128)(2,1)S(1)}, u32[]{:S(2)}, u32[]{:S(2)}) collective-permute-start(bf16[128,256]{1,0:T(8,128)(2,1)S(1)} %fusion.3), channel_id=1, source_target_pairs={{0,4},{4,0},{8,12},{12,8},{16,20},{20,16},{24,28},{28,24},{1,5},{5... | collective-permute-start | bytes 196616 | tf_op jit(solution)/shard_map/ppermute | solution.py:257
  82.7 5.0 %collective-permute-start.8 = (bf16[128,256]{1,0:T(8,128)(2,1)S(1)}, bf16[128,256]{1,0:T(8,128)(2,1)S(1)}, u32[]{:S(2)}, u32[]{:S(2)}) collective-permute-start(bf16[128,256]{1,0:T(8,128)(2,1)S(1)} %fusion.1), channel_id=1, source_target_pairs={{0,8},{4,12},{8,0},{12,4},{16,24},{20,28},{24,16},{28,20},{1,9},{5... | collective-permute-start | bytes 196616 | tf_op jit(solution)/shard_map/ppermute | solution.py:257
  85.3 6.0 %collective-permute-start.15 = (bf16[128,256]{1,0:T(8,128)(2,1)S(1)}, bf16[128,256]{1,0:T(8,128)(2,1)S(1)}, u32[]{:S(2)}, u32[]{:S(2)}) collective-permute-start(bf16[128,256]{1,0:T(8,128)(2,1)S(1)} %fusion.2), channel_id=1, source_target_pairs={{0,8},{4,12},{8,0},{12,4},{16,24},{20,28},{24,16},{28,20},{1,9},{5... | collective-permute-start | bytes 196616 | tf_op jit(solution)/shard_map/ppermute | solution.py:257
  87.8 6.6 %collective-permute-start.9 = (bf16[128,256]{1,0:T(8,128)(2,1)S(1)}, bf16[128,256]{1,0:T(8,128)(2,1)S(1)}, u32[]{:S(2)}, u32[]{:S(2)}) collective-permute-start(bf16[128,256]{1,0:T(8,128)(2,1)S(1)} %get-tuple-element.35), channel_id=1, source_target_pairs={{0,24},{4,28},{8,16},{12,20},{16,8},{20,12},{24,0},{28,4},{1,25},{... | collective-permute-start | bytes 196616 | tf_op jit(solution)/shard_map/ppermute | solution.py:257
  91.3 6.1 %collective-permute-start.16 = (bf16[128,256]{1,0:T(8,128)(2,1)S(1)}, bf16[128,256]{1,0:T(8,128)(2,1)S(1)}, u32[]{:S(2)}, u32[]{:S(2)}) collective-permute-start(bf16[128,256]{1,0:T(8,128)(2,1)S(1)} %get-tuple-element.33), channel_id=1, source_target_pairs={{0,24},{4,28},{8,16},{12,20},{16,8},{20,12},{24,0},{28,4},{1,25},{... | collective-permute-start | bytes 196616 | tf_op jit(solution)/shard_map/ppermute | solution.py:257

commit v3 on v2

--- a/solution.py
+++ b/solution.py
@@ -1,4 +1,3 @@
-import functools
 import jax
 import jax.numpy as jnp
 from jax import lax
@@ -79,20 +78,22 @@
         spread_ref[n * rows : (n + 1) * rows, :] = jnp.where(same, full, 0.0).astype(BF)
 
 
-def masked_columns(l, order, base, three_ref, pattern_ref):
-    group, sub, _ = three_ref.shape
+def masked_columns(l, order, base, three_ref, pattern_ref, first):
+    group = three_ref.shape[0]
     tiles = pattern_ref.shape[1]
     block = tiles * TILE // 4
-    pattern = (pattern_ref[0] > 0).astype(BF)
-    out = []
+    pattern = (pattern_ref[first // TILE] > 0).astype(BF)
+    out = [[] for _ in range(TILE // SUB)]
     for j in order:
         start = (l ^ j) * block
         here = (iota((tiles, block), 0) == (start // TILE) + iota((tiles, block), 1) // TILE).astype(BF)
         mask = lax.dot_general(pattern, here, (((0,), (0,)), ((), ())), preferred_element_type=F32)
-        mask = jnp.broadcast_to(mask[:, None, :], (group, sub, block)).astype(BF)
-        piece = three_ref[:, :, pl.ds(pl.multiple_of(start - base, block), block)]
-        out.append((piece * mask).reshape(group * sub, block))
-    return jnp.concatenate(out, axis=1)
+        mask = jnp.broadcast_to(mask[:, None, :], (group, SUB, block)).astype(BF)
+        for n, pieces in enumerate(out):
+            at = first + n * SUB
+            piece = three_ref[:, at : at + SUB, pl.ds(pl.multiple_of(start - base, block), block)]
+            pieces.append((piece * mask).reshape(group * SUB, block))
+    return [jnp.concatenate(pieces, axis=1) for pieces in out]
 
 
 def near_kernel(l_ref, three_ref, metric_ref, pattern_ref, straight_ref, cross_ref, core_ref, spread_ref):
@@ -102,15 +103,17 @@
     def _():
         spread_metric(l, metric_ref, spread_ref, (2, 3))
 
-    part, sub, width = straight_ref.shape
+    part, rows, width = straight_ref.shape
     block = width // 2
-    data = masked_columns(l, (0, 1), (l // 2) * width, three_ref, pattern_ref)
-    got = dot(spread_ref[...], data).astype(BF)
-    straight_ref[...] = got[: part * sub].reshape(part, sub, width)
-    low = got[part * sub :].reshape(part, sub, width)
-    cross_ref[...] = low[:, :, :block]
-    core_ref[:, :, :block] = low[:, :, block:]
-    core_ref[:, :, block:] = low[:, :, :block]
+    for first in range(0, rows, TILE):
+        strips = masked_columns(l, (0, 1), (l // 2) * width, three_ref, pattern_ref, first)
+        for n, data in enumerate(strips):
+            at = slice(first + n * SUB, first + (n + 1) * SUB)
+            got = dot(spread_ref[...], data).astype(BF)
+            straight_ref[:, at] = got[: part * SUB].reshape(part, SUB, width)
+            low = got[part * SUB :].reshape(part, SUB, width)
+            cross_ref[:, at] = low[:, :, :block]
+            core_ref[:, at] = swapped(low, block)
 
 
 def swapped(x, block):
@@ -121,20 +124,28 @@
     return jnp.concatenate(parts, axis=-1)
 
 
-def rest_kernel(l_ref, three_ref, metric_ref, pattern_ref, keep_ref, send_ref, spread_ref, *, cut, orders):
+def rest_kernel(
+    l_ref, three_ref, metric_ref, pattern_ref, keep_ref, send_ref, keep_far_ref, send_far_ref, spread_ref
+):
     l = l_ref[0]
 
     @pl.when(pl.program_id(0) == 0)
     def _():
-        spread_metric(l, metric_ref, spread_ref, orders)
-
-    part, sub, width = keep_ref.shape
-    block = width // len(cut)
-    base = (l ^ cut[0]) // 2 * width if len(cut) == 2 else 0
-    data = masked_columns(l, cut, base, three_ref, pattern_ref)
-    got = dot(spread_ref[...], data).astype(BF)
-    keep_ref[...] = got[: part * sub].reshape(part, sub, width)
-    send_ref[...] = swapped(got[part * sub :].reshape(part, sub, width), block)
+        spread_metric(l, metric_ref, spread_ref, (0, 1, 2, 3))
+
+    part, rows, width = keep_ref.shape
+    half, block = width // 2, width // 4
+    one = part * SUB
+    for first in range(0, rows, TILE):
+        strips = masked_columns(l, (0, 1, 2, 3), 0, three_ref, pattern_ref, first)
+        for n, data in enumerate(strips):
+            at = slice(first + n * SUB, first + (n + 1) * SUB)
+            got = dot(spread_ref[: 2 * one], data).astype(BF)
+            keep_ref[:, at] = got[:one].reshape(part, SUB, width)
+            send_ref[:, at] = swapped(got[one:].reshape(part, SUB, width), block)
+            got = dot(spread_ref[2 * one :], data[:, half:]).astype(BF)
+            keep_far_ref[:, at] = got[:one].reshape(part, SUB, half)
+            send_far_ref[:, at] = swapped(got[one:].reshape(part, SUB, half), block)
 
 
 def settle_kernel(l_ref, d0_ref, d1_ref, d2_ref, d3_ref, dp_ref, dens_ref, mask_ref):
@@ -226,12 +237,12 @@
         send_ref[block:] = swapped(ba[block:], block)
 
 
-def place_kernel(l_ref, own_ref, own_got_ref, far_ref, far_got_ref, out_ref):
+def place_kernel(l_ref, mine_ref, got_ref, out_ref):
     l = l_ref[0]
-    block = out_ref.shape[0]
-    for j, (a_ref, b_ref) in enumerate(((own_ref, own_got_ref),) * 2 + ((far_ref, far_got_ref),) * 2):
-        at = j % 2 * block
-        total = a_ref[:, at : at + block] + b_ref[:, at : at + block].astype(F32)
+    block, _ = out_ref.shape
+    for j in range(4):
+        at = slice(j * block, (j + 1) * block)
+        total = mine_ref[:, at] + got_ref[:, at].astype(F32)
         out_ref[:, pl.ds(pl.multiple_of((l ^ j) * block, block), block)] = total
 
 
@@ -273,7 +284,6 @@
     group, block, width = three.shape
     part, half = group // 4, width // 2
     tiles = tile_pattern.shape[2]
-    strips = block // SUB
     index = lax.axis_index("lay")
     l = jnp.reshape(index, (1,)).astype(jnp.int32)
     S = jax.ShapeDtypeStruct
@@ -284,44 +294,41 @@
     d3 = swap(d2, "lay", 1)
 
     pattern = jnp.transpose(tile_pattern, (1, 2, 0))
-    per, here = TILE // SUB, block // TILE
-    common = [
-        pl.BlockSpec((group, group), lambda t, s: (0, 0)),
-        pl.BlockSpec((1, tiles, group), lambda t, s: (s[0] * here + t // per, 0, 0)),
-    ]
-    strip = lambda n: pl.BlockSpec((part, SUB, n), lambda t, s: (0, t, 0))
+    metric_spec = pl.BlockSpec((group, group), lambda t, s: (0, 0))
+
+    def pattern_spec(rows):
+        return pl.BlockSpec((rows // TILE, tiles, group), lambda t, s: (s[0] * (block // rows) + t, 0, 0))
+
+    rows = 2 * TILE
+    strip = lambda n: pl.BlockSpec((part, 2 * TILE, n), lambda t, s: (0, t, 0))
     straight, cross, send3 = call(
         near_kernel,
-        (strips,),
-        [pl.BlockSpec((group, SUB, half), lambda t, s: (0, t, s[0] // 2))] + common,
+        (block // rows,),
+        [pl.BlockSpec((group, rows, half), lambda t, s: (0, t, s[0] // 2)), metric_spec, pattern_spec(rows)],
         [strip(half), strip(block), strip(half)],
         [S((part, block, half), BF), S((part, block, block), BF), S((part, block, half), BF)],
         [pltpu.VMEM((2 * part * SUB, group * SUB), BF)],
-        2 * 2 * part * SUB * group * SUB * half * strips,
+        4 * part * SUB * group * half * block,
         group * block * half * 4,
-        vmem=NEAR_VMEM,
+        vmem=57,
     )(l, three, metric, pattern)
     far_straight = swap(straight, "lay", 2)
     far_cross = swap(cross, "lay", 3)
     got3 = swap(send3, "lay", 1)
 
-    def rest(cut, orders, columns):
-        n = len(cut) * block
-        return call(
-            functools.partial(rest_kernel, cut=cut, orders=orders),
-            (strips,),
-            [pl.BlockSpec((group, SUB, n), columns)] + common,
-            [strip(n)] * 2,
-            [S((part, block, n), BF)] * 2,
-            [pltpu.VMEM((2 * part * SUB, group * SUB), BF)],
-            2 * 2 * part * SUB * group * SUB * n * strips,
-            group * block * n * 4,
-            vmem=NEAR_VMEM,
-        )(l, three, metric, pattern)
-
-    keep0, send1 = rest((0, 1, 2, 3), (0, 1), lambda t, s: (0, t, 0))
+    tile = lambda n: pl.BlockSpec((part, TILE, n), lambda t, s: (0, t, 0))
+    keep0, send1, keep2, send4 = call(
+        rest_kernel,
+        (block // TILE,),
+        [pl.BlockSpec((group, TILE, width), lambda t, s: (0, t, 0)), metric_spec, pattern_spec(TILE)],
+        [tile(width)] * 2 + [tile(half)] * 2,
+        [S((part, block, width), BF)] * 2 + [S((part, block, half), BF)] * 2,
+        [pltpu.VMEM((group * SUB, group * SUB), BF)],
+        6 * part * SUB * group * width * block,
+        group * block * width * 4,
+        vmem=57,
+    )(l, three, metric, pattern)
     got1 = swap(send1, "lay", 1)
-    keep2, send4 = rest((2, 3), (2, 3), lambda t, s: (0, t, 1 - s[0] // 2))
     got4 = swap(send4, "lay", 1)
 
     dens = call(
@@ -346,9 +353,11 @@
         [pltpu.VMEM((half, half), F32)],
         2 * part * 2 * half * width * (width + half),
         2 * part * half * width * 2,
+        vmem=57,
     )(l, keep0, got1, straight, keep2, got3, got4, dens)
     own = own_keep + swap(own_send, "lay", 1)
 
+    count = 4
     left, far = call(
         no_index(local_kernel),
         (part // count,),
@@ -359,6 +368,7 @@
         [],
         part * 2 * half * (width * width + 2 * half * half),
         part * half * width * 8,
+        vmem=57,
     )(l, keep0, got1, inter, dens)
 
     count = 4
@@ -371,35 +381,30 @@
         [pltpu.VMEM((width, half), F32)],
         2 * part * width * half * half,
         part * width * half * 4,
+        vmem=57,
     )(l, left, far_straight, far_cross, far)
     far = kept + swap(sent, "lay", 1)
     far = far[:block] + swap(far[block:].astype(BF), "lay", 2).astype(F32)
 
-    def over_groups(x):
-        steps = bits_of(lax.axis_size("blk"))
-        for n, bit in enumerate(steps):
-            x = rounded(x)
-            got = swap(x.astype(BF), "blk", bit if n < 2 else bit | steps[n - 1])
-            if n == len(steps) - 1:
-                return x, got
-            x = x + got.astype(F32)
-        return x, jnp.zeros(x.shape, BF)
-
-    own, own_got = over_groups(own)
-    far, far_got = over_groups(far)
+    steps = bits_of(lax.axis_size("blk"))
+    for bit in steps[:-1]:
+        own = own + swap(own, "blk", bit)
+        far = rounded(far)
+        far = far + swap(far.astype(BF), "blk", bit).astype(F32)
+    total = rounded(jnp.concatenate([own, far], axis=1))
+    got = jnp.zeros(total.shape, BF)
+    if steps:
+        got = swap(total.astype(BF), "blk", steps[-1] | (steps[-1] >> 1 & ~1))
     return call(
         place_kernel,
         (1,),
-        [whole((block, half))] * 4,
+        [whole((block, width))] * 2,
         whole((block, width)),
         S((block, width), F32),
         [],
         block * width,
         block * width * 10,
-    )(l, own, own_got, far, far_got)
-
-
-NEAR_VMEM = 57
+    )(l, total, got)
 
 
 def solution(mesh):

time: 98.9 us -> 93.9 us (0.949)
  starting transfers between devices: 22.9 us -> 17.1 us
  Pallas kernels: 50.6 us -> 47.4 us
  local copies, waits for them, and re-layouts: 1.25 us -> 4.18 us
    pallas_call x4 -> x3, Pallas kernels: 32.3 us -> 19.8 us  [the longest x1 12.4 us: exchange_four(): call(rest_kernel, (block // TILE,), [pl.BlockSpec((group, TILE, width), l...]
    ppermute x17 -> x16, starting transfers between devices: 22.9 us -> 17.1 us  [swap(): lax.ppermute(x, axis, [(i, i ^ bit) for i in range(lax.axis_size(axis))])]
    pallas_call x1, Pallas kernels: 2.12 us -> 5.42 us  [exchange_four(): call(no_index(far_kernel), (part // count,), [many(width, half), many(blo...]
    pallas_call x1, Pallas kernels: 5.22 us -> 8.32 us  [exchange_four(): call(no_index(local_kernel), (part // count,), [many(block, width)] * 2 +...]
    unnamed x12 -> x20, local copies, waits for them, and re-layouts: 1.24 us -> 4.17 us
    pallas_call x1, Pallas kernels: 10.3 us -> 13.2 us  [exchange_four(): call(no_index(own_kernel), (part // count,), [many(block, width)] * 2 + [...]
    ppermute x17 -> x16, waiting for transfers between devices: 23.1 us -> 23.4 us  [swap(): lax.ppermute(x, axis, [(i, i ^ bit) for i in range(lax.axis_size(axis))])]
  transfers between devices with their start and end apart: 17 -> 16, of which waited for: 9 -> 9; matrix products, arithmetic and copies ran while one was open for 0% -> 1% of each run, Pallas kernels for 36% -> 31%
where the time goes in v3:
time: 93.9 us; the launch traced here: 93.4 us
  Pallas kernels  47.4 us (50%)
  waiting for transfers between devices  23.4 us (25%)
  starting transfers between devices  17.1 us (18%)
  local copies, waits for them, and re-layouts  4.18 us (4%)
  other arithmetic  1.15 us (1%)
    ppermute x16, waiting for transfers between devices, swap(): lax.ppermute(x, axis, [(i, i ^ bit) for i in range(lax.axis_size(axis))])  23.4 us
    ppermute x16, starting transfers between devices, swap(): lax.ppermute(x, axis, [(i, i ^ bit) for i in range(lax.axis_size(axis))])  17.1 us
    pallas_call x1, Pallas kernels, exchange_four(): call(no_index(own_kernel), (part // count,), [many(block, width)] * 2 + [...  13.2 us
    pallas_call x1, Pallas kernels, exchange_four(): call(rest_kernel, (block // TILE,), [pl.BlockSpec((group, TILE, width), l...  12.4 us
    pallas_call x1, Pallas kernels, exchange_four(): call(no_index(local_kernel), (part // count,), [many(block, width)] * 2 +...  8.32 us
    pallas_call x1, Pallas kernels, exchange_four(): call(near_kernel, (block // rows,), [pl.BlockSpec((group, rows, half), la...  6.7 us
    pallas_call x1, Pallas kernels, exchange_four(): call(no_index(far_kernel), (part // count,), [many(width, half), many(blo...  5.42 us
    unnamed x20, local copies, waits for them, and re-layouts  4.17 us
  transfers between devices with their start and end apart: 16, of which 9 were waited for; matrix products, arithmetic and copies ran while one was open for 1% of the time, Pallas kernels for 31%

profile of v3, /device:TPU:0, one launch (start us, length us, event | category | flops | bytes accessed | tf_op | source)
XLA Modules:
  0.0 93.4 jit_solution(13138798948039433757)
XLA Ops:
  0.0 12.4 %shard_map.55 = (bf16[16,128,512]{2,1,0:T(8,128)(2,1)}, bf16[16,128,512]{2,1,0:T(8,128)(2,1)}, bf16[16,128,256]{2,1,0:T(8,128)(2,1)}, bf16[16,128,256]{2,1,0:T(8,128)(2,1)}) custom-call(s32[1]{0:T(128)} %bitcast.l_ref, bf16[64,128,512]{2,1,0:T(8,128)(2,1)} %three_ref.3, bf16[64,64]{1,0:T(8,128)(2,1)} %metric_ref.3, s32[16,16,64]{2,1,0:T(8,128)} %bitcast.2), custom_call_target="tpu_custom_call" | custom-call | flops 6442450944 | bytes 16777216 | tf_op jit(solution)/shard_map/pallas_call | solution.py:320
  12.4 0.5 collective-permute-start
  13.0 6.7 %shard_map.56 = (bf16[16,128,256]{2,1,0:T(8,128)(2,1)}, bf16[16,128,128]{2,1,0:T(8,128)(2,1)}, bf16[16,128,256]{2,1,0:T(8,128)(2,1)}) custom-call(s32[1]{0:T(128)} %bitcast.l_ref, bf16[64,128,512]{2,1,0:T(8,128)(2,1)} %three_ref.3, bf16[64,64]{1,0:T(8,128)(2,1)} %metric_ref.3, s32[16,16,64]{2,1,0:T(8,128)} %bitcast.3), custom_call_target="tpu_custom_call" | custom-call | flops 2147483648 | bytes 8388608 | tf_op jit(solution)/shard_map/pallas_call | solution.py:304
  19.7 0.4 collective-permute-start.1
  20.1 2.6 %collective-permute-start.4 = (bf16[128,512]{1,0:T(8,128)(2,1)S(1)}, bf16[128,512]{1,0:T(8,128)(2,1)S(1)}, u32[]{:S(2)}, u32[]{:S(2)}) collective-permute-start(bf16[128,512]{1,0:T(8,128)(2,1)S(1)} %copy-done.1), channel_id=1, source_target_pairs={{0,2},{1,3},{2,0},{3,1},{4,6},{5,7},{6,4},{7,5},{8,10},{9,11},{10,... | collective-permute-start | bytes 393224 | tf_op jit(solution)/shard_map/ppermute | solution.py:268
  22.9 3.9 %collective-permute-done.4.d2_ref = bf16[128,512]{1,0:T(8,128)(2,1)S(1)} collective-permute-done((bf16[128,512]{1,0:T(8,128)(2,1)S(1)}, bf16[128,512]{1,0:T(8,128)(2,1)S(1)}, u32[]{:S(2)}, u32[]{:S(2)}) %collective-permute-start.4) | collective-permute-done | bytes 131104 | tf_op jit(solution)/shard_map/ppermute | solution.py:268
  26.8 1.7 %collective-permute-start.9 = (bf16[16,128,256]{2,1,0:T(8,128)(2,1)}, bf16[16,128,256]{2,1,0:T(8,128)(2,1)S(1)}, u32[]{:S(2)}, u32[]{:S(2)}) collective-permute-start(bf16[16,128,256]{2,1,0:T(8,128)(2,1)} %get-tuple-element.21.refs_2_), channel_id=1, source_target_pairs={{0,2},{1,3},{2,0},{3,1},{4,6},{5,7},{6,4},{7,5},{8,10},{9,11},{10,... | collective-permute-start | bytes 3145736 | tf_op jit(solution)/shard_map/ppermute | solution.py:268
  28.6 1.3 %collective-permute-done.5.d3_ref = bf16[128,512]{1,0:T(8,128)(2,1)S(1)} collective-permute-done((bf16[128,512]{1,0:T(8,128)(2,1)S(1)}, bf16[128,512]{1,0:T(8,128)(2,1)S(1)}, u32[]{:S(2)}, u32[]{:S(2)}) %collective-permute-start.5) | collective-permute-done | bytes 131104 | tf_op jit(solution)/shard_map/ppermute | solution.py:268
  29.9 0.7 shard_map.57.refs_6_.refs_3_
  30.6 1.0 %copy-done = bf16[512,1024]{1,0:T(8,128)(2,1)} copy-done((bf16[512,1024]{1,0:T(8,128)(2,1)}, bf16[512,1024]{1,0:T(8,128)(2,1)S(1)}, u32[]{:S(2)}) %copy-start) | copy-done | bytes 1048600
  31.6 1.0 %copy-done.7 = bf16[16,128,256]{2,1,0:T(8,128)(2,1)} copy-done((bf16[16,128,256]{2,1,0:T(8,128)(2,1)}, bf16[16,128,256]{2,1,0:T(8,128)(2,1)S(1)}, u32[]{:S(2)}) %copy-start.7) | copy-done | bytes 1048600
  32.9 0.7 copy-done.6
  33.7 13.2 %shard_map.58 = (bf16[16,256,512]{2,1,0:T(8,128)(2,1)}, f32[128,256]{1,0:T(8,128)}, f32[128,256]{1,0:T(8,128)}) custom-call(s32[1]{0:T(128)} %bitcast.l_ref, bf16[16,128,512]{2,1,0:T(8,128)(2,1)} %get-tuple-element.19.refs_0_, bf16[16,128,512]{2,1,0:T(8,128)(2,1)} %copy-done.6, bf16[16,128,256]{2,1,0:T(8,128)(2,1)} %get-tuple-element.21.refs_2_, ...), custom_call_target="tpu_custom_call" | custom-call | flops 6442450944 | bytes 8388608 | tf_op jit(solution)/shard_map/pallas_call | solution.py:347
  46.8 8.3 %shard_map.59 = (bf16[16,512,256]{2,1,0:T(8,128)(2,1)}, f32[512,256]{1,0:T(8,128)}) custom-call(s32[1]{0:T(128)} %bitcast.l_ref, bf16[16,128,512]{2,1,0:T(8,128)(2,1)} %get-tuple-element.19.refs_0_, bf16[16,128,512]{2,1,0:T(8,128)(2,1)} %copy-done.6, bf16[16,256,512]{2,1,0:T(8,128)(2,1)} %get-tuple-element.27.refs_2_, bf16[512,1024]{1,0:T(8,128)(2,1)} %copy-done), custom_call_target="tpu_custom_call" | custom-call | flops 3221225472 | bytes 16777216 | tf_op jit(solution)/shard_map/pallas_call | solution.py:361
  55.2 7.1 %collective-permute-done.10.refs_2_ = bf16[16,128,128]{2,1,0:T(8,128)(2,1)S(1)} collective-permute-done((bf16[16,128,128]{2,1,0:T(8,128)(2,1)}, bf16[16,128,128]{2,1,0:T(8,128)(2,1)S(1)}, u32[]{:S(2)}, u32[]{:S(2)}) %collective-permute-start.10) | collective-permute-done | bytes 524320 | tf_op jit(solution)/shard_map/ppermute | solution.py:268
  62.3 0.8 copy-done.4
  63.4 5.4 %shard_map.60 = (f32[256,256]{1,0:T(8,128)}, f32[256,256]{1,0:T(8,128)}) custom-call(s32[1]{0:T(128)} %bitcast.l_ref, bf16[16,512,256]{2,1,0:T(8,128)(2,1)} %get-tuple-element.28.refs_0_, bf16[16,128,256]{2,1,0:T(8,128)(2,1)} %copy-done.3, bf16[16,128,128]{2,1,0:T(8,128)(2,1)} %copy-done.4, f32[512,256]{1,0:T(8,128)} %get-tuple-element.30.refs_3_), custom_call_target="tpu_custom_call" | custom-call | flops 1073741824 | bytes 8388608 | tf_op jit(solution)/shard_map/pallas_call | solution.py:375
  68.8 0.7 collective-permute-start.11
  69.6 1.3 %collective-permute-done.11 = f32[256,256]{1,0:T(8,128)S(1)} collective-permute-done((f32[256,256]{1,0:T(8,128)}, f32[256,256]{1,0:T(8,128)S(1)}, u32[]{:S(2)}, u32[]{:S(2)}) %collective-permute-start.11) | collective-permute-done | bytes 262176 | tf_op jit(solution)/shard_map/ppermute | solution.py:268
  70.9 1.0 %add.24 = f32[256,256]{1,0:T(8,128)S(1)} add(f32[256,256]{1,0:T(8,128)} %get-tuple-element.31, f32[256,256]{1,0:T(8,128)S(1)} %collective-permute-done.11) | non-fusion elementwise | flops 65536 | bytes 786432 | tf_op jit(solution)/shard_map/add | solution.py:386
  71.9 1.5 %collective-permute-start.12 = (bf16[128,256]{1,0:T(8,128)(2,1)S(1)}, bf16[128,256]{1,0:T(8,128)(2,1)S(1)}, u32[]{:S(2)}, u32[]{:S(2)}) collective-permute-start(bf16[128,256]{1,0:T(8,128)(2,1)S(1)} %slice.21), channel_id=1, source_target_pairs={{0,2},{1,3},{2,0},{3,1},{4,6},{5,7},{6,4},{7,5},{8,10},{9,11},{10,... | collective-permute-start | bytes 196616 | tf_op jit(solution)/shard_map/ppermute | solution.py:268
  73.5 1.6 %collective-permute-start.7 = (f32[128,256]{1,0:T(8,128)S(1)}, f32[128,256]{1,0:T(8,128)S(1)}, u32[]{:S(2)}, u32[]{:S(2)}) collective-permute-start(f32[128,256]{1,0:T(8,128)S(1)} %add.21), channel_id=1, source_target_pairs={{0,4},{4,0},{8,12},{12,8},{16,20},{20,16},{24,28},{28,24},{1,5},{5... | collective-permute-start | bytes 393224 | tf_op jit(solution)/shard_map/ppermute | solution.py:268
  75.1 1.3 %collective-permute-done.12 = bf16[128,256]{1,0:T(8,128)(2,1)S(1)} collective-permute-done((bf16[128,256]{1,0:T(8,128)(2,1)S(1)}, bf16[128,256]{1,0:T(8,128)(2,1)S(1)}, u32[]{:S(2)}, u32[]{:S(2)}) %collective-permute-start.12) | collective-permute-done | bytes 65568 | tf_op jit(solution)/shard_map/ppermute | solution.py:268
  76.4 1.5 %collective-permute-start.13 = (bf16[128,256]{1,0:T(8,128)(2,1)S(1)}, bf16[128,256]{1,0:T(8,128)(2,1)S(1)}, u32[]{:S(2)}, u32[]{:S(2)}) collective-permute-start(bf16[128,256]{1,0:T(8,128)(2,1)S(1)} %fusion.2), channel_id=1, source_target_pairs={{0,4},{4,0},{8,12},{12,8},{16,20},{20,16},{24,28},{28,24},{1,5},{5... | collective-permute-start | bytes 196616 | tf_op jit(solution)/shard_map/ppermute | solution.py:268
  77.9 1.7 %collective-permute-done.7 = f32[128,256]{1,0:T(8,128)S(1)} collective-permute-done((f32[128,256]{1,0:T(8,128)S(1)}, f32[128,256]{1,0:T(8,128)S(1)}, u32[]{:S(2)}, u32[]{:S(2)}) %collective-permute-start.7) | collective-permute-done | bytes 131104 | tf_op jit(solution)/shard_map/ppermute | solution.py:268
  79.6 1.7 %collective-permute-start.8 = (f32[128,256]{1,0:T(8,128)S(1)}, f32[128,256]{1,0:T(8,128)S(1)}, u32[]{:S(2)}, u32[]{:S(2)}) collective-permute-start(f32[128,256]{1,0:T(8,128)S(1)} %add.22), channel_id=1, source_target_pairs={{0,8},{4,12},{8,0},{12,4},{16,24},{20,28},{24,16},{28,20},{1,9},{5... | collective-permute-start | bytes 393224 | tf_op jit(solution)/shard_map/ppermute | solution.py:268
  81.3 1.1 %collective-permute-start.14 = (bf16[128,256]{1,0:T(8,128)(2,1)S(1)}, bf16[128,256]{1,0:T(8,128)(2,1)S(1)}, u32[]{:S(2)}, u32[]{:S(2)}) collective-permute-start(bf16[128,256]{1,0:T(8,128)(2,1)S(1)} %fusion.1), channel_id=1, source_target_pairs={{0,8},{4,12},{8,0},{12,4},{16,24},{20,28},{24,16},{28,20},{1,9},{5... | collective-permute-start | bytes 196616 | tf_op jit(solution)/shard_map/ppermute | solution.py:268
  82.3 2.3 %collective-permute-done.8 = f32[128,256]{1,0:T(8,128)S(1)} collective-permute-done((f32[128,256]{1,0:T(8,128)S(1)}, f32[128,256]{1,0:T(8,128)S(1)}, u32[]{:S(2)}, u32[]{:S(2)}) %collective-permute-start.8) | collective-permute-done | bytes 131104 | tf_op jit(solution)/shard_map/ppermute | solution.py:268
  84.6 1.0 %collective-permute-done.14 = bf16[128,256]{1,0:T(8,128)(2,1)S(1)} collective-permute-done((bf16[128,256]{1,0:T(8,128)(2,1)S(1)}, bf16[128,256]{1,0:T(8,128)(2,1)S(1)}, u32[]{:S(2)}, u32[]{:S(2)}) %collective-permute-start.14) | collective-permute-done | bytes 65568 | tf_op jit(solution)/shard_map/ppermute | solution.py:268
  85.7 3.4 %collective-permute-start.15 = (bf16[128,512]{1,0:T(8,128)(2,1)S(1)}, bf16[128,512]{1,0:T(8,128)(2,1)S(1)}, u32[]{:S(2)}, u32[]{:S(2)}) collective-permute-start(bf16[128,512]{1,0:T(8,128)(2,1)S(1)} %get-tuple-element.33), channel_id=1, source_target_pairs={{0,24},{4,28},{8,16},{12,20},{16,8},{20,12},{24,0},{28,4},{1,25},{... | collective-permute-start | bytes 393224 | tf_op jit(solution)/shard_map/ppermute | solution.py:268
  89.1 3.5 %collective-permute-done.15.got_ref = bf16[128,512]{1,0:T(8,128)(2,1)S(1)} collective-permute-done((bf16[128,512]{1,0:T(8,128)(2,1)S(1)}, bf16[128,512]{1,0:T(8,128)(2,1)S(1)}, u32[]{:S(2)}, u32[]{:S(2)}) %collective-permute-start.15) | collective-permute-done | bytes 131104 | tf_op jit(solution)/shard_map/ppermute | solution.py:268
  92.6 0.7 shard_map.61
  (36 shorter events, 1.3 us)
Async XLA Ops:
  12.4 19.2 %collective-permute-start = (bf16[16,128,512]{2,1,0:T(8,128)(2,1)}, bf16[16,128,512]{2,1,0:T(8,128)(2,1)S(1)}, u32[]{:S(2)}, u32[]{:S(2)}) collective-permute-start(bf16[16,128,512]{2,1,0:T(8,128)(2,1)} %get-tuple-element.20), channel_id=1, source_target_pairs={{0,1},{1,0},{2,3},{3,2},{4,5},{5,4},{6,7},{7,6},{8,9},{9,8},{10,11... | collective-permute-start | bytes 6291464 | tf_op jit(solution)/shard_map/ppermute | solution.py:268
  12.9 7.2 %copy-start.1 = (bf16[128,512]{1,0:T(8,128)(2,1)S(1)}, bf16[128,512]{1,0:T(8,128)(2,1)}, u32[]{:S(2)}) copy-start(bf16[128,512]{1,0:T(8,128)(2,1)} %d0_ref.1) | copy-start | bytes 393220
  12.9 17.0 %copy-start.2 = (s32[16,16]{1,0:T(8,128)S(1)}, s32[16,16]{1,0:T(8,128)}, u32[]{:S(2)}) copy-start(s32[16,16]{1,0:T(8,128)} %dp_ref.1) | copy-start | bytes 3076
  12.9 18.7 %collective-permute-start.2 = (bf16[16,128,256]{2,1,0:T(8,128)(2,1)}, bf16[16,128,256]{2,1,0:T(8,128)(2,1)S(1)}, u32[]{:S(2)}, u32[]{:S(2)}) collective-permute-start(bf16[16,128,256]{2,1,0:T(8,128)(2,1)} %get-tuple-element.24), channel_id=1, source_target_pairs={{0,1},{1,0},{2,3},{3,2},{4,5},{5,4},{6,7},{7,6},{8,9},{9,8},{10,11... | collective-permute-start | bytes 3145736 | tf_op jit(solution)/shard_map/ppermute | solution.py:268
  19.7 11.9 %collective-permute-start.1 = (bf16[16,128,256]{2,1,0:T(8,128)(2,1)}, bf16[16,128,256]{2,1,0:T(8,128)(2,1)S(1)}, u32[]{:S(2)}, u32[]{:S(2)}) collective-permute-start(bf16[16,128,256]{2,1,0:T(8,128)(2,1)} %get-tuple-element.23), channel_id=1, source_target_pairs={{0,1},{1,0},{2,3},{3,2},{4,5},{5,4},{6,7},{7,6},{8,9},{9,8},{10,11... | collective-permute-start | bytes 3145736 | tf_op jit(solution)/shard_map/ppermute | solution.py:268
  20.1 6.7 %collective-permute-start.4 = (bf16[128,512]{1,0:T(8,128)(2,1)S(1)}, bf16[128,512]{1,0:T(8,128)(2,1)S(1)}, u32[]{:S(2)}, u32[]{:S(2)}) collective-permute-start(bf16[128,512]{1,0:T(8,128)(2,1)S(1)} %copy-done.1), channel_id=1, source_target_pairs={{0,2},{1,3},{2,0},{3,1},{4,6},{5,7},{6,4},{7,5},{8,10},{9,11},{10,... | collective-permute-start | bytes 393224 | tf_op jit(solution)/shard_map/ppermute | solution.py:268
  22.7 5.8 %collective-permute-start.3 = (bf16[128,512]{1,0:T(8,128)(2,1)S(1)}, bf16[128,512]{1,0:T(8,128)(2,1)S(1)}, u32[]{:S(2)}, u32[]{:S(2)}) collective-permute-start(bf16[128,512]{1,0:T(8,128)(2,1)S(1)} %copy-done.1), channel_id=1, source_target_pairs={{0,1},{1,0},{2,3},{3,2},{4,5},{5,4},{6,7},{7,6},{8,9},{9,8},{10,11... | collective-permute-start | bytes 393224 | tf_op jit(solution)/shard_map/ppermute | solution.py:268
  26.8 35.4 %collective-permute-start.9 = (bf16[16,128,256]{2,1,0:T(8,128)(2,1)}, bf16[16,128,256]{2,1,0:T(8,128)(2,1)S(1)}, u32[]{:S(2)}, u32[]{:S(2)}) collective-permute-start(bf16[16,128,256]{2,1,0:T(8,128)(2,1)} %get-tuple-element.21.refs_2_), channel_id=1, source_target_pairs={{0,2},{1,3},{2,0},{3,1},{4,6},{5,7},{6,4},{7,5},{8,10},{9,11},{10,... | collective-permute-start | bytes 3145736 | tf_op jit(solution)/shard_map/ppermute | solution.py:268
  28.6 1.3 %collective-permute-start.5 = (bf16[128,512]{1,0:T(8,128)(2,1)S(1)}, bf16[128,512]{1,0:T(8,128)(2,1)S(1)}, u32[]{:S(2)}, u32[]{:S(2)}) collective-permute-start(bf16[128,512]{1,0:T(8,128)(2,1)S(1)} %collective-permute-done.4.d2_ref), channel_id=1, source_target_pairs={{0,1},{1,0},{2,3},{3,2},{4,5},{5,4},{6,7},{7,6},{8,9},{9,8},{10,11... | collective-permute-start | bytes 393224 | tf_op jit(solution)/shard_map/ppermute | solution.py:268
  29.9 32.3 %collective-permute-start.10 = (bf16[16,128,128]{2,1,0:T(8,128)(2,1)}, bf16[16,128,128]{2,1,0:T(8,128)(2,1)S(1)}, u32[]{:S(2)}, u32[]{:S(2)}) collective-permute-start(bf16[16,128,128]{2,1,0:T(8,128)(2,1)} %get-tuple-element.29), channel_id=1, source_target_pairs={{0,3},{1,2},{2,1},{3,0},{4,7},{5,6},{6,5},{7,4},{8,11},{9,10},{10,... | collective-permute-start | bytes 1572872 | tf_op jit(solution)/shard_map/ppermute | solution.py:268
  30.6 1.0 %copy-start = (bf16[512,1024]{1,0:T(8,128)(2,1)}, bf16[512,1024]{1,0:T(8,128)(2,1)S(1)}, u32[]{:S(2)}) copy-start(bf16[512,1024]{1,0:T(8,128)(2,1)S(1)} %shard_map.57.refs_6_.refs_3_) | copy-start | bytes 3145732
  31.6 1.0 %copy-start.7 = (bf16[16,128,256]{2,1,0:T(8,128)(2,1)}, bf16[16,128,256]{2,1,0:T(8,128)(2,1)S(1)}, u32[]{:S(2)}) copy-start(bf16[16,128,256]{2,1,0:T(8,128)(2,1)S(1)} %collective-permute-done.2.refs_5_) | copy-start | bytes 3145732
  31.6 1.3 %copy-start.8 = (bf16[16,128,256]{2,1,0:T(8,128)(2,1)}, bf16[16,128,256]{2,1,0:T(8,128)(2,1)S(1)}, u32[]{:S(2)}) copy-start(bf16[16,128,256]{2,1,0:T(8,128)(2,1)S(1)} %collective-permute-done.1.refs_4_) | copy-start | bytes 3145732
  31.6 2.0 %copy-start.6 = (bf16[16,128,512]{2,1,0:T(8,128)(2,1)}, bf16[16,128,512]{2,1,0:T(8,128)(2,1)S(1)}, u32[]{:S(2)}) copy-start(bf16[16,128,512]{2,1,0:T(8,128)(2,1)S(1)} %collective-permute-done.refs_1_) | copy-start | bytes 6291460
  55.2 14.4 %copy-start.9 = (f32[128,256]{1,0:T(8,128)S(1)}, f32[128,256]{1,0:T(8,128)}, u32[]{:S(2)}) copy-start(f32[128,256]{1,0:T(8,128)} %get-tuple-element.26) | copy-start | bytes 393220
  55.2 18.3 %copy-start.5 = (f32[128,256]{1,0:T(8,128)S(1)}, f32[128,256]{1,0:T(8,128)}, u32[]{:S(2)}) copy-start(f32[128,256]{1,0:T(8,128)} %get-tuple-element.25) | copy-start | bytes 393220
  62.2 0.8 copy-start.4
  62.3 1.2 %copy-start.3 = (bf16[16,128,256]{2,1,0:T(8,128)(2,1)}, bf16[16,128,256]{2,1,0:T(8,128)(2,1)S(1)}, u32[]{:S(2)}) copy-start(bf16[16,128,256]{2,1,0:T(8,128)(2,1)S(1)} %collective-permute-done.9.refs_1_) | copy-start | bytes 3145732
  68.8 2.1 %collective-permute-start.11 = (f32[256,256]{1,0:T(8,128)}, f32[256,256]{1,0:T(8,128)S(1)}, u32[]{:S(2)}, u32[]{:S(2)}) collective-permute-start(f32[256,256]{1,0:T(8,128)} %get-tuple-element.32), channel_id=1, source_target_pairs={{0,1},{1,0},{2,3},{3,2},{4,5},{5,4},{6,7},{7,6},{8,9},{9,8},{10,11... | collective-permute-start | bytes 786440 | tf_op jit(solution)/shard_map/ppermute | solution.py:268
  69.6 3.9 %collective-permute-start.6 = (f32[128,256]{1,0:T(8,128)S(1)}, f32[128,256]{1,0:T(8,128)S(1)}, u32[]{:S(2)}, u32[]{:S(2)}) collective-permute-start(f32[128,256]{1,0:T(8,128)S(1)} %copy-done.9), channel_id=1, source_target_pairs={{0,1},{1,0},{2,3},{3,2},{4,5},{5,4},{6,7},{7,6},{8,9},{9,8},{10,11... | collective-permute-start | bytes 393224 | tf_op jit(solution)/shard_map/ppermute | solution.py:268
  71.9 4.4 %collective-permute-start.12 = (bf16[128,256]{1,0:T(8,128)(2,1)S(1)}, bf16[128,256]{1,0:T(8,128)(2,1)S(1)}, u32[]{:S(2)}, u32[]{:S(2)}) collective-permute-start(bf16[128,256]{1,0:T(8,128)(2,1)S(1)} %slice.21), channel_id=1, source_target_pairs={{0,2},{1,3},{2,0},{3,1},{4,6},{5,7},{6,4},{7,5},{8,10},{9,11},{10,... | collective-permute-start | bytes 196616 | tf_op jit(solution)/shard_map/ppermute | solution.py:268
  73.5 6.0 %collective-permute-start.7 = (f32[128,256]{1,0:T(8,128)S(1)}, f32[128,256]{1,0:T(8,128)S(1)}, u32[]{:S(2)}, u32[]{:S(2)}) collective-permute-start(f32[128,256]{1,0:T(8,128)S(1)} %add.21), channel_id=1, source_target_pairs={{0,4},{4,0},{8,12},{12,8},{16,20},{20,16},{24,28},{28,24},{1,5},{5... | collective-permute-start | bytes 393224 | tf_op jit(solution)/shard_map/ppermute | solution.py:268
  76.4 4.9 %collective-permute-start.13 = (bf16[128,256]{1,0:T(8,128)(2,1)S(1)}, bf16[128,256]{1,0:T(8,128)(2,1)S(1)}, u32[]{:S(2)}, u32[]{:S(2)}) collective-permute-start(bf16[128,256]{1,0:T(8,128)(2,1)S(1)} %fusion.2), channel_id=1, source_target_pairs={{0,4},{4,0},{8,12},{12,8},{16,20},{20,16},{24,28},{28,24},{1,5},{5... | collective-permute-start | bytes 196616 | tf_op jit(solution)/shard_map/ppermute | solution.py:268
  79.6 5.0 %collective-permute-start.8 = (f32[128,256]{1,0:T(8,128)S(1)}, f32[128,256]{1,0:T(8,128)S(1)}, u32[]{:S(2)}, u32[]{:S(2)}) collective-permute-start(f32[128,256]{1,0:T(8,128)S(1)} %add.22), channel_id=1, source_target_pairs={{0,8},{4,12},{8,0},{12,4},{16,24},{20,28},{24,16},{28,20},{1,9},{5... | collective-permute-start | bytes 393224 | tf_op jit(solution)/shard_map/ppermute | solution.py:268
  81.3 4.3 %collective-permute-start.14 = (bf16[128,256]{1,0:T(8,128)(2,1)S(1)}, bf16[128,256]{1,0:T(8,128)(2,1)S(1)}, u32[]{:S(2)}, u32[]{:S(2)}) collective-permute-start(bf16[128,256]{1,0:T(8,128)(2,1)S(1)} %fusion.1), channel_id=1, source_target_pairs={{0,8},{4,12},{8,0},{12,4},{16,24},{20,28},{24,16},{28,20},{1,9},{5... | collective-permute-start | bytes 196616 | tf_op jit(solution)/shard_map/ppermute | solution.py:268
  85.7 6.9 %collective-permute-start.15 = (bf16[128,512]{1,0:T(8,128)(2,1)S(1)}, bf16[128,512]{1,0:T(8,128)(2,1)S(1)}, u32[]{:S(2)}, u32[]{:S(2)}) collective-permute-start(bf16[128,512]{1,0:T(8,128)(2,1)S(1)} %get-tuple-element.33), channel_id=1, source_target_pairs={{0,24},{4,28},{8,16},{12,20},{16,8},{20,12},{24,0},{28,4},{1,25},{... | collective-permute-start | bytes 393224 | tf_op jit(solution)/shard_map/ppermute | solution.py:268

commit v4 on v3

--- a/solution.py
+++ b/solution.py
@@ -287,13 +287,15 @@
     index = lax.axis_index("lay")
     l = jnp.reshape(index, (1,)).astype(jnp.int32)
     S = jax.ShapeDtypeStruct
+    three = pltpu.with_memory_space_constraint(three, pltpu.HBM)
+    metric = pltpu.with_memory_space_constraint(metric, pltpu.HBM)
     whole = lambda shape: pl.BlockSpec(shape, lambda t, s: (0,) * len(shape))
 
     d2 = swap(density, "lay", 2)
     d1 = swap(density, "lay", 1)
     d3 = swap(d2, "lay", 1)
 
-    pattern = jnp.transpose(tile_pattern, (1, 2, 0))
+    pattern = pltpu.with_memory_space_constraint(jnp.transpose(tile_pattern, (1, 2, 0)), pltpu.HBM)
     metric_spec = pl.BlockSpec((group, group), lambda t, s: (0, 0))
 
     def pattern_spec(rows):
@@ -310,7 +312,7 @@
         [pltpu.VMEM((2 * part * SUB, group * SUB), BF)],
         4 * part * SUB * group * half * block,
         group * block * half * 4,
-        vmem=57,
+        vmem=24,
     )(l, three, metric, pattern)
     far_straight = swap(straight, "lay", 2)
     far_cross = swap(cross, "lay", 3)
@@ -326,7 +328,7 @@
         [pltpu.VMEM((group * SUB, group * SUB), BF)],
         6 * part * SUB * group * width * block,
         group * block * width * 4,
-        vmem=57,
+        vmem=30,
     )(l, three, metric, pattern)
     got1 = swap(send1, "lay", 1)
     got4 = swap(send4, "lay", 1)
@@ -353,7 +355,6 @@
         [pltpu.VMEM((half, half), F32)],
         2 * part * 2 * half * width * (width + half),
         2 * part * half * width * 2,
-        vmem=57,
     )(l, keep0, got1, straight, keep2, got3, got4, dens)
     own = own_keep + swap(own_send, "lay", 1)
 
@@ -368,7 +369,6 @@
         [],
         part * 2 * half * (width * width + 2 * half * half),
         part * half * width * 8,
-        vmem=57,
     )(l, keep0, got1, inter, dens)
 
     count = 4
@@ -381,7 +381,6 @@
         [pltpu.VMEM((width, half), F32)],
         2 * part * width * half * half,
         part * width * half * 4,
-        vmem=57,
     )(l, left, far_straight, far_cross, far)
     far = kept + swap(sent, "lay", 1)
     far = far[:block] + swap(far[block:].astype(BF), "lay", 2).astype(F32)

time: 93.9 us -> 86.1 us (0.917)
  Pallas kernels: 47.4 us -> 35.7 us
  waiting for transfers between devices: 23.4 us -> 32.7 us
  local copies, waits for them, and re-layouts: 4.18 us -> 0.02 us
  other arithmetic: 1.15 us -> 0.2 us
    ppermute x16, waiting for transfers between devices: 23.4 us -> 32.7 us  [swap(): lax.ppermute(x, axis, [(i, i ^ bit) for i in range(lax.axis_size(axis))])]
    unnamed x20 -> x4, local copies, waits for them, and re-layouts: 4.17 us -> 0.01 us
    pallas_call x1, Pallas kernels: 8.32 us -> 4.37 us  [exchange_four(): call(no_index(local_kernel), (part // count,), [many(block, width)] * 2 +...]
    pallas_call x1, Pallas kernels: 5.42 us -> 2.12 us  [exchange_four(): call(no_index(far_kernel), (part // count,), [many(width, half), many(blo...]
    pallas_call x1, Pallas kernels: 13.2 us -> 10.4 us  [exchange_four(): call(no_index(own_kernel), (part // count,), [many(block, width)] * 2 + [...]
    add x1, other arithmetic: 0.99 us -> 0.03 us  [exchange_four(): far = kept + swap(sent, 'lay', 1)]
  transfers between devices with their start and end apart: 16 -> 16, of which waited for: 9 -> 9; matrix products, arithmetic and copies ran while one was open for 1% -> 0% of each run, Pallas kernels for 31% -> 25%
where the time goes in v4:
time: 86.1 us; the launch traced here: 86 us
  Pallas kernels  35.7 us (41%)
  waiting for transfers between devices  32.7 us (38%)
  starting transfers between devices  17.3 us (20%)
    ppermute x16, waiting for transfers between devices, swap(): lax.ppermute(x, axis, [(i, i ^ bit) for i in range(lax.axis_size(axis))])  32.7 us
    ppermute x16, starting transfers between devices, swap(): lax.ppermute(x, axis, [(i, i ^ bit) for i in range(lax.axis_size(axis))])  17.3 us
    pallas_call x1, Pallas kernels, exchange_four(): call(rest_kernel, (block // TILE,), [pl.BlockSpec((group, TILE, width), l...  11.6 us
    pallas_call x1, Pallas kernels, exchange_four(): call(no_index(own_kernel), (part // count,), [many(block, width)] * 2 + [...  10.4 us
    pallas_call x1, Pallas kernels, exchange_four(): call(near_kernel, (block // rows,), [pl.BlockSpec((group, rows, half), la...  5.79 us
    pallas_call x1, Pallas kernels, exchange_four(): call(no_index(local_kernel), (part // count,), [many(block, width)] * 2 +...  4.37 us
    pallas_call x1, Pallas kernels, exchange_four(): call(no_index(far_kernel), (part // count,), [many(width, half), many(blo...  2.12 us
  transfers between devices with their start and end apart: 16, of which 9 were waited for; matrix products, arithmetic and copies ran while one was open for 0% of the time, Pallas kernels for 25%

profile of v4, /device:TPU:0, one launch (start us, length us, event | category | flops | bytes accessed | tf_op | source)
XLA Modules:
  0.0 86.0 jit_solution(9931250485091103869)
XLA Ops:
  0.0 11.6 %shard_map.55 = (bf16[16,128,512]{2,1,0:T(8,128)(2,1)S(1)}, bf16[16,128,512]{2,1,0:T(8,128)(2,1)S(1)}, bf16[16,128,256]{2,1,0:T(8,128)(2,1)S(1)}, bf16[16,128,256]{2,1,0:T(8,128)(2,1)S(1)}) custom-call(s32[1]{0:T(128)} %bitcast.l_ref, bf16[64,128,512]{2,1,0:T(8,128)(2,1)} %three_ref.3, bf16[64,64]{1,0:T(8,128)(2,1)} %metric_ref.3, s32[16,16,64]{2,1,0:T(8,128)} %bitcast.2), custom_call_target="tpu_custom_call" | custom-call | flops 6442450944 | bytes 16777216 | tf_op jit(solution)/shard_map/pallas_call | solution.py:322
  11.6 0.6 collective-permute-start
  12.1 0.1 collective-permute-start.2
  12.2 5.8 %shard_map.56 = (bf16[16,128,256]{2,1,0:T(8,128)(2,1)S(1)}, bf16[16,128,128]{2,1,0:T(8,128)(2,1)S(1)}, bf16[16,128,256]{2,1,0:T(8,128)(2,1)S(1)}) custom-call(s32[1]{0:T(128)} %bitcast.l_ref, bf16[64,128,512]{2,1,0:T(8,128)(2,1)} %three_ref.3, bf16[64,64]{1,0:T(8,128)(2,1)} %metric_ref.3, s32[16,16,64]{2,1,0:T(8,128)} %bitcast.3), custom_call_target="tpu_custom_call" | custom-call | flops 2147483648 | bytes 8388608 | tf_op jit(solution)/shard_map/pallas_call | solution.py:306
  18.0 0.5 collective-permute-start.1
  18.5 2.6 %collective-permute-start.4 = (bf16[128,512]{1,0:T(8,128)(2,1)S(1)}, bf16[128,512]{1,0:T(8,128)(2,1)S(1)}, u32[]{:S(2)}, u32[]{:S(2)}) collective-permute-start(bf16[128,512]{1,0:T(8,128)(2,1)S(1)} %copy-done), channel_id=1, source_target_pairs={{0,2},{1,3},{2,0},{3,1},{4,6},{5,7},{6,4},{7,5},{8,10},{9,11},{10,... | collective-permute-start | bytes 393224 | tf_op jit(solution)/shard_map/ppermute | solution.py:268
  21.1 0.1 collective-permute-start.3
  21.2 3.9 %collective-permute-done.4.d2_ref = bf16[128,512]{1,0:T(8,128)(2,1)S(1)} collective-permute-done((bf16[128,512]{1,0:T(8,128)(2,1)S(1)}, bf16[128,512]{1,0:T(8,128)(2,1)S(1)}, u32[]{:S(2)}, u32[]{:S(2)}) %collective-permute-start.4) | collective-permute-done | bytes 131104 | tf_op jit(solution)/shard_map/ppermute | solution.py:268
  25.2 1.7 %collective-permute-start.9 = (bf16[16,128,256]{2,1,0:T(8,128)(2,1)S(1)}, bf16[16,128,256]{2,1,0:T(8,128)(2,1)S(1)}, u32[]{:S(2)}, u32[]{:S(2)}) collective-permute-start(bf16[16,128,256]{2,1,0:T(8,128)(2,1)S(1)} %get-tuple-element.21.refs_2_), channel_id=1, source_target_pairs={{0,2},{1,3},{2,0},{3,1},{4,6},{5,7},{6,4},{7,5},{8,10},{9,11},{10,... | collective-permute-start | bytes 3145736 | tf_op jit(solution)/shard_map/ppermute | solution.py:268
  26.9 1.3 %collective-permute-done.5.d3_ref = bf16[128,512]{1,0:T(8,128)(2,1)S(1)} collective-permute-done((bf16[128,512]{1,0:T(8,128)(2,1)S(1)}, bf16[128,512]{1,0:T(8,128)(2,1)S(1)}, u32[]{:S(2)}, u32[]{:S(2)}) %collective-permute-start.5) | collective-permute-done | bytes 131104 | tf_op jit(solution)/shard_map/ppermute | solution.py:268
  28.3 0.0 collective-permute-start.10
  28.3 0.7 shard_map.57.refs_6_.refs_3_
  29.0 0.0 collective-permute-done.2.refs_5_
  29.0 10.4 %shard_map.58 = (bf16[16,256,512]{2,1,0:T(8,128)(2,1)S(1)}, f32[128,256]{1,0:T(8,128)S(1)}, f32[128,256]{1,0:T(8,128)S(1)}) custom-call(s32[1]{0:T(128)} %bitcast.l_ref, bf16[16,128,512]{2,1,0:T(8,128)(2,1)S(1)} %get-tuple-element.19.refs_0_, bf16[16,128,512]{2,1,0:T(8,128)(2,1)S(1)} %collective-permute-done.refs_1_, ...), custom_call_target="tpu_custom_call" | custom-call | flops 6442450944 | bytes 8388608 | tf_op jit(solution)/shard_map/pallas_call | solution.py:349
  39.4 4.4 %shard_map.59 = (bf16[16,512,256]{2,1,0:T(8,128)(2,1)S(1)}, f32[512,256]{1,0:T(8,128)S(1)}) custom-call(s32[1]{0:T(128)} %bitcast.l_ref, bf16[16,128,512]{2,1,0:T(8,128)(2,1)S(1)} %get-tuple-element.19.refs_0_, bf16[16,128,512]{2,1,0:T(8,128)(2,1)S(1)} %collective-permute-done.refs_1_, bf16[16,256,512]{2,1,0:T(8,128)(2,1)S(1)} %get-tuple-element.27.refs_2_, ...), custom_call_target="tpu_custom_call" | custom-call | flops 3221225472 | bytes 16777216 | tf_op jit(solution)/shard_map/pallas_call | solution.py:362
  43.8 16.5 %collective-permute-done.10.refs_2_ = bf16[16,128,128]{2,1,0:T(8,128)(2,1)S(1)} collective-permute-done((bf16[16,128,128]{2,1,0:T(8,128)(2,1)S(1)}, bf16[16,128,128]{2,1,0:T(8,128)(2,1)S(1)}, u32[]{:S(2)}, u32[]{:S(2)}) %collective-permute-start.10) | collective-permute-done | bytes 524320 | tf_op jit(solution)/shard_map/ppermute | solution.py:268
  60.3 2.1 %shard_map.60 = (f32[256,256]{1,0:T(8,128)S(1)}, f32[256,256]{1,0:T(8,128)S(1)}) custom-call(s32[1]{0:T(128)} %bitcast.l_ref, bf16[16,512,256]{2,1,0:T(8,128)(2,1)S(1)} %get-tuple-element.28.refs_0_, bf16[16,128,256]{2,1,0:T(8,128)(2,1)S(1)} %collective-permute-done.9.refs_1_, bf16[16,128,128]{2,1,0:T(8,128)(2,1)S(1)} %collective-permute-done.10.refs_2_, ...), custom_call_target="tpu_custom_call" | custom-call | flops 1073741824 | bytes 8388608 | tf_op jit(solution)/shard_map/pallas_call | solution.py:375
  62.4 0.9 %collective-permute-start.11 = (f32[256,256]{1,0:T(8,128)S(1)}, f32[256,256]{1,0:T(8,128)S(1)}, u32[]{:S(2)}, u32[]{:S(2)}) collective-permute-start(f32[256,256]{1,0:T(8,128)S(1)} %get-tuple-element.32), channel_id=1, source_target_pairs={{0,1},{1,0},{2,3},{3,2},{4,5},{5,4},{6,7},{7,6},{8,9},{9,8},{10,11... | collective-permute-start | bytes 786440 | tf_op jit(solution)/shard_map/ppermute | solution.py:268
  63.3 0.1 collective-permute-start.6
  63.4 1.1 %collective-permute-done.11 = f32[256,256]{1,0:T(8,128)S(1)} collective-permute-done((f32[256,256]{1,0:T(8,128)S(1)}, f32[256,256]{1,0:T(8,128)S(1)}, u32[]{:S(2)}, u32[]{:S(2)}) %collective-permute-start.11) | collective-permute-done | bytes 262176 | tf_op jit(solution)/shard_map/ppermute | solution.py:268
  64.6 1.5 %collective-permute-start.12 = (bf16[128,256]{1,0:T(8,128)(2,1)S(1)}, bf16[128,256]{1,0:T(8,128)(2,1)S(1)}, u32[]{:S(2)}, u32[]{:S(2)}) collective-permute-start(bf16[128,256]{1,0:T(8,128)(2,1)S(1)} %slice.21), channel_id=1, source_target_pairs={{0,2},{1,3},{2,0},{3,1},{4,6},{5,7},{6,4},{7,5},{8,10},{9,11},{10,... | collective-permute-start | bytes 196616 | tf_op jit(solution)/shard_map/ppermute | solution.py:268
  66.1 1.6 %collective-permute-start.7 = (f32[128,256]{1,0:T(8,128)S(1)}, f32[128,256]{1,0:T(8,128)S(1)}, u32[]{:S(2)}, u32[]{:S(2)}) collective-permute-start(f32[128,256]{1,0:T(8,128)S(1)} %add.21), channel_id=1, source_target_pairs={{0,4},{4,0},{8,12},{12,8},{16,20},{20,16},{24,28},{28,24},{1,5},{5... | collective-permute-start | bytes 393224 | tf_op jit(solution)/shard_map/ppermute | solution.py:268
  67.7 1.3 %collective-permute-done.12 = bf16[128,256]{1,0:T(8,128)(2,1)S(1)} collective-permute-done((bf16[128,256]{1,0:T(8,128)(2,1)S(1)}, bf16[128,256]{1,0:T(8,128)(2,1)S(1)}, u32[]{:S(2)}, u32[]{:S(2)}) %collective-permute-start.12) | collective-permute-done | bytes 65568 | tf_op jit(solution)/shard_map/ppermute | solution.py:268
  69.0 1.5 %collective-permute-start.13 = (bf16[128,256]{1,0:T(8,128)(2,1)S(1)}, bf16[128,256]{1,0:T(8,128)(2,1)S(1)}, u32[]{:S(2)}, u32[]{:S(2)}) collective-permute-start(bf16[128,256]{1,0:T(8,128)(2,1)S(1)} %fusion.2), channel_id=1, source_target_pairs={{0,4},{4,0},{8,12},{12,8},{16,20},{20,16},{24,28},{28,24},{1,5},{5... | collective-permute-start | bytes 196616 | tf_op jit(solution)/shard_map/ppermute | solution.py:268
  70.5 1.7 %collective-permute-done.7 = f32[128,256]{1,0:T(8,128)S(1)} collective-permute-done((f32[128,256]{1,0:T(8,128)S(1)}, f32[128,256]{1,0:T(8,128)S(1)}, u32[]{:S(2)}, u32[]{:S(2)}) %collective-permute-start.7) | collective-permute-done | bytes 131104 | tf_op jit(solution)/shard_map/ppermute | solution.py:268
  72.2 1.7 %collective-permute-start.8 = (f32[128,256]{1,0:T(8,128)S(1)}, f32[128,256]{1,0:T(8,128)S(1)}, u32[]{:S(2)}, u32[]{:S(2)}) collective-permute-start(f32[128,256]{1,0:T(8,128)S(1)} %add.22), channel_id=1, source_target_pairs={{0,8},{4,12},{8,0},{12,4},{16,24},{20,28},{24,16},{28,20},{1,9},{5... | collective-permute-start | bytes 393224 | tf_op jit(solution)/shard_map/ppermute | solution.py:268
  73.9 1.0 %collective-permute-start.14 = (bf16[128,256]{1,0:T(8,128)(2,1)S(1)}, bf16[128,256]{1,0:T(8,128)(2,1)S(1)}, u32[]{:S(2)}, u32[]{:S(2)}) collective-permute-start(bf16[128,256]{1,0:T(8,128)(2,1)S(1)} %fusion.1), channel_id=1, source_target_pairs={{0,8},{4,12},{8,0},{12,4},{16,24},{20,28},{24,16},{28,20},{1,9},{5... | collective-permute-start | bytes 196616 | tf_op jit(solution)/shard_map/ppermute | solution.py:268
  74.9 2.3 %collective-permute-done.8 = f32[128,256]{1,0:T(8,128)S(1)} collective-permute-done((f32[128,256]{1,0:T(8,128)S(1)}, f32[128,256]{1,0:T(8,128)S(1)}, u32[]{:S(2)}, u32[]{:S(2)}) %collective-permute-start.8) | collective-permute-done | bytes 131104 | tf_op jit(solution)/shard_map/ppermute | solution.py:268
  77.2 1.0 %collective-permute-done.14 = bf16[128,256]{1,0:T(8,128)(2,1)S(1)} collective-permute-done((bf16[128,256]{1,0:T(8,128)(2,1)S(1)}, bf16[128,256]{1,0:T(8,128)(2,1)S(1)}, u32[]{:S(2)}, u32[]{:S(2)}) %collective-permute-start.14) | collective-permute-done | bytes 65568 | tf_op jit(solution)/shard_map/ppermute | solution.py:268
  78.3 3.4 %collective-permute-start.15 = (bf16[128,512]{1,0:T(8,128)(2,1)S(1)}, bf16[128,512]{1,0:T(8,128)(2,1)S(1)}, u32[]{:S(2)}, u32[]{:S(2)}) collective-permute-start(bf16[128,512]{1,0:T(8,128)(2,1)S(1)} %get-tuple-element.33), channel_id=1, source_target_pairs={{0,24},{4,28},{8,16},{12,20},{16,8},{20,12},{24,0},{28,4},{1,25},{... | collective-permute-start | bytes 393224 | tf_op jit(solution)/shard_map/ppermute | solution.py:268
  81.7 3.5 %collective-permute-done.15.got_ref = bf16[128,512]{1,0:T(8,128)(2,1)S(1)} collective-permute-done((bf16[128,512]{1,0:T(8,128)(2,1)S(1)}, bf16[128,512]{1,0:T(8,128)(2,1)S(1)}, u32[]{:S(2)}, u32[]{:S(2)}) %collective-permute-start.15) | collective-permute-done | bytes 131104 | tf_op jit(solution)/shard_map/ppermute | solution.py:268
  85.3 0.7 shard_map.61
  (20 shorter events, 0.2 us)
Async XLA Ops:
  11.6 17.4 %collective-permute-start = (bf16[16,128,512]{2,1,0:T(8,128)(2,1)S(1)}, bf16[16,128,512]{2,1,0:T(8,128)(2,1)S(1)}, u32[]{:S(2)}, u32[]{:S(2)}) collective-permute-start(bf16[16,128,512]{2,1,0:T(8,128)(2,1)S(1)} %get-tuple-element.20), channel_id=1, source_target_pairs={{0,1},{1,0},{2,3},{3,2},{4,5},{5,4},{6,7},{7,6},{8,9},{9,8},{10,11... | collective-permute-start | bytes 6291464 | tf_op jit(solution)/shard_map/ppermute | solution.py:268
  12.1 6.4 %copy-start = (bf16[128,512]{1,0:T(8,128)(2,1)S(1)}, bf16[128,512]{1,0:T(8,128)(2,1)}, u32[]{:S(2)}) copy-start(bf16[128,512]{1,0:T(8,128)(2,1)} %d0_ref.1) | copy-start | bytes 393220
  12.1 16.2 %copy-start.1 = (s32[16,16]{1,0:T(8,128)S(1)}, s32[16,16]{1,0:T(8,128)}, u32[]{:S(2)}) copy-start(s32[16,16]{1,0:T(8,128)} %dp_ref.1) | copy-start | bytes 3076
  12.1 16.9 %collective-permute-start.2 = (bf16[16,128,256]{2,1,0:T(8,128)(2,1)S(1)}, bf16[16,128,256]{2,1,0:T(8,128)(2,1)S(1)}, u32[]{:S(2)}, u32[]{:S(2)}) collective-permute-start(bf16[16,128,256]{2,1,0:T(8,128)(2,1)S(1)} %get-tuple-element.24), channel_id=1, source_target_pairs={{0,1},{1,0},{2,3},{3,2},{4,5},{5,4},{6,7},{7,6},{8,9},{9,8},{10,11... | collective-permute-start | bytes 3145736 | tf_op jit(solution)/shard_map/ppermute | solution.py:268
  18.0 11.0 %collective-permute-start.1 = (bf16[16,128,256]{2,1,0:T(8,128)(2,1)S(1)}, bf16[16,128,256]{2,1,0:T(8,128)(2,1)S(1)}, u32[]{:S(2)}, u32[]{:S(2)}) collective-permute-start(bf16[16,128,256]{2,1,0:T(8,128)(2,1)S(1)} %get-tuple-element.23), channel_id=1, source_target_pairs={{0,1},{1,0},{2,3},{3,2},{4,5},{5,4},{6,7},{7,6},{8,9},{9,8},{10,11... | collective-permute-start | bytes 3145736 | tf_op jit(solution)/shard_map/ppermute | solution.py:268
  18.5 6.7 %collective-permute-start.4 = (bf16[128,512]{1,0:T(8,128)(2,1)S(1)}, bf16[128,512]{1,0:T(8,128)(2,1)S(1)}, u32[]{:S(2)}, u32[]{:S(2)}) collective-permute-start(bf16[128,512]{1,0:T(8,128)(2,1)S(1)} %copy-done), channel_id=1, source_target_pairs={{0,2},{1,3},{2,0},{3,1},{4,6},{5,7},{6,4},{7,5},{8,10},{9,11},{10,... | collective-permute-start | bytes 393224 | tf_op jit(solution)/shard_map/ppermute | solution.py:268
  21.1 5.8 %collective-permute-start.3 = (bf16[128,512]{1,0:T(8,128)(2,1)S(1)}, bf16[128,512]{1,0:T(8,128)(2,1)S(1)}, u32[]{:S(2)}, u32[]{:S(2)}) collective-permute-start(bf16[128,512]{1,0:T(8,128)(2,1)S(1)} %copy-done), channel_id=1, source_target_pairs={{0,1},{1,0},{2,3},{3,2},{4,5},{5,4},{6,7},{7,6},{8,9},{9,8},{10,11... | collective-permute-start | bytes 393224 | tf_op jit(solution)/shard_map/ppermute | solution.py:268
  25.2 35.1 %collective-permute-start.9 = (bf16[16,128,256]{2,1,0:T(8,128)(2,1)S(1)}, bf16[16,128,256]{2,1,0:T(8,128)(2,1)S(1)}, u32[]{:S(2)}, u32[]{:S(2)}) collective-permute-start(bf16[16,128,256]{2,1,0:T(8,128)(2,1)S(1)} %get-tuple-element.21.refs_2_), channel_id=1, source_target_pairs={{0,2},{1,3},{2,0},{3,1},{4,6},{5,7},{6,4},{7,5},{8,10},{9,11},{10,... | collective-permute-start | bytes 3145736 | tf_op jit(solution)/shard_map/ppermute | solution.py:268
  26.9 1.3 %collective-permute-start.5 = (bf16[128,512]{1,0:T(8,128)(2,1)S(1)}, bf16[128,512]{1,0:T(8,128)(2,1)S(1)}, u32[]{:S(2)}, u32[]{:S(2)}) collective-permute-start(bf16[128,512]{1,0:T(8,128)(2,1)S(1)} %collective-permute-done.4.d2_ref), channel_id=1, source_target_pairs={{0,1},{1,0},{2,3},{3,2},{4,5},{5,4},{6,7},{7,6},{8,9},{9,8},{10,11... | collective-permute-start | bytes 393224 | tf_op jit(solution)/shard_map/ppermute | solution.py:268
  28.3 32.0 %collective-permute-start.10 = (bf16[16,128,128]{2,1,0:T(8,128)(2,1)S(1)}, bf16[16,128,128]{2,1,0:T(8,128)(2,1)S(1)}, u32[]{:S(2)}, u32[]{:S(2)}) collective-permute-start(bf16[16,128,128]{2,1,0:T(8,128)(2,1)S(1)} %get-tuple-element.29), channel_id=1, source_target_pairs={{0,3},{1,2},{2,1},{3,0},{4,7},{5,6},{6,5},{7,4},{8,11},{9,10},{10,... | collective-permute-start | bytes 1572872 | tf_op jit(solution)/shard_map/ppermute | solution.py:268
  62.4 2.1 %collective-permute-start.11 = (f32[256,256]{1,0:T(8,128)S(1)}, f32[256,256]{1,0:T(8,128)S(1)}, u32[]{:S(2)}, u32[]{:S(2)}) collective-permute-start(f32[256,256]{1,0:T(8,128)S(1)} %get-tuple-element.32), channel_id=1, source_target_pairs={{0,1},{1,0},{2,3},{3,2},{4,5},{5,4},{6,7},{7,6},{8,9},{9,8},{10,11... | collective-permute-start | bytes 786440 | tf_op jit(solution)/shard_map/ppermute | solution.py:268
  63.3 2.7 %collective-permute-start.6 = (f32[128,256]{1,0:T(8,128)S(1)}, f32[128,256]{1,0:T(8,128)S(1)}, u32[]{:S(2)}, u32[]{:S(2)}) collective-permute-start(f32[128,256]{1,0:T(8,128)S(1)} %get-tuple-element.26), channel_id=1, source_target_pairs={{0,1},{1,0},{2,3},{3,2},{4,5},{5,4},{6,7},{7,6},{8,9},{9,8},{10,11... | collective-permute-start | bytes 393224 | tf_op jit(solution)/shard_map/ppermute | solution.py:268
  64.6 4.4 %collective-permute-start.12 = (bf16[128,256]{1,0:T(8,128)(2,1)S(1)}, bf16[128,256]{1,0:T(8,128)(2,1)S(1)}, u32[]{:S(2)}, u32[]{:S(2)}) collective-permute-start(bf16[128,256]{1,0:T(8,128)(2,1)S(1)} %slice.21), channel_id=1, source_target_pairs={{0,2},{1,3},{2,0},{3,1},{4,6},{5,7},{6,4},{7,5},{8,10},{9,11},{10,... | collective-permute-start | bytes 196616 | tf_op jit(solution)/shard_map/ppermute | solution.py:268
  66.1 6.0 %collective-permute-start.7 = (f32[128,256]{1,0:T(8,128)S(1)}, f32[128,256]{1,0:T(8,128)S(1)}, u32[]{:S(2)}, u32[]{:S(2)}) collective-permute-start(f32[128,256]{1,0:T(8,128)S(1)} %add.21), channel_id=1, source_target_pairs={{0,4},{4,0},{8,12},{12,8},{16,20},{20,16},{24,28},{28,24},{1,5},{5... | collective-permute-start | bytes 393224 | tf_op jit(solution)/shard_map/ppermute | solution.py:268
  69.0 4.9 %collective-permute-start.13 = (bf16[128,256]{1,0:T(8,128)(2,1)S(1)}, bf16[128,256]{1,0:T(8,128)(2,1)S(1)}, u32[]{:S(2)}, u32[]{:S(2)}) collective-permute-start(bf16[128,256]{1,0:T(8,128)(2,1)S(1)} %fusion.2), channel_id=1, source_target_pairs={{0,4},{4,0},{8,12},{12,8},{16,20},{20,16},{24,28},{28,24},{1,5},{5... | collective-permute-start | bytes 196616 | tf_op jit(solution)/shard_map/ppermute | solution.py:268
  72.2 5.0 %collective-permute-start.8 = (f32[128,256]{1,0:T(8,128)S(1)}, f32[128,256]{1,0:T(8,128)S(1)}, u32[]{:S(2)}, u32[]{:S(2)}) collective-permute-start(f32[128,256]{1,0:T(8,128)S(1)} %add.22), channel_id=1, source_target_pairs={{0,8},{4,12},{8,0},{12,4},{16,24},{20,28},{24,16},{28,20},{1,9},{5... | collective-permute-start | bytes 393224 | tf_op jit(solution)/shard_map/ppermute | solution.py:268
  73.9 4.3 %collective-permute-start.14 = (bf16[128,256]{1,0:T(8,128)(2,1)S(1)}, bf16[128,256]{1,0:T(8,128)(2,1)S(1)}, u32[]{:S(2)}, u32[]{:S(2)}) collective-permute-start(bf16[128,256]{1,0:T(8,128)(2,1)S(1)} %fusion.1), channel_id=1, source_target_pairs={{0,8},{4,12},{8,0},{12,4},{16,24},{20,28},{24,16},{28,20},{1,9},{5... | collective-permute-start | bytes 196616 | tf_op jit(solution)/shard_map/ppermute | solution.py:268
  78.3 6.9 %collective-permute-start.15 = (bf16[128,512]{1,0:T(8,128)(2,1)S(1)}, bf16[128,512]{1,0:T(8,128)(2,1)S(1)}, u32[]{:S(2)}, u32[]{:S(2)}) collective-permute-start(bf16[128,512]{1,0:T(8,128)(2,1)S(1)} %get-tuple-element.33), channel_id=1, source_target_pairs={{0,24},{4,28},{8,16},{12,20},{16,8},{20,12},{24,0},{28,4},{1,25},{... | collective-permute-start | bytes 393224 | tf_op jit(solution)/shard_map/ppermute | solution.py:268

commit v5 on v4

--- a/solution.py
+++ b/solution.py
@@ -165,25 +165,36 @@
             dens_ref[j * block : (j + 1) * block, width + i * block : width + (i + 1) * block] = tile.T.astype(BF)
 
 
-def own_kernel(a_ref, pa_ref, b0_ref, b1_ref, pb0_ref, pb1_ref, dens_ref, inter_ref, keep_ref, send_ref, sum_ref):
+def own_far_kernel(b0_ref, b1_ref, pb0_ref, pb1_ref, dens_ref, sum_ref):
+    @pl.when(pl.program_id(0) == 0)
+    def _():
+        sum_ref[...] = jnp.zeros_like(sum_ref)
+
+    dens = dens_ref[...]
+    total = sum_ref[...]
+    for n in range(b0_ref.shape[0]):
+        top = jnp.concatenate([b0_ref[n], b1_ref[n]], axis=1)
+        low = jnp.concatenate([pb0_ref[n], pb1_ref[n]], axis=1)
+        rows = jnp.concatenate([top, low], axis=0)
+        total += dot_t(dot(rows, dens).astype(BF), rows)
+    sum_ref[...] = total
+
+
+def own_kernel(a_ref, pa_ref, dens_ref, begun_ref, inter_ref, keep_ref, send_ref, sum_ref):
     step = pl.program_id(0)
     count, block, _ = a_ref.shape
+
+    @pl.when(step == 0)
+    def _():
+        sum_ref[...] = begun_ref[...]
+
     dens = dens_ref[...]
-
-    @pl.when(step == 0)
-    def _():
-        sum_ref[...] = jnp.zeros_like(sum_ref)
-
     total = sum_ref[...]
     for n in range(count):
         rows = jnp.concatenate([a_ref[n], pa_ref[n]], axis=0)
         inter = dot(rows, dens).astype(BF)
         inter_ref[n] = inter
         total += dot_t(inter, rows)
-        top = jnp.concatenate([b0_ref[n], b1_ref[n]], axis=1)
-        low = jnp.concatenate([pb0_ref[n], pb1_ref[n]], axis=1)
-        rows = jnp.concatenate([top, low], axis=0)
-        total += dot_t(dot(rows, dens).astype(BF), rows)
     sum_ref[...] = total
 
     @pl.when(step == pl.num_programs(0) - 1)
@@ -344,21 +355,33 @@
         4 * width * width * 2,
     )(l, density, d1, d2, d3, dens_pattern)
 
-    count = 2
+    count = min(4, part)
     many = lambda a, b: pl.BlockSpec((count, a, b), lambda t, s: (t, 0, 0))
+    square = pl.BlockSpec((width, width), lambda t, s: (0, 0))
+    own_flops = 2 * part * half * width * (width + half)
+    begun = call(
+        no_index(own_far_kernel),
+        (part // count,),
+        [many(block, half)] * 4 + [square],
+        whole((half, half)),
+        S((half, half), F32),
+        [],
+        own_flops,
+        part * half * width * 2,
+    )(l, straight, keep2, got3, got4, dens)
     inter, own_keep, own_send = call(
         no_index(own_kernel),
         (part // count,),
-        [many(block, width)] * 2 + [many(block, half)] * 4 + [pl.BlockSpec((width, width), lambda t, s: (0, 0))],
+        [many(block, width)] * 2 + [square, whole((half, half))],
         [many(half, width), whole((block, half)), whole((block, half))],
         [S((part, half, width), BF), S((block, half), F32), S((block, half), F32)],
         [pltpu.VMEM((half, half), F32)],
-        2 * part * 2 * half * width * (width + half),
-        2 * part * half * width * 2,
-    )(l, keep0, got1, straight, keep2, got3, got4, dens)
+        own_flops,
+        part * half * width * 4,
+    )(l, keep0, got1, dens, begun)
     own = own_keep + swap(own_send, "lay", 1)
 
-    count = 4
+    count = min(8, part)
     left, far = call(
         no_index(local_kernel),
         (part // count,),
@@ -371,7 +394,6 @@
         part * half * width * 8,
     )(l, keep0, got1, inter, dens)
 
-    count = 4
     kept, sent = call(
         no_index(far_kernel),
         (part // count,),

time: 86.1 us -> 85.7 us (level)
  Pallas kernels: 35.7 us -> 34.6 us
    pallas_call x1, Pallas kernels: 10.4 us -> 5.15 us  [exchange_four(): call(no_index(own_kernel), (part // count,), [many(block, width)] * 2 + [...]
    pallas_call x0 -> x1, Pallas kernels: none -> 5.13 us  [exchange_four(): call(no_index(own_far_kernel), (part // count,), [many(block, half)] * 4...]
  transfers between devices with their start and end apart: 16 -> 16, of which waited for: 9 -> 9; matrix products, arithmetic and copies ran while one was open for 0% -> 0% of each run, Pallas kernels for 25% -> 24%
where the time goes in v5:
time: 85.7 us; the launch traced here: 85.6 us
  Pallas kernels  34.6 us (40%)
  waiting for transfers between devices  33.3 us (39%)
  starting transfers between devices  17.3 us (20%)
    ppermute x16, waiting for transfers between devices, swap(): lax.ppermute(x, axis, [(i, i ^ bit) for i in range(lax.axis_size(axis))])  33.3 us
    ppermute x16, starting transfers between devices, swap(): lax.ppermute(x, axis, [(i, i ^ bit) for i in range(lax.axis_size(axis))])  17.3 us
    pallas_call x1, Pallas kernels, exchange_four(): call(rest_kernel, (block // TILE,), [pl.BlockSpec((group, TILE, width), l...  11.6 us
    pallas_call x1, Pallas kernels, exchange_four(): call(near_kernel, (block // rows,), [pl.BlockSpec((group, rows, half), la...  5.79 us
    pallas_call x1, Pallas kernels, exchange_four(): call(no_index(own_kernel), (part // count,), [many(block, width)] * 2 + [...  5.15 us
    pallas_call x1, Pallas kernels, exchange_four(): call(no_index(own_far_kernel), (part // count,), [many(block, half)] * 4...  5.13 us
    pallas_call x1, Pallas kernels, exchange_four(): call(no_index(local_kernel), (part // count,), [many(block, width)] * 2 +...  3.87 us
  transfers between devices with their start and end apart: 16, of which 9 were waited for; matrix products, arithmetic and copies ran while one was open for 0% of the time, Pallas kernels for 24%

profile of v5, /device:TPU:0, one launch (start us, length us, event | category | flops | bytes accessed | tf_op | source)
XLA Modules:
  0.0 85.6 jit_solution(14731967600458845490)
XLA Ops:
  0.0 11.6 %shard_map.55 = (bf16[16,128,512]{2,1,0:T(8,128)(2,1)S(1)}, bf16[16,128,512]{2,1,0:T(8,128)(2,1)S(1)}, bf16[16,128,256]{2,1,0:T(8,128)(2,1)S(1)}, bf16[16,128,256]{2,1,0:T(8,128)(2,1)S(1)}) custom-call(s32[1]{0:T(128)} %bitcast.l_ref, bf16[64,128,512]{2,1,0:T(8,128)(2,1)} %three_ref.3, bf16[64,64]{1,0:T(8,128)(2,1)} %metric_ref.3, s32[16,16,64]{2,1,0:T(8,128)} %bitcast.2), custom_call_target="tpu_custom_call" | custom-call | flops 6442450944 | bytes 16777216 | tf_op jit(solution)/shard_map/pallas_call | solution.py:333
  11.6 0.6 collective-permute-start
  12.1 0.1 collective-permute-start.5
  12.2 5.8 %shard_map.57 = (bf16[16,128,256]{2,1,0:T(8,128)(2,1)S(1)}, bf16[16,128,128]{2,1,0:T(8,128)(2,1)S(1)}, bf16[16,128,256]{2,1,0:T(8,128)(2,1)S(1)}) custom-call(s32[1]{0:T(128)} %bitcast.l_ref, bf16[64,128,512]{2,1,0:T(8,128)(2,1)} %three_ref.3, bf16[64,64]{1,0:T(8,128)(2,1)} %metric_ref.3, s32[16,16,64]{2,1,0:T(8,128)} %bitcast.3), custom_call_target="tpu_custom_call" | custom-call | flops 2147483648 | bytes 8388608 | tf_op jit(solution)/shard_map/pallas_call | solution.py:317
  18.0 0.5 collective-permute-start.4
  18.5 2.6 %collective-permute-start.2 = (bf16[128,512]{1,0:T(8,128)(2,1)S(1)}, bf16[128,512]{1,0:T(8,128)(2,1)S(1)}, u32[]{:S(2)}, u32[]{:S(2)}) collective-permute-start(bf16[128,512]{1,0:T(8,128)(2,1)S(1)} %copy-done), channel_id=1, source_target_pairs={{0,2},{1,3},{2,0},{3,1},{4,6},{5,7},{6,4},{7,5},{8,10},{9,11},{10,... | collective-permute-start | bytes 393224 | tf_op jit(solution)/shard_map/ppermute | solution.py:279
  21.1 0.1 collective-permute-start.1
  21.2 3.9 %collective-permute-done.2.d2_ref = bf16[128,512]{1,0:T(8,128)(2,1)S(1)} collective-permute-done((bf16[128,512]{1,0:T(8,128)(2,1)S(1)}, bf16[128,512]{1,0:T(8,128)(2,1)S(1)}, u32[]{:S(2)}, u32[]{:S(2)}) %collective-permute-start.2) | collective-permute-done | bytes 131104 | tf_op jit(solution)/shard_map/ppermute | solution.py:279
  25.2 1.7 %collective-permute-start.9 = (bf16[16,128,256]{2,1,0:T(8,128)(2,1)S(1)}, bf16[16,128,256]{2,1,0:T(8,128)(2,1)S(1)}, u32[]{:S(2)}, u32[]{:S(2)}) collective-permute-start(bf16[16,128,256]{2,1,0:T(8,128)(2,1)S(1)} %get-tuple-element.21.refs_0_), channel_id=1, source_target_pairs={{0,2},{1,3},{2,0},{3,1},{4,6},{5,7},{6,4},{7,5},{8,10},{9,11},{10,... | collective-permute-start | bytes 3145736 | tf_op jit(solution)/shard_map/ppermute | solution.py:279
  26.9 1.3 %collective-permute-done.3.d3_ref = bf16[128,512]{1,0:T(8,128)(2,1)S(1)} collective-permute-done((bf16[128,512]{1,0:T(8,128)(2,1)S(1)}, bf16[128,512]{1,0:T(8,128)(2,1)S(1)}, u32[]{:S(2)}, u32[]{:S(2)}) %collective-permute-start.3) | collective-permute-done | bytes 131104 | tf_op jit(solution)/shard_map/ppermute | solution.py:279
  28.3 0.0 collective-permute-start.10
  28.3 0.7 shard_map.56.refs_4_.refs_2_.refs_3_
  29.0 5.1 %shard_map.58.refs_3_ = f32[256,256]{1,0:T(8,128)S(1)} custom-call(s32[1]{0:T(128)} %bitcast.l_ref, bf16[16,128,256]{2,1,0:T(8,128)(2,1)S(1)} %get-tuple-element.21.refs_0_, bf16[16,128,256]{2,1,0:T(8,128)(2,1)S(1)} %get-tuple-element.22.refs_1_, bf16[16,128,256]{2,1,0:T(8,128)(2,1)S(1)} %collective-permute-done.4.refs_2_, ...), custom_call_target="tpu_custom_call" | custom-call | flops 3221225472 | bytes 4194304 | tf_op jit(solution)/shard_map/pallas_call | solution.py:362
  34.2 5.2 %shard_map.59 = (bf16[16,256,512]{2,1,0:T(8,128)(2,1)S(1)}, f32[128,256]{1,0:T(8,128)S(1)}, f32[128,256]{1,0:T(8,128)S(1)}) custom-call(s32[1]{0:T(128)} %bitcast.l_ref, bf16[16,128,512]{2,1,0:T(8,128)(2,1)S(1)} %get-tuple-element.19.refs_0_, bf16[16,128,512]{2,1,0:T(8,128)(2,1)S(1)} %collective-permute-done.refs_1_, ...), custom_call_target="tpu_custom_call" | custom-call | flops 3221225472 | bytes 8388608 | tf_op jit(solution)/shard_map/pallas_call | solution.py:372
  39.3 3.9 %shard_map.60 = (bf16[16,512,256]{2,1,0:T(8,128)(2,1)S(1)}, f32[512,256]{1,0:T(8,128)S(1)}) custom-call(s32[1]{0:T(128)} %bitcast.l_ref, bf16[16,128,512]{2,1,0:T(8,128)(2,1)S(1)} %get-tuple-element.19.refs_0_, bf16[16,128,512]{2,1,0:T(8,128)(2,1)S(1)} %collective-permute-done.refs_1_, bf16[16,256,512]{2,1,0:T(8,128)(2,1)S(1)} %get-tuple-element.27.refs_2_, ...), custom_call_target="tpu_custom_call" | custom-call | flops 3221225472 | bytes 16777216 | tf_op jit(solution)/shard_map/pallas_call | solution.py:385
  43.2 17.1 %collective-permute-done.10.refs_2_ = bf16[16,128,128]{2,1,0:T(8,128)(2,1)S(1)} collective-permute-done((bf16[16,128,128]{2,1,0:T(8,128)(2,1)S(1)}, bf16[16,128,128]{2,1,0:T(8,128)(2,1)S(1)}, u32[]{:S(2)}, u32[]{:S(2)}) %collective-permute-start.10) | collective-permute-done | bytes 524320 | tf_op jit(solution)/shard_map/ppermute | solution.py:279
  60.3 1.7 %shard_map.61 = (f32[256,256]{1,0:T(8,128)S(1)}, f32[256,256]{1,0:T(8,128)S(1)}) custom-call(s32[1]{0:T(128)} %bitcast.l_ref, bf16[16,512,256]{2,1,0:T(8,128)(2,1)S(1)} %get-tuple-element.28.refs_0_, bf16[16,128,256]{2,1,0:T(8,128)(2,1)S(1)} %collective-permute-done.9.refs_1_, bf16[16,128,128]{2,1,0:T(8,128)(2,1)S(1)} %collective-permute-done.10.refs_2_, ...), custom_call_target="tpu_custom_call" | custom-call | flops 1073741824 | bytes 8388608 | tf_op jit(solution)/shard_map/pallas_call | solution.py:397
  62.0 0.9 %collective-permute-start.11 = (f32[256,256]{1,0:T(8,128)S(1)}, f32[256,256]{1,0:T(8,128)S(1)}, u32[]{:S(2)}, u32[]{:S(2)}) collective-permute-start(f32[256,256]{1,0:T(8,128)S(1)} %get-tuple-element.32), channel_id=1, source_target_pairs={{0,1},{1,0},{2,3},{3,2},{4,5},{5,4},{6,7},{7,6},{8,9},{9,8},{10,11... | collective-permute-start | bytes 786440 | tf_op jit(solution)/shard_map/ppermute | solution.py:279
  62.9 0.1 collective-permute-start.6
  63.0 1.1 %collective-permute-done.11 = f32[256,256]{1,0:T(8,128)S(1)} collective-permute-done((f32[256,256]{1,0:T(8,128)S(1)}, f32[256,256]{1,0:T(8,128)S(1)}, u32[]{:S(2)}, u32[]{:S(2)}) %collective-permute-start.11) | collective-permute-done | bytes 262176 | tf_op jit(solution)/shard_map/ppermute | solution.py:279
  64.1 1.5 %collective-permute-start.12 = (bf16[128,256]{1,0:T(8,128)(2,1)S(1)}, bf16[128,256]{1,0:T(8,128)(2,1)S(1)}, u32[]{:S(2)}, u32[]{:S(2)}) collective-permute-start(bf16[128,256]{1,0:T(8,128)(2,1)S(1)} %slice.21), channel_id=1, source_target_pairs={{0,2},{1,3},{2,0},{3,1},{4,6},{5,7},{6,4},{7,5},{8,10},{9,11},{10,... | collective-permute-start | bytes 196616 | tf_op jit(solution)/shard_map/ppermute | solution.py:279
  65.7 1.6 %collective-permute-start.7 = (f32[128,256]{1,0:T(8,128)S(1)}, f32[128,256]{1,0:T(8,128)S(1)}, u32[]{:S(2)}, u32[]{:S(2)}) collective-permute-start(f32[128,256]{1,0:T(8,128)S(1)} %add.21), channel_id=1, source_target_pairs={{0,4},{4,0},{8,12},{12,8},{16,20},{20,16},{24,28},{28,24},{1,5},{5... | collective-permute-start | bytes 393224 | tf_op jit(solution)/shard_map/ppermute | solution.py:279
  67.2 1.3 %collective-permute-done.12 = bf16[128,256]{1,0:T(8,128)(2,1)S(1)} collective-permute-done((bf16[128,256]{1,0:T(8,128)(2,1)S(1)}, bf16[128,256]{1,0:T(8,128)(2,1)S(1)}, u32[]{:S(2)}, u32[]{:S(2)}) %collective-permute-start.12) | collective-permute-done | bytes 65568 | tf_op jit(solution)/shard_map/ppermute | solution.py:279
  68.6 1.5 %collective-permute-start.13 = (bf16[128,256]{1,0:T(8,128)(2,1)S(1)}, bf16[128,256]{1,0:T(8,128)(2,1)S(1)}, u32[]{:S(2)}, u32[]{:S(2)}) collective-permute-start(bf16[128,256]{1,0:T(8,128)(2,1)S(1)} %fusion.2), channel_id=1, source_target_pairs={{0,4},{4,0},{8,12},{12,8},{16,20},{20,16},{24,28},{28,24},{1,5},{5... | collective-permute-start | bytes 196616 | tf_op jit(solution)/shard_map/ppermute | solution.py:279
  70.1 1.7 %collective-permute-done.7 = f32[128,256]{1,0:T(8,128)S(1)} collective-permute-done((f32[128,256]{1,0:T(8,128)S(1)}, f32[128,256]{1,0:T(8,128)S(1)}, u32[]{:S(2)}, u32[]{:S(2)}) %collective-permute-start.7) | collective-permute-done | bytes 131104 | tf_op jit(solution)/shard_map/ppermute | solution.py:279
  71.7 1.7 %collective-permute-start.8 = (f32[128,256]{1,0:T(8,128)S(1)}, f32[128,256]{1,0:T(8,128)S(1)}, u32[]{:S(2)}, u32[]{:S(2)}) collective-permute-start(f32[128,256]{1,0:T(8,128)S(1)} %add.22), channel_id=1, source_target_pairs={{0,8},{4,12},{8,0},{12,4},{16,24},{20,28},{24,16},{28,20},{1,9},{5... | collective-permute-start | bytes 393224 | tf_op jit(solution)/shard_map/ppermute | solution.py:279
  73.5 1.0 %collective-permute-start.14 = (bf16[128,256]{1,0:T(8,128)(2,1)S(1)}, bf16[128,256]{1,0:T(8,128)(2,1)S(1)}, u32[]{:S(2)}, u32[]{:S(2)}) collective-permute-start(bf16[128,256]{1,0:T(8,128)(2,1)S(1)} %fusion.1), channel_id=1, source_target_pairs={{0,8},{4,12},{8,0},{12,4},{16,24},{20,28},{24,16},{28,20},{1,9},{5... | collective-permute-start | bytes 196616 | tf_op jit(solution)/shard_map/ppermute | solution.py:279
  74.5 2.3 %collective-permute-done.8 = f32[128,256]{1,0:T(8,128)S(1)} collective-permute-done((f32[128,256]{1,0:T(8,128)S(1)}, f32[128,256]{1,0:T(8,128)S(1)}, u32[]{:S(2)}, u32[]{:S(2)}) %collective-permute-start.8) | collective-permute-done | bytes 131104 | tf_op jit(solution)/shard_map/ppermute | solution.py:279
  76.8 1.0 %collective-permute-done.14 = bf16[128,256]{1,0:T(8,128)(2,1)S(1)} collective-permute-done((bf16[128,256]{1,0:T(8,128)(2,1)S(1)}, bf16[128,256]{1,0:T(8,128)(2,1)S(1)}, u32[]{:S(2)}, u32[]{:S(2)}) %collective-permute-start.14) | collective-permute-done | bytes 65568 | tf_op jit(solution)/shard_map/ppermute | solution.py:279
  77.9 3.4 %collective-permute-start.15 = (bf16[128,512]{1,0:T(8,128)(2,1)S(1)}, bf16[128,512]{1,0:T(8,128)(2,1)S(1)}, u32[]{:S(2)}, u32[]{:S(2)}) collective-permute-start(bf16[128,512]{1,0:T(8,128)(2,1)S(1)} %get-tuple-element.33), channel_id=1, source_target_pairs={{0,24},{4,28},{8,16},{12,20},{16,8},{20,12},{24,0},{28,4},{1,25},{... | collective-permute-start | bytes 393224 | tf_op jit(solution)/shard_map/ppermute | solution.py:279
  81.3 3.5 %collective-permute-done.15.got_ref = bf16[128,512]{1,0:T(8,128)(2,1)S(1)} collective-permute-done((bf16[128,512]{1,0:T(8,128)(2,1)S(1)}, bf16[128,512]{1,0:T(8,128)(2,1)S(1)}, u32[]{:S(2)}, u32[]{:S(2)}) %collective-permute-start.15) | collective-permute-done | bytes 131104 | tf_op jit(solution)/shard_map/ppermute | solution.py:279
  84.8 0.7 shard_map.62
  (21 shorter events, 0.2 us)
Async XLA Ops:
  11.6 22.6 %collective-permute-start = (bf16[16,128,512]{2,1,0:T(8,128)(2,1)S(1)}, bf16[16,128,512]{2,1,0:T(8,128)(2,1)S(1)}, u32[]{:S(2)}, u32[]{:S(2)}) collective-permute-start(bf16[16,128,512]{2,1,0:T(8,128)(2,1)S(1)} %get-tuple-element.20), channel_id=1, source_target_pairs={{0,1},{1,0},{2,3},{3,2},{4,5},{5,4},{6,7},{7,6},{8,9},{9,8},{10,11... | collective-permute-start | bytes 6291464 | tf_op jit(solution)/shard_map/ppermute | solution.py:279
  12.1 6.4 %copy-start = (bf16[128,512]{1,0:T(8,128)(2,1)S(1)}, bf16[128,512]{1,0:T(8,128)(2,1)}, u32[]{:S(2)}) copy-start(bf16[128,512]{1,0:T(8,128)(2,1)} %d0_ref.1) | copy-start | bytes 393220
  12.1 16.2 %copy-start.1 = (s32[16,16]{1,0:T(8,128)S(1)}, s32[16,16]{1,0:T(8,128)}, u32[]{:S(2)}) copy-start(s32[16,16]{1,0:T(8,128)} %dp_ref.1) | copy-start | bytes 3076
  12.1 16.9 %collective-permute-start.5 = (bf16[16,128,256]{2,1,0:T(8,128)(2,1)S(1)}, bf16[16,128,256]{2,1,0:T(8,128)(2,1)S(1)}, u32[]{:S(2)}, u32[]{:S(2)}) collective-permute-start(bf16[16,128,256]{2,1,0:T(8,128)(2,1)S(1)} %get-tuple-element.24), channel_id=1, source_target_pairs={{0,1},{1,0},{2,3},{3,2},{4,5},{5,4},{6,7},{7,6},{8,9},{9,8},{10,11... | collective-permute-start | bytes 3145736 | tf_op jit(solution)/shard_map/ppermute | solution.py:279
  18.0 11.0 %collective-permute-start.4 = (bf16[16,128,256]{2,1,0:T(8,128)(2,1)S(1)}, bf16[16,128,256]{2,1,0:T(8,128)(2,1)S(1)}, u32[]{:S(2)}, u32[]{:S(2)}) collective-permute-start(bf16[16,128,256]{2,1,0:T(8,128)(2,1)S(1)} %get-tuple-element.23), channel_id=1, source_target_pairs={{0,1},{1,0},{2,3},{3,2},{4,5},{5,4},{6,7},{7,6},{8,9},{9,8},{10,11... | collective-permute-start | bytes 3145736 | tf_op jit(solution)/shard_map/ppermute | solution.py:279
  18.5 6.7 %collective-permute-start.2 = (bf16[128,512]{1,0:T(8,128)(2,1)S(1)}, bf16[128,512]{1,0:T(8,128)(2,1)S(1)}, u32[]{:S(2)}, u32[]{:S(2)}) collective-permute-start(bf16[128,512]{1,0:T(8,128)(2,1)S(1)} %copy-done), channel_id=1, source_target_pairs={{0,2},{1,3},{2,0},{3,1},{4,6},{5,7},{6,4},{7,5},{8,10},{9,11},{10,... | collective-permute-start | bytes 393224 | tf_op jit(solution)/shard_map/ppermute | solution.py:279
  21.1 5.8 %collective-permute-start.1 = (bf16[128,512]{1,0:T(8,128)(2,1)S(1)}, bf16[128,512]{1,0:T(8,128)(2,1)S(1)}, u32[]{:S(2)}, u32[]{:S(2)}) collective-permute-start(bf16[128,512]{1,0:T(8,128)(2,1)S(1)} %copy-done), channel_id=1, source_target_pairs={{0,1},{1,0},{2,3},{3,2},{4,5},{5,4},{6,7},{7,6},{8,9},{9,8},{10,11... | collective-permute-start | bytes 393224 | tf_op jit(solution)/shard_map/ppermute | solution.py:279
  25.2 35.1 %collective-permute-start.9 = (bf16[16,128,256]{2,1,0:T(8,128)(2,1)S(1)}, bf16[16,128,256]{2,1,0:T(8,128)(2,1)S(1)}, u32[]{:S(2)}, u32[]{:S(2)}) collective-permute-start(bf16[16,128,256]{2,1,0:T(8,128)(2,1)S(1)} %get-tuple-element.21.refs_0_), channel_id=1, source_target_pairs={{0,2},{1,3},{2,0},{3,1},{4,6},{5,7},{6,4},{7,5},{8,10},{9,11},{10,... | collective-permute-start | bytes 3145736 | tf_op jit(solution)/shard_map/ppermute | solution.py:279
  26.9 1.3 %collective-permute-start.3 = (bf16[128,512]{1,0:T(8,128)(2,1)S(1)}, bf16[128,512]{1,0:T(8,128)(2,1)S(1)}, u32[]{:S(2)}, u32[]{:S(2)}) collective-permute-start(bf16[128,512]{1,0:T(8,128)(2,1)S(1)} %collective-permute-done.2.d2_ref), channel_id=1, source_target_pairs={{0,1},{1,0},{2,3},{3,2},{4,5},{5,4},{6,7},{7,6},{8,9},{9,8},{10,11... | collective-permute-start | bytes 393224 | tf_op jit(solution)/shard_map/ppermute | solution.py:279
  28.3 32.0 %collective-permute-start.10 = (bf16[16,128,128]{2,1,0:T(8,128)(2,1)S(1)}, bf16[16,128,128]{2,1,0:T(8,128)(2,1)S(1)}, u32[]{:S(2)}, u32[]{:S(2)}) collective-permute-start(bf16[16,128,128]{2,1,0:T(8,128)(2,1)S(1)} %get-tuple-element.29), channel_id=1, source_target_pairs={{0,3},{1,2},{2,1},{3,0},{4,7},{5,6},{6,5},{7,4},{8,11},{9,10},{10,... | collective-permute-start | bytes 1572872 | tf_op jit(solution)/shard_map/ppermute | solution.py:279
  62.0 2.1 %collective-permute-start.11 = (f32[256,256]{1,0:T(8,128)S(1)}, f32[256,256]{1,0:T(8,128)S(1)}, u32[]{:S(2)}, u32[]{:S(2)}) collective-permute-start(f32[256,256]{1,0:T(8,128)S(1)} %get-tuple-element.32), channel_id=1, source_target_pairs={{0,1},{1,0},{2,3},{3,2},{4,5},{5,4},{6,7},{7,6},{8,9},{9,8},{10,11... | collective-permute-start | bytes 786440 | tf_op jit(solution)/shard_map/ppermute | solution.py:279
  62.9 2.7 %collective-permute-start.6 = (f32[128,256]{1,0:T(8,128)S(1)}, f32[128,256]{1,0:T(8,128)S(1)}, u32[]{:S(2)}, u32[]{:S(2)}) collective-permute-start(f32[128,256]{1,0:T(8,128)S(1)} %get-tuple-element.26), channel_id=1, source_target_pairs={{0,1},{1,0},{2,3},{3,2},{4,5},{5,4},{6,7},{7,6},{8,9},{9,8},{10,11... | collective-permute-start | bytes 393224 | tf_op jit(solution)/shard_map/ppermute | solution.py:279
  64.1 4.4 %collective-permute-start.12 = (bf16[128,256]{1,0:T(8,128)(2,1)S(1)}, bf16[128,256]{1,0:T(8,128)(2,1)S(1)}, u32[]{:S(2)}, u32[]{:S(2)}) collective-permute-start(bf16[128,256]{1,0:T(8,128)(2,1)S(1)} %slice.21), channel_id=1, source_target_pairs={{0,2},{1,3},{2,0},{3,1},{4,6},{5,7},{6,4},{7,5},{8,10},{9,11},{10,... | collective-permute-start | bytes 196616 | tf_op jit(solution)/shard_map/ppermute | solution.py:279
  65.7 6.0 %collective-permute-start.7 = (f32[128,256]{1,0:T(8,128)S(1)}, f32[128,256]{1,0:T(8,128)S(1)}, u32[]{:S(2)}, u32[]{:S(2)}) collective-permute-start(f32[128,256]{1,0:T(8,128)S(1)} %add.21), channel_id=1, source_target_pairs={{0,4},{4,0},{8,12},{12,8},{16,20},{20,16},{24,28},{28,24},{1,5},{5... | collective-permute-start | bytes 393224 | tf_op jit(solution)/shard_map/ppermute | solution.py:279
  68.6 4.9 %collective-permute-start.13 = (bf16[128,256]{1,0:T(8,128)(2,1)S(1)}, bf16[128,256]{1,0:T(8,128)(2,1)S(1)}, u32[]{:S(2)}, u32[]{:S(2)}) collective-permute-start(bf16[128,256]{1,0:T(8,128)(2,1)S(1)} %fusion.2), channel_id=1, source_target_pairs={{0,4},{4,0},{8,12},{12,8},{16,20},{20,16},{24,28},{28,24},{1,5},{5... | collective-permute-start | bytes 196616 | tf_op jit(solution)/shard_map/ppermute | solution.py:279
  71.7 5.0 %collective-permute-start.8 = (f32[128,256]{1,0:T(8,128)S(1)}, f32[128,256]{1,0:T(8,128)S(1)}, u32[]{:S(2)}, u32[]{:S(2)}) collective-permute-start(f32[128,256]{1,0:T(8,128)S(1)} %add.22), channel_id=1, source_target_pairs={{0,8},{4,12},{8,0},{12,4},{16,24},{20,28},{24,16},{28,20},{1,9},{5... | collective-permute-start | bytes 393224 | tf_op jit(solution)/shard_map/ppermute | solution.py:279
  73.5 4.3 %collective-permute-start.14 = (bf16[128,256]{1,0:T(8,128)(2,1)S(1)}, bf16[128,256]{1,0:T(8,128)(2,1)S(1)}, u32[]{:S(2)}, u32[]{:S(2)}) collective-permute-start(bf16[128,256]{1,0:T(8,128)(2,1)S(1)} %fusion.1), channel_id=1, source_target_pairs={{0,8},{4,12},{8,0},{12,4},{16,24},{20,28},{24,16},{28,20},{1,9},{5... | collective-permute-start | bytes 196616 | tf_op jit(solution)/shard_map/ppermute | solution.py:279
  77.9 6.9 %collective-permute-start.15 = (bf16[128,512]{1,0:T(8,128)(2,1)S(1)}, bf16[128,512]{1,0:T(8,128)(2,1)S(1)}, u32[]{:S(2)}, u32[]{:S(2)}) collective-permute-start(bf16[128,512]{1,0:T(8,128)(2,1)S(1)} %get-tuple-element.33), channel_id=1, source_target_pairs={{0,24},{4,28},{8,16},{12,20},{16,8},{20,12},{24,0},{28,4},{1,25},{... | collective-permute-start | bytes 393224 | tf_op jit(solution)/shard_map/ppermute | solution.py:279

commit v6 on v5

--- a/solution.py
+++ b/solution.py
@@ -96,7 +96,34 @@
     return [jnp.concatenate(pieces, axis=1) for pieces in out]
 
 
-def near_kernel(l_ref, three_ref, metric_ref, pattern_ref, straight_ref, cross_ref, core_ref, spread_ref):
+def packed(ref, at, x, first):
+    part, sub, block = x.shape
+    half = block // 2
+    if first < half:
+        ref[:, at + first : at + first + sub] = x
+        return
+    corner = jnp.concatenate([x[: part // 2, :, half:], x[part // 2 :, :, half:]], axis=2)
+    row = first - half
+    low = row // (half // 2)
+    row = at + half + row % (half // 2)
+    ref[low * (part // 2) : (low + 1) * (part // 2), row : row + sub] = corner
+
+
+def unpacked(ref, n, at):
+    part, _, block = ref.shape
+    half, quarter = block // 2, block // 4
+    top = ref[n, at : at + half]
+    k = n % (part // 2)
+    pair = [ref[k + m * (part // 2), at + half : at + half + quarter] for m in range(2)]
+    corner = jnp.concatenate(pair, axis=0)
+    corner = corner[:, half:] if n >= part // 2 else corner[:, :half]
+    low = jnp.concatenate([top[:, half:].T, corner], axis=1)
+    return jnp.concatenate([top, low], axis=0)
+
+
+def near_kernel(
+    l_ref, three_ref, metric_ref, pattern_ref, straight_ref, core_ref, straight_out, cross_out, spread_ref
+):
     l = l_ref[0]
 
     @pl.when(pl.program_id(0) == 0)
@@ -105,15 +132,24 @@
 
     part, rows, width = straight_ref.shape
     block = width // 2
+    steps = block // rows
     for first in range(0, rows, TILE):
         strips = masked_columns(l, (0, 1), (l // 2) * width, three_ref, pattern_ref, first)
         for n, data in enumerate(strips):
-            at = slice(first + n * SUB, first + (n + 1) * SUB)
+            lead = first + n * SUB
+            at = slice(lead, lead + SUB)
             got = dot(spread_ref[...], data).astype(BF)
-            straight_ref[:, at] = got[: part * SUB].reshape(part, SUB, width)
+            high = got[: part * SUB].reshape(part, SUB, width)
             low = got[part * SUB :].reshape(part, SUB, width)
-            cross_ref[:, at] = low[:, :, :block]
+            straight_ref[:, at] = high
             core_ref[:, at] = swapped(low, block)
+            for step in range(steps):
+
+                @pl.when(pl.program_id(0) == step)
+                def _(row=step * rows + lead):
+                    straight_out[:, row : row + SUB] = high[:, :, block:]
+                    packed(straight_out, block, high[:, :, :block], row)
+                    packed(cross_out, 0, low[:, :, :block], row)
 
 
 def swapped(x, block):
@@ -223,29 +259,21 @@
         left_ref[n, half:] = turned[:, half:]
 
 
-def far_kernel(left_ref, straight_ref, cross_ref, begun_ref, keep_ref, send_ref, sum_ref):
-    step = pl.program_id(0)
-    count, block, half = straight_ref.shape
-
-    @pl.when(step == 0)
-    def _():
-        sum_ref[...] = begun_ref[...]
-
-    total = sum_ref[...]
-    for n in range(count):
-        top = straight_ref[n]
-        low = jnp.concatenate([top[:, block:].T, cross_ref[n]], axis=1)
+def far_kernel(left_ref, straight_ref, cross_ref, begun_ref, keep_ref, send_ref):
+    part, _, block = cross_ref.shape
+    half = 2 * block
+    total = begun_ref[...]
+    for n in range(part):
+        side = straight_ref[n, :block]
+        top = jnp.concatenate([unpacked(straight_ref, n, block), side], axis=1)
+        low = jnp.concatenate([side.T, unpacked(cross_ref, n, 0)], axis=1)
         total += dot(left_ref[n], jnp.concatenate([top, low], axis=0))
-    sum_ref[...] = total
-
-    @pl.when(step == pl.num_programs(0) - 1)
-    def _():
-        ab = total[:half]
-        ba = total[half:].T
-        keep_ref[:block] = ab[:block]
-        keep_ref[block:] = ba[:block]
-        send_ref[:block] = swapped(ab[block:], block)
-        send_ref[block:] = swapped(ba[block:], block)
+    ab = total[:half]
+    ba = total[half:].T
+    keep_ref[:block] = ab[:block]
+    keep_ref[block:] = ba[:block]
+    send_ref[:block] = swapped(ab[block:], block)
+    send_ref[block:] = swapped(ba[block:], block)
 
 
 def place_kernel(l_ref, mine_ref, got_ref, out_ref):
@@ -312,21 +340,23 @@
     def pattern_spec(rows):
         return pl.BlockSpec((rows // TILE, tiles, group), lambda t, s: (s[0] * (block // rows) + t, 0, 0))
 
-    rows = 2 * TILE
-    strip = lambda n: pl.BlockSpec((part, 2 * TILE, n), lambda t, s: (0, t, 0))
-    straight, cross, send3 = call(
+    rows = block // 2
+    sent = block // 2 + block // 4
+    strip = lambda n: pl.BlockSpec((part, block // 2, n), lambda t, s: (0, t, 0))
+    straight, send3, straight_out, cross_out = call(
         near_kernel,
         (block // rows,),
         [pl.BlockSpec((group, rows, half), lambda t, s: (0, t, s[0] // 2)), metric_spec, pattern_spec(rows)],
-        [strip(half), strip(block), strip(half)],
-        [S((part, block, half), BF), S((part, block, block), BF), S((part, block, half), BF)],
+        [strip(half)] * 2 + [whole((part, block + sent, block)), whole((part, sent, block))],
+        [S((part, block, half), BF)] * 2
+        + [S((part, block + sent, block), BF), S((part, sent, block), BF)],
         [pltpu.VMEM((2 * part * SUB, group * SUB), BF)],
         4 * part * SUB * group * half * block,
         group * block * half * 4,
         vmem=24,
     )(l, three, metric, pattern)
-    far_straight = swap(straight, "lay", 2)
-    far_cross = swap(cross, "lay", 3)
+    far_straight = swap(straight_out, "lay", 2)
+    far_cross = swap(cross_out, "lay", 3)
     got3 = swap(send3, "lay", 1)
 
     tile = lambda n: pl.BlockSpec((part, TILE, n), lambda t, s: (0, t, 0))
@@ -355,7 +385,7 @@
         4 * width * width * 2,
     )(l, density, d1, d2, d3, dens_pattern)
 
-    count = min(4, part)
+    count = min(8, part)
     many = lambda a, b: pl.BlockSpec((count, a, b), lambda t, s: (t, 0, 0))
     square = pl.BlockSpec((width, width), lambda t, s: (0, 0))
     own_flops = 2 * part * half * width * (width + half)
@@ -394,17 +424,22 @@
         part * half * width * 8,
     )(l, keep0, got1, inter, dens)
 
-    kept, sent = call(
+    kept, sent_sum = call(
         no_index(far_kernel),
-        (part // count,),
-        [many(width, half), many(block, half), many(block, block), whole((width, half))],
+        (1,),
+        [
+            whole((part, width, half)),
+            whole((part, block + sent, block)),
+            whole((part, sent, block)),
+            whole((width, half)),
+        ],
         [whole((half, half))] * 2,
         [S((half, half), F32)] * 2,
-        [pltpu.VMEM((width, half), F32)],
+        [],
         2 * part * width * half * half,
         part * width * half * 4,
     )(l, left, far_straight, far_cross, far)
-    far = kept + swap(sent, "lay", 1)
+    far = kept + swap(sent_sum, "lay", 1)
     far = far[:block] + swap(far[block:].astype(BF), "lay", 2).astype(F32)
 
     steps = bits_of(lax.axis_size("blk"))

time: 85.7 us -> 84.6 us (0.987)
  waiting for transfers between devices: 33.3 us -> 29.4 us
  Pallas kernels: 34.6 us -> 36.3 us
  starting transfers between devices: 17.3 us -> 18.3 us
    ppermute x16, waiting for transfers between devices: 33.3 us -> 29.4 us  [swap(): lax.ppermute(x, axis, [(i, i ^ bit) for i in range(lax.axis_size(axis))])]
    pallas_call x1, Pallas kernels: 5.79 us -> 9.31 us  [exchange_four(): call(near_kernel, (block // rows,), [pl.BlockSpec((group, rows, half), la...]
    ppermute x16, starting transfers between devices: 17.3 us -> 18.3 us  [swap(): lax.ppermute(x, axis, [(i, i ^ bit) for i in range(lax.axis_size(axis))])]
    pallas_call x1, Pallas kernels: 5.15 us -> 4.27 us  [exchange_four(): call(no_index(own_kernel), (part // count,), [many(block, width)] * 2 + [...]
    pallas_call x1, Pallas kernels: 5.13 us -> 4.25 us  [exchange_four(): call(no_index(own_far_kernel), (part // count,), [many(block, half)] * 4...]
  transfers between devices with their start and end apart: 16 -> 16, of which waited for: 9 -> 8; matrix products, arithmetic and copies ran while one was open for 0% -> 0% of each run, Pallas kernels for 24% -> 27%
where the time goes in v6:
time: 84.6 us; the launch traced here: 84.4 us
  Pallas kernels  36.3 us (43%)
  waiting for transfers between devices  29.4 us (35%)
  starting transfers between devices  18.3 us (22%)
    ppermute x16, waiting for transfers between devices, swap(): lax.ppermute(x, axis, [(i, i ^ bit) for i in range(lax.axis_size(axis))])  29.4 us
    ppermute x16, starting transfers between devices, swap(): lax.ppermute(x, axis, [(i, i ^ bit) for i in range(lax.axis_size(axis))])  18.3 us
    pallas_call x1, Pallas kernels, exchange_four(): call(rest_kernel, (block // TILE,), [pl.BlockSpec((group, TILE, width), l...  11.6 us
    pallas_call x1, Pallas kernels, exchange_four(): call(near_kernel, (block // rows,), [pl.BlockSpec((group, rows, half), la...  9.31 us
    pallas_call x1, Pallas kernels, exchange_four(): call(no_index(own_kernel), (part // count,), [many(block, width)] * 2 + [...  4.27 us
    pallas_call x1, Pallas kernels, exchange_four(): call(no_index(own_far_kernel), (part // count,), [many(block, half)] * 4...  4.25 us
    pallas_call x1, Pallas kernels, exchange_four(): call(no_index(local_kernel), (part // count,), [many(block, width)] * 2 +...  3.87 us
  transfers between devices with their start and end apart: 16, of which 8 were waited for; matrix products, arithmetic and copies ran while one was open for 0% of the time, Pallas kernels for 27%

profile of v6, /device:TPU:0, one launch (start us, length us, event | category | flops | bytes accessed | tf_op | source)
XLA Modules:
  0.0 84.4 jit_solution(16172316068271024333)
XLA Ops:
  0.0 11.6 %shard_map.55 = (bf16[16,128,512]{2,1,0:T(8,128)(2,1)S(1)}, bf16[16,128,512]{2,1,0:T(8,128)(2,1)S(1)}, bf16[16,128,256]{2,1,0:T(8,128)(2,1)S(1)}, bf16[16,128,256]{2,1,0:T(8,128)(2,1)S(1)}) custom-call(s32[1]{0:T(128)} %bitcast.l_ref, bf16[64,128,512]{2,1,0:T(8,128)(2,1)} %three_ref.3, bf16[64,64]{1,0:T(8,128)(2,1)} %metric_ref.3, s32[16,16,64]{2,1,0:T(8,128)} %bitcast.2), custom_call_target="tpu_custom_call" | custom-call | flops 6442450944 | bytes 16777216 | tf_op jit(solution)/shard_map/pallas_call | solution.py:363
  11.6 0.6 collective-permute-start
  12.1 0.1 collective-permute-start.5
  12.2 9.3 %shard_map.57 = (bf16[16,128,256]{2,1,0:T(8,128)(2,1)S(1)}, bf16[16,128,256]{2,1,0:T(8,128)(2,1)S(1)}, bf16[16,224,128]{2,1,0:T(8,128)(2,1)S(1)}, bf16[16,96,128]{2,1,0:T(8,128)(2,1)S(1)}) custom-call(s32[1]{0:T(128)} %bitcast.l_ref, bf16[64,128,512]{2,1,0:T(8,128)(2,1)} %three_ref.3, bf16[64,64]{1,0:T(8,128)(2,1)} %metric_ref.3, s32[16,16,64]{2,1,0:T(8,128)} %bitcast.3), custom_call_target="tpu_custom_call" | custom-call | flops 2147483648 | bytes 8388608 | tf_op jit(solution)/shard_map/pallas_call | solution.py:346
  21.6 0.5 collective-permute-start.4
  22.0 2.6 %collective-permute-start.2 = (bf16[128,512]{1,0:T(8,128)(2,1)S(1)}, bf16[128,512]{1,0:T(8,128)(2,1)S(1)}, u32[]{:S(2)}, u32[]{:S(2)}) collective-permute-start(bf16[128,512]{1,0:T(8,128)(2,1)S(1)} %copy-done), channel_id=1, source_target_pairs={{0,2},{1,3},{2,0},{3,1},{4,6},{5,7},{6,4},{7,5},{8,10},{9,11},{10,... | collective-permute-start | bytes 393224 | tf_op jit(solution)/shard_map/ppermute | solution.py:307
  24.6 0.1 collective-permute-start.1
  24.8 3.9 %collective-permute-done.2.d2_ref = bf16[128,512]{1,0:T(8,128)(2,1)S(1)} collective-permute-done((bf16[128,512]{1,0:T(8,128)(2,1)S(1)}, bf16[128,512]{1,0:T(8,128)(2,1)S(1)}, u32[]{:S(2)}, u32[]{:S(2)}) %collective-permute-start.2) | collective-permute-done | bytes 131104 | tf_op jit(solution)/shard_map/ppermute | solution.py:307
  28.7 0.0 collective-permute-start.3
  28.7 1.7 %collective-permute-start.9 = (bf16[16,224,128]{2,1,0:T(8,128)(2,1)S(1)}, bf16[16,224,128]{2,1,0:T(8,128)(2,1)S(1)}, u32[]{:S(2)}, u32[]{:S(2)}) collective-permute-start(bf16[16,224,128]{2,1,0:T(8,128)(2,1)S(1)} %get-tuple-element.30), channel_id=1, source_target_pairs={{0,2},{1,3},{2,0},{3,1},{4,6},{5,7},{6,4},{7,5},{8,10},{9,11},{10,... | collective-permute-start | bytes 2752520 | tf_op jit(solution)/shard_map/ppermute | solution.py:307
  30.5 1.1 %collective-permute-start.10 = (bf16[16,96,128]{2,1,0:T(8,128)(2,1)S(1)}, bf16[16,96,128]{2,1,0:T(8,128)(2,1)S(1)}, u32[]{:S(2)}, u32[]{:S(2)}) collective-permute-start(bf16[16,96,128]{2,1,0:T(8,128)(2,1)S(1)} %get-tuple-element.31), channel_id=1, source_target_pairs={{0,3},{1,2},{2,1},{3,0},{4,7},{5,6},{6,5},{7,4},{8,11},{9,10},{10,... | collective-permute-start | bytes 1179656 | tf_op jit(solution)/shard_map/ppermute | solution.py:307
  31.6 0.7 shard_map.56.refs_4_.refs_2_.refs_3_
  32.3 4.3 %shard_map.58.refs_3_ = f32[256,256]{1,0:T(8,128)S(1)} custom-call(s32[1]{0:T(128)} %bitcast.l_ref, bf16[16,128,256]{2,1,0:T(8,128)(2,1)S(1)} %get-tuple-element.22.refs_0_, bf16[16,128,256]{2,1,0:T(8,128)(2,1)S(1)} %get-tuple-element.23.refs_1_, bf16[16,128,256]{2,1,0:T(8,128)(2,1)S(1)} %collective-permute-done.4.refs_2_, ...), custom_call_target="tpu_custom_call" | custom-call | flops 3221225472 | bytes 4194304 | tf_op jit(solution)/shard_map/pallas_call | solution.py:392
  36.5 4.3 %shard_map.59 = (bf16[16,256,512]{2,1,0:T(8,128)(2,1)S(1)}, f32[128,256]{1,0:T(8,128)S(1)}, f32[128,256]{1,0:T(8,128)S(1)}) custom-call(s32[1]{0:T(128)} %bitcast.l_ref, bf16[16,128,512]{2,1,0:T(8,128)(2,1)S(1)} %get-tuple-element.20.refs_0_, bf16[16,128,512]{2,1,0:T(8,128)(2,1)S(1)} %collective-permute-done.refs_1_, ...), custom_call_target="tpu_custom_call" | custom-call | flops 3221225472 | bytes 8388608 | tf_op jit(solution)/shard_map/pallas_call | solution.py:402
  40.8 3.9 %shard_map.60 = (bf16[16,512,256]{2,1,0:T(8,128)(2,1)S(1)}, f32[512,256]{1,0:T(8,128)S(1)}) custom-call(s32[1]{0:T(128)} %bitcast.l_ref, bf16[16,128,512]{2,1,0:T(8,128)(2,1)S(1)} %get-tuple-element.20.refs_0_, bf16[16,128,512]{2,1,0:T(8,128)(2,1)S(1)} %collective-permute-done.refs_1_, bf16[16,256,512]{2,1,0:T(8,128)(2,1)S(1)} %get-tuple-element.28.refs_2_, ...), custom_call_target="tpu_custom_call" | custom-call | flops 3221225472 | bytes 16777216 | tf_op jit(solution)/shard_map/pallas_call | solution.py:415
  44.7 14.8 %collective-permute-done.10.refs_2_ = bf16[16,96,128]{2,1,0:T(8,128)(2,1)S(1)} collective-permute-done((bf16[16,96,128]{2,1,0:T(8,128)(2,1)S(1)}, bf16[16,96,128]{2,1,0:T(8,128)(2,1)S(1)}, u32[]{:S(2)}, u32[]{:S(2)}) %collective-permute-start.10) | collective-permute-done | bytes 393248 | tf_op jit(solution)/shard_map/ppermute | solution.py:307
  59.4 1.6 %shard_map.61 = (f32[256,256]{1,0:T(8,128)S(1)}, f32[256,256]{1,0:T(8,128)S(1)}) custom-call(s32[1]{0:T(128)} %bitcast.l_ref, bf16[16,512,256]{2,1,0:T(8,128)(2,1)S(1)} %get-tuple-element.29.refs_0_, bf16[16,224,128]{2,1,0:T(8,128)(2,1)S(1)} %collective-permute-done.9.refs_1_, bf16[16,96,128]{2,1,0:T(8,128)(2,1)S(1)} %collective-permute-done.10.refs_2_, ...), custom_call_target="tpu_custom_call" | custom-call | flops 1073741824 | bytes 8388608 | tf_op jit(solution)/shard_map/pallas_call | solution.py:427
  61.1 0.4 collective-permute-start.11
  61.4 0.2 collective-permute-start.6
  61.7 1.0 %collective-permute-done.11 = f32[256,256]{1,0:T(8,128)S(1)} collective-permute-done((f32[256,256]{1,0:T(8,128)S(1)}, f32[256,256]{1,0:T(8,128)S(1)}, u32[]{:S(2)}, u32[]{:S(2)}) %collective-permute-start.11) | collective-permute-done | bytes 262176 | tf_op jit(solution)/shard_map/ppermute | solution.py:307
  62.7 1.8 %collective-permute-start.12 = (bf16[128,256]{1,0:T(8,128)(2,1)S(1)}, bf16[128,256]{1,0:T(8,128)(2,1)S(1)}, u32[]{:S(2)}, u32[]{:S(2)}) collective-permute-start(bf16[128,256]{1,0:T(8,128)(2,1)S(1)} %slice.21), channel_id=1, source_target_pairs={{0,2},{1,3},{2,0},{3,1},{4,6},{5,7},{6,4},{7,5},{8,10},{9,11},{10,... | collective-permute-start | bytes 196616 | tf_op jit(solution)/shard_map/ppermute | solution.py:307
  64.6 1.6 %collective-permute-start.7 = (f32[128,256]{1,0:T(8,128)S(1)}, f32[128,256]{1,0:T(8,128)S(1)}, u32[]{:S(2)}, u32[]{:S(2)}) collective-permute-start(f32[128,256]{1,0:T(8,128)S(1)} %add.21), channel_id=1, source_target_pairs={{0,4},{4,0},{8,12},{12,8},{16,20},{20,16},{24,28},{28,24},{1,5},{5... | collective-permute-start | bytes 393224 | tf_op jit(solution)/shard_map/ppermute | solution.py:307
  66.1 1.0 %collective-permute-done.12 = bf16[128,256]{1,0:T(8,128)(2,1)S(1)} collective-permute-done((bf16[128,256]{1,0:T(8,128)(2,1)S(1)}, bf16[128,256]{1,0:T(8,128)(2,1)S(1)}, u32[]{:S(2)}, u32[]{:S(2)}) %collective-permute-start.12) | collective-permute-done | bytes 65568 | tf_op jit(solution)/shard_map/ppermute | solution.py:307
  67.1 1.8 %collective-permute-start.13 = (bf16[128,256]{1,0:T(8,128)(2,1)S(1)}, bf16[128,256]{1,0:T(8,128)(2,1)S(1)}, u32[]{:S(2)}, u32[]{:S(2)}) collective-permute-start(bf16[128,256]{1,0:T(8,128)(2,1)S(1)} %fusion.2), channel_id=1, source_target_pairs={{0,4},{4,0},{8,12},{12,8},{16,20},{20,16},{24,28},{28,24},{1,5},{5... | collective-permute-start | bytes 196616 | tf_op jit(solution)/shard_map/ppermute | solution.py:307
  68.9 1.9 %collective-permute-done.7 = f32[128,256]{1,0:T(8,128)S(1)} collective-permute-done((f32[128,256]{1,0:T(8,128)S(1)}, f32[128,256]{1,0:T(8,128)S(1)}, u32[]{:S(2)}, u32[]{:S(2)}) %collective-permute-start.7) | collective-permute-done | bytes 131104 | tf_op jit(solution)/shard_map/ppermute | solution.py:307
  70.8 1.6 %collective-permute-start.8 = (f32[128,256]{1,0:T(8,128)S(1)}, f32[128,256]{1,0:T(8,128)S(1)}, u32[]{:S(2)}, u32[]{:S(2)}) collective-permute-start(f32[128,256]{1,0:T(8,128)S(1)} %add.22), channel_id=1, source_target_pairs={{0,8},{4,12},{8,0},{12,4},{16,24},{20,28},{24,16},{28,20},{1,9},{5... | collective-permute-start | bytes 393224 | tf_op jit(solution)/shard_map/ppermute | solution.py:307
  72.4 1.0 %collective-permute-start.14 = (bf16[128,256]{1,0:T(8,128)(2,1)S(1)}, bf16[128,256]{1,0:T(8,128)(2,1)S(1)}, u32[]{:S(2)}, u32[]{:S(2)}) collective-permute-start(bf16[128,256]{1,0:T(8,128)(2,1)S(1)} %fusion.1), channel_id=1, source_target_pairs={{0,8},{4,12},{8,0},{12,4},{16,24},{20,28},{24,16},{28,20},{1,9},{5... | collective-permute-start | bytes 196616 | tf_op jit(solution)/shard_map/ppermute | solution.py:307
  73.3 2.5 %collective-permute-done.8 = f32[128,256]{1,0:T(8,128)S(1)} collective-permute-done((f32[128,256]{1,0:T(8,128)S(1)}, f32[128,256]{1,0:T(8,128)S(1)}, u32[]{:S(2)}, u32[]{:S(2)}) %collective-permute-start.8) | collective-permute-done | bytes 131104 | tf_op jit(solution)/shard_map/ppermute | solution.py:307
  75.8 0.9 %collective-permute-done.14 = bf16[128,256]{1,0:T(8,128)(2,1)S(1)} collective-permute-done((bf16[128,256]{1,0:T(8,128)(2,1)S(1)}, bf16[128,256]{1,0:T(8,128)(2,1)S(1)}, u32[]{:S(2)}, u32[]{:S(2)}) %collective-permute-start.14) | collective-permute-done | bytes 65568 | tf_op jit(solution)/shard_map/ppermute | solution.py:307
  76.8 3.4 %collective-permute-start.15 = (bf16[128,512]{1,0:T(8,128)(2,1)S(1)}, bf16[128,512]{1,0:T(8,128)(2,1)S(1)}, u32[]{:S(2)}, u32[]{:S(2)}) collective-permute-start(bf16[128,512]{1,0:T(8,128)(2,1)S(1)} %get-tuple-element.35), channel_id=1, source_target_pairs={{0,24},{4,28},{8,16},{12,20},{16,8},{20,12},{24,0},{28,4},{1,25},{... | collective-permute-start | bytes 393224 | tf_op jit(solution)/shard_map/ppermute | solution.py:307
  80.2 3.5 %collective-permute-done.15.got_ref = bf16[128,512]{1,0:T(8,128)(2,1)S(1)} collective-permute-done((bf16[128,512]{1,0:T(8,128)(2,1)S(1)}, bf16[128,512]{1,0:T(8,128)(2,1)S(1)}, u32[]{:S(2)}, u32[]{:S(2)}) %collective-permute-start.15) | collective-permute-done | bytes 131104 | tf_op jit(solution)/shard_map/ppermute | solution.py:307
  83.7 0.7 shard_map.62
  (21 shorter events, 0.2 us)
Async XLA Ops:
  11.6 24.9 %collective-permute-start = (bf16[16,128,512]{2,1,0:T(8,128)(2,1)S(1)}, bf16[16,128,512]{2,1,0:T(8,128)(2,1)S(1)}, u32[]{:S(2)}, u32[]{:S(2)}) collective-permute-start(bf16[16,128,512]{2,1,0:T(8,128)(2,1)S(1)} %get-tuple-element.21), channel_id=1, source_target_pairs={{0,1},{1,0},{2,3},{3,2},{4,5},{5,4},{6,7},{7,6},{8,9},{9,8},{10,11... | collective-permute-start | bytes 6291464 | tf_op jit(solution)/shard_map/ppermute | solution.py:307
  12.1 9.9 %copy-start = (bf16[128,512]{1,0:T(8,128)(2,1)S(1)}, bf16[128,512]{1,0:T(8,128)(2,1)}, u32[]{:S(2)}) copy-start(bf16[128,512]{1,0:T(8,128)(2,1)} %d0_ref.1) | copy-start | bytes 393220
  12.1 19.4 %copy-start.1 = (s32[16,16]{1,0:T(8,128)S(1)}, s32[16,16]{1,0:T(8,128)}, u32[]{:S(2)}) copy-start(s32[16,16]{1,0:T(8,128)} %dp_ref.1) | copy-start | bytes 3076
  12.1 20.1 %collective-permute-start.5 = (bf16[16,128,256]{2,1,0:T(8,128)(2,1)S(1)}, bf16[16,128,256]{2,1,0:T(8,128)(2,1)S(1)}, u32[]{:S(2)}, u32[]{:S(2)}) collective-permute-start(bf16[16,128,256]{2,1,0:T(8,128)(2,1)S(1)} %get-tuple-element.25), channel_id=1, source_target_pairs={{0,1},{1,0},{2,3},{3,2},{4,5},{5,4},{6,7},{7,6},{8,9},{9,8},{10,11... | collective-permute-start | bytes 3145736 | tf_op jit(solution)/shard_map/ppermute | solution.py:307
  21.6 10.7 %collective-permute-start.4 = (bf16[16,128,256]{2,1,0:T(8,128)(2,1)S(1)}, bf16[16,128,256]{2,1,0:T(8,128)(2,1)S(1)}, u32[]{:S(2)}, u32[]{:S(2)}) collective-permute-start(bf16[16,128,256]{2,1,0:T(8,128)(2,1)S(1)} %get-tuple-element.24), channel_id=1, source_target_pairs={{0,1},{1,0},{2,3},{3,2},{4,5},{5,4},{6,7},{7,6},{8,9},{9,8},{10,11... | collective-permute-start | bytes 3145736 | tf_op jit(solution)/shard_map/ppermute | solution.py:307
  22.0 6.7 %collective-permute-start.2 = (bf16[128,512]{1,0:T(8,128)(2,1)S(1)}, bf16[128,512]{1,0:T(8,128)(2,1)S(1)}, u32[]{:S(2)}, u32[]{:S(2)}) collective-permute-start(bf16[128,512]{1,0:T(8,128)(2,1)S(1)} %copy-done), channel_id=1, source_target_pairs={{0,2},{1,3},{2,0},{3,1},{4,6},{5,7},{6,4},{7,5},{8,10},{9,11},{10,... | collective-permute-start | bytes 393224 | tf_op jit(solution)/shard_map/ppermute | solution.py:307
  24.6 4.1 %collective-permute-start.1 = (bf16[128,512]{1,0:T(8,128)(2,1)S(1)}, bf16[128,512]{1,0:T(8,128)(2,1)S(1)}, u32[]{:S(2)}, u32[]{:S(2)}) collective-permute-start(bf16[128,512]{1,0:T(8,128)(2,1)S(1)} %copy-done), channel_id=1, source_target_pairs={{0,1},{1,0},{2,3},{3,2},{4,5},{5,4},{6,7},{7,6},{8,9},{9,8},{10,11... | collective-permute-start | bytes 393224 | tf_op jit(solution)/shard_map/ppermute | solution.py:307
  28.7 1.8 %collective-permute-start.3 = (bf16[128,512]{1,0:T(8,128)(2,1)S(1)}, bf16[128,512]{1,0:T(8,128)(2,1)S(1)}, u32[]{:S(2)}, u32[]{:S(2)}) collective-permute-start(bf16[128,512]{1,0:T(8,128)(2,1)S(1)} %collective-permute-done.2.d2_ref), channel_id=1, source_target_pairs={{0,1},{1,0},{2,3},{3,2},{4,5},{5,4},{6,7},{7,6},{8,9},{9,8},{10,11... | collective-permute-start | bytes 393224 | tf_op jit(solution)/shard_map/ppermute | solution.py:307
  28.7 30.7 %collective-permute-start.9 = (bf16[16,224,128]{2,1,0:T(8,128)(2,1)S(1)}, bf16[16,224,128]{2,1,0:T(8,128)(2,1)S(1)}, u32[]{:S(2)}, u32[]{:S(2)}) collective-permute-start(bf16[16,224,128]{2,1,0:T(8,128)(2,1)S(1)} %get-tuple-element.30), channel_id=1, source_target_pairs={{0,2},{1,3},{2,0},{3,1},{4,6},{5,7},{6,4},{7,5},{8,10},{9,11},{10,... | collective-permute-start | bytes 2752520 | tf_op jit(solution)/shard_map/ppermute | solution.py:307
  30.5 29.0 %collective-permute-start.10 = (bf16[16,96,128]{2,1,0:T(8,128)(2,1)S(1)}, bf16[16,96,128]{2,1,0:T(8,128)(2,1)S(1)}, u32[]{:S(2)}, u32[]{:S(2)}) collective-permute-start(bf16[16,96,128]{2,1,0:T(8,128)(2,1)S(1)} %get-tuple-element.31), channel_id=1, source_target_pairs={{0,3},{1,2},{2,1},{3,0},{4,7},{5,6},{6,5},{7,4},{8,11},{9,10},{10,... | collective-permute-start | bytes 1179656 | tf_op jit(solution)/shard_map/ppermute | solution.py:307
  61.1 1.6 %collective-permute-start.11 = (f32[256,256]{1,0:T(8,128)S(1)}, f32[256,256]{1,0:T(8,128)S(1)}, u32[]{:S(2)}, u32[]{:S(2)}) collective-permute-start(f32[256,256]{1,0:T(8,128)S(1)} %get-tuple-element.34), channel_id=1, source_target_pairs={{0,1},{1,0},{2,3},{3,2},{4,5},{5,4},{6,7},{7,6},{8,9},{9,8},{10,11... | collective-permute-start | bytes 786440 | tf_op jit(solution)/shard_map/ppermute | solution.py:307
  61.4 3.1 %collective-permute-start.6 = (f32[128,256]{1,0:T(8,128)S(1)}, f32[128,256]{1,0:T(8,128)S(1)}, u32[]{:S(2)}, u32[]{:S(2)}) collective-permute-start(f32[128,256]{1,0:T(8,128)S(1)} %get-tuple-element.27), channel_id=1, source_target_pairs={{0,1},{1,0},{2,3},{3,2},{4,5},{5,4},{6,7},{7,6},{8,9},{9,8},{10,11... | collective-permute-start | bytes 393224 | tf_op jit(solution)/shard_map/ppermute | solution.py:307
  62.7 4.3 %collective-permute-start.12 = (bf16[128,256]{1,0:T(8,128)(2,1)S(1)}, bf16[128,256]{1,0:T(8,128)(2,1)S(1)}, u32[]{:S(2)}, u32[]{:S(2)}) collective-permute-start(bf16[128,256]{1,0:T(8,128)(2,1)S(1)} %slice.21), channel_id=1, source_target_pairs={{0,2},{1,3},{2,0},{3,1},{4,6},{5,7},{6,4},{7,5},{8,10},{9,11},{10,... | collective-permute-start | bytes 196616 | tf_op jit(solution)/shard_map/ppermute | solution.py:307
  64.6 6.2 %collective-permute-start.7 = (f32[128,256]{1,0:T(8,128)S(1)}, f32[128,256]{1,0:T(8,128)S(1)}, u32[]{:S(2)}, u32[]{:S(2)}) collective-permute-start(f32[128,256]{1,0:T(8,128)S(1)} %add.21), channel_id=1, source_target_pairs={{0,4},{4,0},{8,12},{12,8},{16,20},{20,16},{24,28},{28,24},{1,5},{5... | collective-permute-start | bytes 393224 | tf_op jit(solution)/shard_map/ppermute | solution.py:307
  67.1 5.2 %collective-permute-start.13 = (bf16[128,256]{1,0:T(8,128)(2,1)S(1)}, bf16[128,256]{1,0:T(8,128)(2,1)S(1)}, u32[]{:S(2)}, u32[]{:S(2)}) collective-permute-start(bf16[128,256]{1,0:T(8,128)(2,1)S(1)} %fusion.2), channel_id=1, source_target_pairs={{0,4},{4,0},{8,12},{12,8},{16,20},{20,16},{24,28},{28,24},{1,5},{5... | collective-permute-start | bytes 196616 | tf_op jit(solution)/shard_map/ppermute | solution.py:307
  70.8 5.0 %collective-permute-start.8 = (f32[128,256]{1,0:T(8,128)S(1)}, f32[128,256]{1,0:T(8,128)S(1)}, u32[]{:S(2)}, u32[]{:S(2)}) collective-permute-start(f32[128,256]{1,0:T(8,128)S(1)} %add.22), channel_id=1, source_target_pairs={{0,8},{4,12},{8,0},{12,4},{16,24},{20,28},{24,16},{28,20},{1,9},{5... | collective-permute-start | bytes 393224 | tf_op jit(solution)/shard_map/ppermute | solution.py:307
  72.4 4.3 %collective-permute-start.14 = (bf16[128,256]{1,0:T(8,128)(2,1)S(1)}, bf16[128,256]{1,0:T(8,128)(2,1)S(1)}, u32[]{:S(2)}, u32[]{:S(2)}) collective-permute-start(bf16[128,256]{1,0:T(8,128)(2,1)S(1)} %fusion.1), channel_id=1, source_target_pairs={{0,8},{4,12},{8,0},{12,4},{16,24},{20,28},{24,16},{28,20},{1,9},{5... | collective-permute-start | bytes 196616 | tf_op jit(solution)/shard_map/ppermute | solution.py:307
  76.8 6.9 %collective-permute-start.15 = (bf16[128,512]{1,0:T(8,128)(2,1)S(1)}, bf16[128,512]{1,0:T(8,128)(2,1)S(1)}, u32[]{:S(2)}, u32[]{:S(2)}) collective-permute-start(bf16[128,512]{1,0:T(8,128)(2,1)S(1)} %get-tuple-element.35), channel_id=1, source_target_pairs={{0,24},{4,28},{8,16},{12,20},{16,8},{20,12},{24,0},{28,4},{1,25},{... | collective-permute-start | bytes 393224 | tf_op jit(solution)/shard_map/ppermute | solution.py:307

commit v7 on v6

--- a/solution.py
+++ b/solution.py
@@ -96,17 +96,15 @@
     return [jnp.concatenate(pieces, axis=1) for pieces in out]
 
 
-def packed(ref, at, x, first):
-    part, sub, block = x.shape
-    half = block // 2
-    if first < half:
-        ref[:, at + first : at + first + sub] = x
+def packed(ref, at, x, upper):
+    part, half, _ = x.shape
+    if upper:
+        ref[:, at : at + half] = x
         return
     corner = jnp.concatenate([x[: part // 2, :, half:], x[part // 2 :, :, half:]], axis=2)
-    row = first - half
-    low = row // (half // 2)
-    row = at + half + row % (half // 2)
-    ref[low * (part // 2) : (low + 1) * (part // 2), row : row + sub] = corner
+    row, quarter = at + half, half // 2
+    ref[: part // 2, row : row + quarter] = corner[:, :quarter]
+    ref[part // 2 :, row : row + quarter] = corner[:, quarter:]
 
 
 def unpacked(ref, n, at):
@@ -143,13 +141,13 @@
             low = got[part * SUB :].reshape(part, SUB, width)
             straight_ref[:, at] = high
             core_ref[:, at] = swapped(low, block)
-            for step in range(steps):
-
-                @pl.when(pl.program_id(0) == step)
-                def _(row=step * rows + lead):
-                    straight_out[:, row : row + SUB] = high[:, :, block:]
-                    packed(straight_out, block, high[:, :, :block], row)
-                    packed(cross_out, 0, low[:, :, :block], row)
+    straight_out[:, pl.ds(pl.multiple_of(pl.program_id(0) * rows, rows), rows)] = straight_ref[:, :, block:]
+    for step in range(steps):
+
+        @pl.when(pl.program_id(0) == step)
+        def _(upper=step == 0):
+            packed(straight_out, block, straight_ref[:, :, :block], upper)
+            packed(cross_out, 0, core_ref[:, :, block:], upper)
 
 
 def swapped(x, block):

time: 84.6 us -> 81.4 us (0.962)
  Pallas kernels: 36.3 us -> 33.1 us
    pallas_call x1, Pallas kernels: 9.31 us -> 6.09 us  [exchange_four(): call(near_kernel, (block // rows,), [pl.BlockSpec((group, rows, half), la...]
  transfers between devices with their start and end apart: 16 -> 16, of which waited for: 8 -> 8; matrix products, arithmetic and copies ran while one was open for 0% -> 0% of each run, Pallas kernels for 27% -> 24%
where the time goes in v7:
time: 81.4 us; the launch traced here: 81.2 us
  Pallas kernels  33.1 us (41%)
  waiting for transfers between devices  29.4 us (36%)
  starting transfers between devices  18.3 us (22%)
    ppermute x16, waiting for transfers between devices, swap(): lax.ppermute(x, axis, [(i, i ^ bit) for i in range(lax.axis_size(axis))])  29.4 us
    ppermute x16, starting transfers between devices, swap(): lax.ppermute(x, axis, [(i, i ^ bit) for i in range(lax.axis_size(axis))])  18.3 us
    pallas_call x1, Pallas kernels, exchange_four(): call(rest_kernel, (block // TILE,), [pl.BlockSpec((group, TILE, width), l...  11.6 us
    pallas_call x1, Pallas kernels, exchange_four(): call(near_kernel, (block // rows,), [pl.BlockSpec((group, rows, half), la...  6.09 us
    pallas_call x1, Pallas kernels, exchange_four(): call(no_index(own_kernel), (part // count,), [many(block, width)] * 2 + [...  4.27 us
    pallas_call x1, Pallas kernels, exchange_four(): call(no_index(own_far_kernel), (part // count,), [many(block, half)] * 4...  4.25 us
    pallas_call x1, Pallas kernels, exchange_four(): call(no_index(local_kernel), (part // count,), [many(block, width)] * 2 +...  3.87 us
    pallas_call x1, Pallas kernels, exchange_four(): call(no_index(far_kernel), (1,), [whole((part, width, half)), whole((part...  1.63 us
  transfers between devices with their start and end apart: 16, of which 8 were waited for; matrix products, arithmetic and copies ran while one was open for 0% of the time, Pallas kernels for 24%

profile of v7, /device:TPU:0, one launch (start us, length us, event | category | flops | bytes accessed | tf_op | source)
XLA Modules:
  0.0 81.2 jit_solution(10646345830956199617)
XLA Ops:
  0.0 11.6 %shard_map.55 = (bf16[16,128,512]{2,1,0:T(8,128)(2,1)S(1)}, bf16[16,128,512]{2,1,0:T(8,128)(2,1)S(1)}, bf16[16,128,256]{2,1,0:T(8,128)(2,1)S(1)}, bf16[16,128,256]{2,1,0:T(8,128)(2,1)S(1)}) custom-call(s32[1]{0:T(128)} %bitcast.l_ref, bf16[64,128,512]{2,1,0:T(8,128)(2,1)} %three_ref.3, bf16[64,64]{1,0:T(8,128)(2,1)} %metric_ref.3, s32[16,16,64]{2,1,0:T(8,128)} %bitcast.2), custom_call_target="tpu_custom_call" | custom-call | flops 6442450944 | bytes 16777216 | tf_op jit(solution)/shard_map/pallas_call | solution.py:361
  11.6 0.6 collective-permute-start
  12.1 0.1 collective-permute-start.5
  12.2 6.1 %shard_map.57 = (bf16[16,128,256]{2,1,0:T(8,128)(2,1)S(1)}, bf16[16,128,256]{2,1,0:T(8,128)(2,1)S(1)}, bf16[16,224,128]{2,1,0:T(8,128)(2,1)S(1)}, bf16[16,96,128]{2,1,0:T(8,128)(2,1)S(1)}) custom-call(s32[1]{0:T(128)} %bitcast.l_ref, bf16[64,128,512]{2,1,0:T(8,128)(2,1)} %three_ref.3, bf16[64,64]{1,0:T(8,128)(2,1)} %metric_ref.3, s32[16,16,64]{2,1,0:T(8,128)} %bitcast.3), custom_call_target="tpu_custom_call" | custom-call | flops 2147483648 | bytes 8388608 | tf_op jit(solution)/shard_map/pallas_call | solution.py:344
  18.3 0.5 collective-permute-start.4
  18.8 2.6 %collective-permute-start.2 = (bf16[128,512]{1,0:T(8,128)(2,1)S(1)}, bf16[128,512]{1,0:T(8,128)(2,1)S(1)}, u32[]{:S(2)}, u32[]{:S(2)}) collective-permute-start(bf16[128,512]{1,0:T(8,128)(2,1)S(1)} %copy-done), channel_id=1, source_target_pairs={{0,2},{1,3},{2,0},{3,1},{4,6},{5,7},{6,4},{7,5},{8,10},{9,11},{10,... | collective-permute-start | bytes 393224 | tf_op jit(solution)/shard_map/ppermute | solution.py:305
  21.4 0.1 collective-permute-start.1
  21.5 3.9 %collective-permute-done.2.d2_ref = bf16[128,512]{1,0:T(8,128)(2,1)S(1)} collective-permute-done((bf16[128,512]{1,0:T(8,128)(2,1)S(1)}, bf16[128,512]{1,0:T(8,128)(2,1)S(1)}, u32[]{:S(2)}, u32[]{:S(2)}) %collective-permute-start.2) | collective-permute-done | bytes 131104 | tf_op jit(solution)/shard_map/ppermute | solution.py:305
  25.5 0.0 collective-permute-start.3
  25.5 1.7 %collective-permute-start.9 = (bf16[16,224,128]{2,1,0:T(8,128)(2,1)S(1)}, bf16[16,224,128]{2,1,0:T(8,128)(2,1)S(1)}, u32[]{:S(2)}, u32[]{:S(2)}) collective-permute-start(bf16[16,224,128]{2,1,0:T(8,128)(2,1)S(1)} %get-tuple-element.30), channel_id=1, source_target_pairs={{0,2},{1,3},{2,0},{3,1},{4,6},{5,7},{6,4},{7,5},{8,10},{9,11},{10,... | collective-permute-start | bytes 2752520 | tf_op jit(solution)/shard_map/ppermute | solution.py:305
  27.2 1.1 %collective-permute-start.10 = (bf16[16,96,128]{2,1,0:T(8,128)(2,1)S(1)}, bf16[16,96,128]{2,1,0:T(8,128)(2,1)S(1)}, u32[]{:S(2)}, u32[]{:S(2)}) collective-permute-start(bf16[16,96,128]{2,1,0:T(8,128)(2,1)S(1)} %get-tuple-element.31), channel_id=1, source_target_pairs={{0,3},{1,2},{2,1},{3,0},{4,7},{5,6},{6,5},{7,4},{8,11},{9,10},{10,... | collective-permute-start | bytes 1179656 | tf_op jit(solution)/shard_map/ppermute | solution.py:305
  28.3 0.7 shard_map.56.refs_4_.refs_2_.refs_3_
  29.0 4.3 %shard_map.58.refs_3_ = f32[256,256]{1,0:T(8,128)S(1)} custom-call(s32[1]{0:T(128)} %bitcast.l_ref, bf16[16,128,256]{2,1,0:T(8,128)(2,1)S(1)} %get-tuple-element.22.refs_0_, bf16[16,128,256]{2,1,0:T(8,128)(2,1)S(1)} %get-tuple-element.23.refs_1_, bf16[16,128,256]{2,1,0:T(8,128)(2,1)S(1)} %collective-permute-done.4.refs_2_, ...), custom_call_target="tpu_custom_call" | custom-call | flops 3221225472 | bytes 4194304 | tf_op jit(solution)/shard_map/pallas_call | solution.py:390
  33.3 4.3 %shard_map.59 = (bf16[16,256,512]{2,1,0:T(8,128)(2,1)S(1)}, f32[128,256]{1,0:T(8,128)S(1)}, f32[128,256]{1,0:T(8,128)S(1)}) custom-call(s32[1]{0:T(128)} %bitcast.l_ref, bf16[16,128,512]{2,1,0:T(8,128)(2,1)S(1)} %get-tuple-element.20.refs_0_, bf16[16,128,512]{2,1,0:T(8,128)(2,1)S(1)} %collective-permute-done.refs_1_, ...), custom_call_target="tpu_custom_call" | custom-call | flops 3221225472 | bytes 8388608 | tf_op jit(solution)/shard_map/pallas_call | solution.py:400
  37.6 3.9 %shard_map.60 = (bf16[16,512,256]{2,1,0:T(8,128)(2,1)S(1)}, f32[512,256]{1,0:T(8,128)S(1)}) custom-call(s32[1]{0:T(128)} %bitcast.l_ref, bf16[16,128,512]{2,1,0:T(8,128)(2,1)S(1)} %get-tuple-element.20.refs_0_, bf16[16,128,512]{2,1,0:T(8,128)(2,1)S(1)} %collective-permute-done.refs_1_, bf16[16,256,512]{2,1,0:T(8,128)(2,1)S(1)} %get-tuple-element.28.refs_2_, ...), custom_call_target="tpu_custom_call" | custom-call | flops 3221225472 | bytes 16777216 | tf_op jit(solution)/shard_map/pallas_call | solution.py:413
  41.5 14.8 %collective-permute-done.10.refs_2_ = bf16[16,96,128]{2,1,0:T(8,128)(2,1)S(1)} collective-permute-done((bf16[16,96,128]{2,1,0:T(8,128)(2,1)S(1)}, bf16[16,96,128]{2,1,0:T(8,128)(2,1)S(1)}, u32[]{:S(2)}, u32[]{:S(2)}) %collective-permute-start.10) | collective-permute-done | bytes 393248 | tf_op jit(solution)/shard_map/ppermute | solution.py:305
  56.2 1.6 %shard_map.61 = (f32[256,256]{1,0:T(8,128)S(1)}, f32[256,256]{1,0:T(8,128)S(1)}) custom-call(s32[1]{0:T(128)} %bitcast.l_ref, bf16[16,512,256]{2,1,0:T(8,128)(2,1)S(1)} %get-tuple-element.29.refs_0_, bf16[16,224,128]{2,1,0:T(8,128)(2,1)S(1)} %collective-permute-done.9.refs_1_, bf16[16,96,128]{2,1,0:T(8,128)(2,1)S(1)} %collective-permute-done.10.refs_2_, ...), custom_call_target="tpu_custom_call" | custom-call | flops 1073741824 | bytes 8388608 | tf_op jit(solution)/shard_map/pallas_call | solution.py:425
  57.9 0.4 collective-permute-start.11
  58.2 0.2 collective-permute-start.6
  58.4 1.0 %collective-permute-done.11 = f32[256,256]{1,0:T(8,128)S(1)} collective-permute-done((f32[256,256]{1,0:T(8,128)S(1)}, f32[256,256]{1,0:T(8,128)S(1)}, u32[]{:S(2)}, u32[]{:S(2)}) %collective-permute-start.11) | collective-permute-done | bytes 262176 | tf_op jit(solution)/shard_map/ppermute | solution.py:305
  59.5 1.8 %collective-permute-start.12 = (bf16[128,256]{1,0:T(8,128)(2,1)S(1)}, bf16[128,256]{1,0:T(8,128)(2,1)S(1)}, u32[]{:S(2)}, u32[]{:S(2)}) collective-permute-start(bf16[128,256]{1,0:T(8,128)(2,1)S(1)} %slice.21), channel_id=1, source_target_pairs={{0,2},{1,3},{2,0},{3,1},{4,6},{5,7},{6,4},{7,5},{8,10},{9,11},{10,... | collective-permute-start | bytes 196616 | tf_op jit(solution)/shard_map/ppermute | solution.py:305
  61.3 1.6 %collective-permute-start.7 = (f32[128,256]{1,0:T(8,128)S(1)}, f32[128,256]{1,0:T(8,128)S(1)}, u32[]{:S(2)}, u32[]{:S(2)}) collective-permute-start(f32[128,256]{1,0:T(8,128)S(1)} %add.21), channel_id=1, source_target_pairs={{0,4},{4,0},{8,12},{12,8},{16,20},{20,16},{24,28},{28,24},{1,5},{5... | collective-permute-start | bytes 393224 | tf_op jit(solution)/shard_map/ppermute | solution.py:305
  62.9 1.0 %collective-permute-done.12 = bf16[128,256]{1,0:T(8,128)(2,1)S(1)} collective-permute-done((bf16[128,256]{1,0:T(8,128)(2,1)S(1)}, bf16[128,256]{1,0:T(8,128)(2,1)S(1)}, u32[]{:S(2)}, u32[]{:S(2)}) %collective-permute-start.12) | collective-permute-done | bytes 65568 | tf_op jit(solution)/shard_map/ppermute | solution.py:305
  63.9 1.8 %collective-permute-start.13 = (bf16[128,256]{1,0:T(8,128)(2,1)S(1)}, bf16[128,256]{1,0:T(8,128)(2,1)S(1)}, u32[]{:S(2)}, u32[]{:S(2)}) collective-permute-start(bf16[128,256]{1,0:T(8,128)(2,1)S(1)} %fusion.2), channel_id=1, source_target_pairs={{0,4},{4,0},{8,12},{12,8},{16,20},{20,16},{24,28},{28,24},{1,5},{5... | collective-permute-start | bytes 196616 | tf_op jit(solution)/shard_map/ppermute | solution.py:305
  65.6 1.9 %collective-permute-done.7 = f32[128,256]{1,0:T(8,128)S(1)} collective-permute-done((f32[128,256]{1,0:T(8,128)S(1)}, f32[128,256]{1,0:T(8,128)S(1)}, u32[]{:S(2)}, u32[]{:S(2)}) %collective-permute-start.7) | collective-permute-done | bytes 131104 | tf_op jit(solution)/shard_map/ppermute | solution.py:305
  67.5 1.6 %collective-permute-start.8 = (f32[128,256]{1,0:T(8,128)S(1)}, f32[128,256]{1,0:T(8,128)S(1)}, u32[]{:S(2)}, u32[]{:S(2)}) collective-permute-start(f32[128,256]{1,0:T(8,128)S(1)} %add.22), channel_id=1, source_target_pairs={{0,8},{4,12},{8,0},{12,4},{16,24},{20,28},{24,16},{28,20},{1,9},{5... | collective-permute-start | bytes 393224 | tf_op jit(solution)/shard_map/ppermute | solution.py:305
  69.1 0.9 %collective-permute-start.14 = (bf16[128,256]{1,0:T(8,128)(2,1)S(1)}, bf16[128,256]{1,0:T(8,128)(2,1)S(1)}, u32[]{:S(2)}, u32[]{:S(2)}) collective-permute-start(bf16[128,256]{1,0:T(8,128)(2,1)S(1)} %fusion.1), channel_id=1, source_target_pairs={{0,8},{4,12},{8,0},{12,4},{16,24},{20,28},{24,16},{28,20},{1,9},{5... | collective-permute-start | bytes 196616 | tf_op jit(solution)/shard_map/ppermute | solution.py:305
  70.1 2.5 %collective-permute-done.8 = f32[128,256]{1,0:T(8,128)S(1)} collective-permute-done((f32[128,256]{1,0:T(8,128)S(1)}, f32[128,256]{1,0:T(8,128)S(1)}, u32[]{:S(2)}, u32[]{:S(2)}) %collective-permute-start.8) | collective-permute-done | bytes 131104 | tf_op jit(solution)/shard_map/ppermute | solution.py:305
  72.6 0.9 %collective-permute-done.14 = bf16[128,256]{1,0:T(8,128)(2,1)S(1)} collective-permute-done((bf16[128,256]{1,0:T(8,128)(2,1)S(1)}, bf16[128,256]{1,0:T(8,128)(2,1)S(1)}, u32[]{:S(2)}, u32[]{:S(2)}) %collective-permute-start.14) | collective-permute-done | bytes 65568 | tf_op jit(solution)/shard_map/ppermute | solution.py:305
  73.5 3.4 %collective-permute-start.15 = (bf16[128,512]{1,0:T(8,128)(2,1)S(1)}, bf16[128,512]{1,0:T(8,128)(2,1)S(1)}, u32[]{:S(2)}, u32[]{:S(2)}) collective-permute-start(bf16[128,512]{1,0:T(8,128)(2,1)S(1)} %get-tuple-element.35), channel_id=1, source_target_pairs={{0,24},{4,28},{8,16},{12,20},{16,8},{20,12},{24,0},{28,4},{1,25},{... | collective-permute-start | bytes 393224 | tf_op jit(solution)/shard_map/ppermute | solution.py:305
  77.0 3.5 %collective-permute-done.15.got_ref = bf16[128,512]{1,0:T(8,128)(2,1)S(1)} collective-permute-done((bf16[128,512]{1,0:T(8,128)(2,1)S(1)}, bf16[128,512]{1,0:T(8,128)(2,1)S(1)}, u32[]{:S(2)}, u32[]{:S(2)}) %collective-permute-start.15) | collective-permute-done | bytes 131104 | tf_op jit(solution)/shard_map/ppermute | solution.py:305
  80.5 0.7 shard_map.62
  (21 shorter events, 0.2 us)
Async XLA Ops:
  11.6 21.7 %collective-permute-start = (bf16[16,128,512]{2,1,0:T(8,128)(2,1)S(1)}, bf16[16,128,512]{2,1,0:T(8,128)(2,1)S(1)}, u32[]{:S(2)}, u32[]{:S(2)}) collective-permute-start(bf16[16,128,512]{2,1,0:T(8,128)(2,1)S(1)} %get-tuple-element.21), channel_id=1, source_target_pairs={{0,1},{1,0},{2,3},{3,2},{4,5},{5,4},{6,7},{7,6},{8,9},{9,8},{10,11... | collective-permute-start | bytes 6291464 | tf_op jit(solution)/shard_map/ppermute | solution.py:305
  12.1 6.7 %copy-start = (bf16[128,512]{1,0:T(8,128)(2,1)S(1)}, bf16[128,512]{1,0:T(8,128)(2,1)}, u32[]{:S(2)}) copy-start(bf16[128,512]{1,0:T(8,128)(2,1)} %d0_ref.1) | copy-start | bytes 393220
  12.1 16.2 %copy-start.1 = (s32[16,16]{1,0:T(8,128)S(1)}, s32[16,16]{1,0:T(8,128)}, u32[]{:S(2)}) copy-start(s32[16,16]{1,0:T(8,128)} %dp_ref.1) | copy-start | bytes 3076
  12.1 16.9 %collective-permute-start.5 = (bf16[16,128,256]{2,1,0:T(8,128)(2,1)S(1)}, bf16[16,128,256]{2,1,0:T(8,128)(2,1)S(1)}, u32[]{:S(2)}, u32[]{:S(2)}) collective-permute-start(bf16[16,128,256]{2,1,0:T(8,128)(2,1)S(1)} %get-tuple-element.25), channel_id=1, source_target_pairs={{0,1},{1,0},{2,3},{3,2},{4,5},{5,4},{6,7},{7,6},{8,9},{9,8},{10,11... | collective-permute-start | bytes 3145736 | tf_op jit(solution)/shard_map/ppermute | solution.py:305
  18.3 10.7 %collective-permute-start.4 = (bf16[16,128,256]{2,1,0:T(8,128)(2,1)S(1)}, bf16[16,128,256]{2,1,0:T(8,128)(2,1)S(1)}, u32[]{:S(2)}, u32[]{:S(2)}) collective-permute-start(bf16[16,128,256]{2,1,0:T(8,128)(2,1)S(1)} %get-tuple-element.24), channel_id=1, source_target_pairs={{0,1},{1,0},{2,3},{3,2},{4,5},{5,4},{6,7},{7,6},{8,9},{9,8},{10,11... | collective-permute-start | bytes 3145736 | tf_op jit(solution)/shard_map/ppermute | solution.py:305
  18.8 6.7 %collective-permute-start.2 = (bf16[128,512]{1,0:T(8,128)(2,1)S(1)}, bf16[128,512]{1,0:T(8,128)(2,1)S(1)}, u32[]{:S(2)}, u32[]{:S(2)}) collective-permute-start(bf16[128,512]{1,0:T(8,128)(2,1)S(1)} %copy-done), channel_id=1, source_target_pairs={{0,2},{1,3},{2,0},{3,1},{4,6},{5,7},{6,4},{7,5},{8,10},{9,11},{10,... | collective-permute-start | bytes 393224 | tf_op jit(solution)/shard_map/ppermute | solution.py:305
  21.4 4.1 %collective-permute-start.1 = (bf16[128,512]{1,0:T(8,128)(2,1)S(1)}, bf16[128,512]{1,0:T(8,128)(2,1)S(1)}, u32[]{:S(2)}, u32[]{:S(2)}) collective-permute-start(bf16[128,512]{1,0:T(8,128)(2,1)S(1)} %copy-done), channel_id=1, source_target_pairs={{0,1},{1,0},{2,3},{3,2},{4,5},{5,4},{6,7},{7,6},{8,9},{9,8},{10,11... | collective-permute-start | bytes 393224 | tf_op jit(solution)/shard_map/ppermute | solution.py:305
  25.5 1.8 %collective-permute-start.3 = (bf16[128,512]{1,0:T(8,128)(2,1)S(1)}, bf16[128,512]{1,0:T(8,128)(2,1)S(1)}, u32[]{:S(2)}, u32[]{:S(2)}) collective-permute-start(bf16[128,512]{1,0:T(8,128)(2,1)S(1)} %collective-permute-done.2.d2_ref), channel_id=1, source_target_pairs={{0,1},{1,0},{2,3},{3,2},{4,5},{5,4},{6,7},{7,6},{8,9},{9,8},{10,11... | collective-permute-start | bytes 393224 | tf_op jit(solution)/shard_map/ppermute | solution.py:305
  25.5 30.7 %collective-permute-start.9 = (bf16[16,224,128]{2,1,0:T(8,128)(2,1)S(1)}, bf16[16,224,128]{2,1,0:T(8,128)(2,1)S(1)}, u32[]{:S(2)}, u32[]{:S(2)}) collective-permute-start(bf16[16,224,128]{2,1,0:T(8,128)(2,1)S(1)} %get-tuple-element.30), channel_id=1, source_target_pairs={{0,2},{1,3},{2,0},{3,1},{4,6},{5,7},{6,4},{7,5},{8,10},{9,11},{10,... | collective-permute-start | bytes 2752520 | tf_op jit(solution)/shard_map/ppermute | solution.py:305
  27.2 29.0 %collective-permute-start.10 = (bf16[16,96,128]{2,1,0:T(8,128)(2,1)S(1)}, bf16[16,96,128]{2,1,0:T(8,128)(2,1)S(1)}, u32[]{:S(2)}, u32[]{:S(2)}) collective-permute-start(bf16[16,96,128]{2,1,0:T(8,128)(2,1)S(1)} %get-tuple-element.31), channel_id=1, source_target_pairs={{0,3},{1,2},{2,1},{3,0},{4,7},{5,6},{6,5},{7,4},{8,11},{9,10},{10,... | collective-permute-start | bytes 1179656 | tf_op jit(solution)/shard_map/ppermute | solution.py:305
  57.9 1.6 %collective-permute-start.11 = (f32[256,256]{1,0:T(8,128)S(1)}, f32[256,256]{1,0:T(8,128)S(1)}, u32[]{:S(2)}, u32[]{:S(2)}) collective-permute-start(f32[256,256]{1,0:T(8,128)S(1)} %get-tuple-element.34), channel_id=1, source_target_pairs={{0,1},{1,0},{2,3},{3,2},{4,5},{5,4},{6,7},{7,6},{8,9},{9,8},{10,11... | collective-permute-start | bytes 786440 | tf_op jit(solution)/shard_map/ppermute | solution.py:305
  58.2 3.1 %collective-permute-start.6 = (f32[128,256]{1,0:T(8,128)S(1)}, f32[128,256]{1,0:T(8,128)S(1)}, u32[]{:S(2)}, u32[]{:S(2)}) collective-permute-start(f32[128,256]{1,0:T(8,128)S(1)} %get-tuple-element.27), channel_id=1, source_target_pairs={{0,1},{1,0},{2,3},{3,2},{4,5},{5,4},{6,7},{7,6},{8,9},{9,8},{10,11... | collective-permute-start | bytes 393224 | tf_op jit(solution)/shard_map/ppermute | solution.py:305
  59.5 4.3 %collective-permute-start.12 = (bf16[128,256]{1,0:T(8,128)(2,1)S(1)}, bf16[128,256]{1,0:T(8,128)(2,1)S(1)}, u32[]{:S(2)}, u32[]{:S(2)}) collective-permute-start(bf16[128,256]{1,0:T(8,128)(2,1)S(1)} %slice.21), channel_id=1, source_target_pairs={{0,2},{1,3},{2,0},{3,1},{4,6},{5,7},{6,4},{7,5},{8,10},{9,11},{10,... | collective-permute-start | bytes 196616 | tf_op jit(solution)/shard_map/ppermute | solution.py:305
  61.3 6.2 %collective-permute-start.7 = (f32[128,256]{1,0:T(8,128)S(1)}, f32[128,256]{1,0:T(8,128)S(1)}, u32[]{:S(2)}, u32[]{:S(2)}) collective-permute-start(f32[128,256]{1,0:T(8,128)S(1)} %add.21), channel_id=1, source_target_pairs={{0,4},{4,0},{8,12},{12,8},{16,20},{20,16},{24,28},{28,24},{1,5},{5... | collective-permute-start | bytes 393224 | tf_op jit(solution)/shard_map/ppermute | solution.py:305
  63.9 5.2 %collective-permute-start.13 = (bf16[128,256]{1,0:T(8,128)(2,1)S(1)}, bf16[128,256]{1,0:T(8,128)(2,1)S(1)}, u32[]{:S(2)}, u32[]{:S(2)}) collective-permute-start(bf16[128,256]{1,0:T(8,128)(2,1)S(1)} %fusion.2), channel_id=1, source_target_pairs={{0,4},{4,0},{8,12},{12,8},{16,20},{20,16},{24,28},{28,24},{1,5},{5... | collective-permute-start | bytes 196616 | tf_op jit(solution)/shard_map/ppermute | solution.py:305
  67.5 5.0 %collective-permute-start.8 = (f32[128,256]{1,0:T(8,128)S(1)}, f32[128,256]{1,0:T(8,128)S(1)}, u32[]{:S(2)}, u32[]{:S(2)}) collective-permute-start(f32[128,256]{1,0:T(8,128)S(1)} %add.22), channel_id=1, source_target_pairs={{0,8},{4,12},{8,0},{12,4},{16,24},{20,28},{24,16},{28,20},{1,9},{5... | collective-permute-start | bytes 393224 | tf_op jit(solution)/shard_map/ppermute | solution.py:305
  69.1 4.3 %collective-permute-start.14 = (bf16[128,256]{1,0:T(8,128)(2,1)S(1)}, bf16[128,256]{1,0:T(8,128)(2,1)S(1)}, u32[]{:S(2)}, u32[]{:S(2)}) collective-permute-start(bf16[128,256]{1,0:T(8,128)(2,1)S(1)} %fusion.1), channel_id=1, source_target_pairs={{0,8},{4,12},{8,0},{12,4},{16,24},{20,28},{24,16},{28,20},{1,9},{5... | collective-permute-start | bytes 196616 | tf_op jit(solution)/shard_map/ppermute | solution.py:305
  73.5 6.9 %collective-permute-start.15 = (bf16[128,512]{1,0:T(8,128)(2,1)S(1)}, bf16[128,512]{1,0:T(8,128)(2,1)S(1)}, u32[]{:S(2)}, u32[]{:S(2)}) collective-permute-start(bf16[128,512]{1,0:T(8,128)(2,1)S(1)} %get-tuple-element.35), channel_id=1, source_target_pairs={{0,24},{4,28},{8,16},{12,20},{16,8},{20,12},{24,0},{28,4},{1,25},{... | collective-permute-start | bytes 393224 | tf_op jit(solution)/shard_map/ppermute | solution.py:305
